TPU v7x, 32 devices: a whole 2x2x4 slice. The times are simulated.
32 devices in a mesh: ctx: 8 (over z, x), tp: 4 (over y, core).
Axes of the slice: x: 2, y: 2, z: 4, core: 2. Of those that a mesh axis runs over, the one named last changes fastest.
Arguments:
- queries: bfloat16 [2048, 8192], P('ctx', 'tp'), may hold values from -8 to 8
- keys: bfloat16 [2048, 1024], P('ctx'), may hold values from -7 to 7
- values: bfloat16 [2048, 1024], P('ctx'), may hold values from -6 to 6
- out_weight: bfloat16 [8192, 4096], P('tp'), may hold values from -0.25 to 0.25
- block_order: int32 [16], P('ctx'), may hold values from 0 to 15, each once
Outputs:
- projected: bfloat16 [2048, 4096], P('ctx', 'tp')
Inputs may be any that keep to these rules, and one draw needn't show every extreme that they name: `block_order`: every sequence block appears exactly once.
All inputs are finite; a program needn't handle non-finite values.
Results may differ from a plain program's by a relative error of at most 0.015.
Values may be sent and summed in bfloat16 or wider, within the bound.
No kernel may reach another device: no remote copies, remote signals or barrier semaphores. Data moves between devices by JAX's collectives and lax.ppermute only.
A program may use at most 64 MiB of HBM per device.

v0:
```python
import functools
import math

import jax
import jax.numpy as jnp
from jax import lax
from jax.experimental import pallas as pl
from jax.experimental.pallas import tpu as pltpu
from jax.sharding import PartitionSpec as P

QUERY_HEADS = 64
KEY_VALUE_HEADS = 8
HEAD_SIZE = 128
HIDDEN = -1e30
TAIL = 16
DIGIT = 128
NT = (((1,), (1,)), ((), ()))
VMEM_LIMIT = 16 << 20


def attend_kernel(n_blocks, first, last, scale, kv_heads, span, *refs):
    order_ref, q_ref = refs[:2]
    blocks = refs[2 : 2 + n_blocks]
    refs = refs[2 + n_blocks :]
    if not first:
        old_top, old_total, old_acc = refs[:3]
        refs = refs[3:]
    outs = refs[: 1 if last else 3]
    bias_ref, flip_ref = refs[-6:-4]
    score_refs, weight_refs = refs[-4:-2], refs[-2:]
    parts = order_ref.shape[0]
    rows = q_ref.shape[0] // parts
    heads = q_ref.shape[1] // kv_heads // HEAD_SIZE
    pair = span // rows
    lengths = [block.shape[0] - TAIL for block in blocks]
    offsets = [sum(lengths[:b]) for b in range(n_blocks)]

    key_at = lax.broadcasted_iota(jnp.int32, (rows, rows), 0).astype(jnp.float32)
    query_iota = lax.broadcasted_iota(jnp.int32, (rows, rows), 1)
    for block, length, offset in zip(blocks, lengths, offsets):
        tail = block[length : length + TAIL, 0:HEAD_SIZE].astype(jnp.float32)
        for part in range(length // rows):
            high, low = tail[2 * part : 2 * part + 1, :], tail[2 * part + 1 : 2 * part + 2, :]
            key_pos = (high * DIGIT + low)[:, 0:rows] * float(rows) + key_at
            at = slice(offset + part * rows, offset + (part + 1) * rows)
            for i in range(parts):
                query_pos = (query_iota + order_ref[i] * rows).astype(jnp.float32)
                bias_ref[i, at, :] = jnp.where(key_pos > query_pos, HIDDEN, 0.0)
        for k in range(kv_heads):
            at = slice((2 * k + 1) * HEAD_SIZE, (2 * k + 2) * HEAD_SIZE)
            flip_ref[k, :, offset : offset + length] = block[0:length, at].T

    pieces = [
        (k, i, p) for k in range(kv_heads) for i in range(parts) for p in range(heads // pair)
    ]
    tops, totals = {}, {}

    def head_cols(k, p, j):
        head = k * heads + p * pair + j
        return slice(head * HEAD_SIZE, (head + 1) * HEAD_SIZE)

    def score(t):
        k, i, p = pieces[t]
        q = jnp.concatenate(
            [q_ref[i * rows : (i + 1) * rows, head_cols(k, p, j)] for j in range(pair)], axis=0
        )
        top = None
        for block, length, offset in zip(blocks, lengths, offsets):
            key = block[0:length, 2 * k * HEAD_SIZE : (2 * k + 1) * HEAD_SIZE]
            tile = bias_ref[i, offset : offset + length, :]
            scores = lax.dot_general(key, q, NT, preferred_element_type=jnp.float32)
            scores = scores * scale + jnp.concatenate([tile] * pair, axis=1)
            score_refs[t % 2][offset : offset + length, :] = scores
            part = jnp.max(scores, axis=0, keepdims=True)
            top = part if top is None else jnp.maximum(top, part)
        if not first:
            top = jnp.maximum(top, old_top[k * parts + i, :, p * span : (p + 1) * span])
        tops[t] = top

    def weigh(t):
        weights = jnp.exp2(score_refs[t % 2][...] - tops[t])
        totals[t] = jnp.sum(weights, axis=0, keepdims=True)
        weight_refs[t % 2][...] = weights.astype(jnp.bfloat16)

    def spread(t):
        k, i, p = pieces[t]
        at = slice(p * span, (p + 1) * span)
        c = k * parts + i
        acc = jnp.dot(flip_ref[k], weight_refs[t % 2][...], preferred_element_type=jnp.float32)
        total = totals[t]
        if not first:
            factor = jnp.exp2(old_top[c, :, at] - tops[t])
            total = total + old_total[c, :, at] * factor
            acc = acc + old_acc[c, :, at] * factor
        if last:
            done = (acc * (1.0 / total)).T.astype(jnp.bfloat16)
            for j in range(pair):
                outs[0][i * rows : (i + 1) * rows, head_cols(k, p, j)] = done[
                    j * rows : (j + 1) * rows, :
                ]
        else:
            outs[0][c, :, at] = tops[t]
            outs[1][c, :, at] = total
            outs[2][c, :, at] = acc

    for t in range(len(pieces) + 2):
        if t < len(pieces):
            score(t)
        if t >= 2:
            spread(t - 2)
        if 1 <= t <= len(pieces):
            weigh(t - 1)


def attend(order, queries, blocks, state, last, kv_heads):
    tokens, width = queries.shape
    parts = order.shape[0]
    rows = tokens // parts
    heads = width // kv_heads // HEAD_SIZE
    span = math.gcd(heads, 2) * rows
    scale = math.log2(math.e) / math.sqrt(HEAD_SIZE)
    first = state is None
    seen = sum(block.shape[0] - TAIL for block in blocks)
    pairs = tokens * width // HEAD_SIZE * seen
    whole = pl.BlockSpec(memory_space=pltpu.VMEM)
    combos = kv_heads * parts
    state_shape = [
        jax.ShapeDtypeStruct((combos, 1, heads * rows), jnp.float32),
        jax.ShapeDtypeStruct((combos, 1, heads * rows), jnp.float32),
        jax.ShapeDtypeStruct((combos, HEAD_SIZE, heads * rows), jnp.float32),
    ]
    return pl.pallas_call(
        functools.partial(attend_kernel, len(blocks), first, last, scale, kv_heads, span),
        in_specs=[pl.BlockSpec(memory_space=pltpu.SMEM)]
        + [whole] * (1 + len(blocks) + (0 if first else 3)),
        out_specs=[whole] if last else [whole] * 3,
        out_shape=[jax.ShapeDtypeStruct(queries.shape, jnp.bfloat16)] if last else state_shape,
        scratch_shapes=[
            pltpu.VMEM((parts, seen, rows), jnp.float32),
            pltpu.VMEM((kv_heads, HEAD_SIZE, seen), jnp.bfloat16),
        ]
        + [pltpu.VMEM((seen, span), jnp.float32)] * 2
        + [pltpu.VMEM((seen, span), jnp.bfloat16)] * 2,
        compiler_params=pltpu.CompilerParams(vmem_limit_bytes=VMEM_LIMIT),
        cost_estimate=pl.CostEstimate(
            flops=4 * pairs * HEAD_SIZE, bytes_accessed=4 * pairs, transcendentals=pairs
        ),
    )(order, queries, *blocks, *(() if first else state))


def project_kernel(at_ref, a_ref, w_ref, *refs):
    send_ref, keep_ref = refs[-2:]
    wide = math.gcd(send_ref.shape[1], 256)
    for out, which in ((send_ref, 0), (keep_ref, 1)):
        for tile in range(out.shape[1] // wide):
            column = pl.multiple_of(at_ref[which] + tile * wide, wide)
            out[:, tile * wide : (tile + 1) * wide] = jnp.dot(
                a_ref[...], w_ref[:, pl.ds(column, wide)], preferred_element_type=jnp.float32
            ).astype(out.dtype)


def project(attended, weight, send_at, keep_at, columns, after):
    tokens, depth = attended.shape
    whole = pl.BlockSpec(memory_space=pltpu.VMEM)
    return pl.pallas_call(
        project_kernel,
        in_specs=[pl.BlockSpec(memory_space=pltpu.SMEM), whole, whole]
        + [pl.BlockSpec(memory_space=pl.ANY)] * len(after),
        out_specs=[whole] * 2,
        out_shape=[
            jax.ShapeDtypeStruct((tokens, columns), jnp.bfloat16),
            jax.ShapeDtypeStruct((tokens, columns), jnp.float32),
        ],
        compiler_params=pltpu.CompilerParams(vmem_limit_bytes=VMEM_LIMIT),
        cost_estimate=pl.CostEstimate(
            flops=4 * tokens * depth * columns,
            bytes_accessed=4 * depth * columns,
            transcendentals=0,
        ),
    )(jnp.stack([send_at, keep_at]).astype(jnp.int32), attended, weight, *after)


def shards(n_ctx, n_tp, queries, keys, values, out_weight, block_order):
    heads_dev = queries.shape[1] // HEAD_SIZE
    group_size = QUERY_HEADS // KEY_VALUE_HEADS
    kv_heads = max(1, heads_dev // group_size)
    tp = lax.axis_index("tp")
    start = tp * heads_dev // group_size * HEAD_SIZE
    own_keys = lax.dynamic_slice_in_dim(keys, start, kv_heads * HEAD_SIZE, 1)
    own_values = lax.dynamic_slice_in_dim(values, start, kv_heads * HEAD_SIZE, 1)
    pieces = []
    for head in range(kv_heads):
        at = slice(head * HEAD_SIZE, (head + 1) * HEAD_SIZE)
        pieces += [own_keys[:, at], own_values[:, at]]
    body = jnp.concatenate(pieces, axis=1)
    digits = jnp.stack([block_order // DIGIT, block_order % DIGIT], axis=1).reshape(-1)
    digits = jnp.pad(digits, (0, TAIL - digits.shape[0])).astype(jnp.bfloat16)
    tail = jnp.broadcast_to(digits[:, None], (TAIL, body.shape[1]))
    own = jnp.concatenate([body, tail], axis=0)

    inner = math.gcd(n_ctx, 2)
    outer = n_ctx // inner

    def along_outer(block, k):
        pairs = [
            (o * inner + i, (o + k) % outer * inner + i) for o in range(outer) for i in range(inner)
        ]
        return lax.ppermute(block, "ctx", pairs)

    def along_inner(block):
        found = []
        for k in range(1, inner):
            pairs = [
                (o * inner + i, o * inner + (i + k) % inner)
                for o in range(outer)
                for i in range(inner)
            ]
            found.append(lax.ppermute(block, "ctx", pairs))
        return found

    steps = []
    for k in range(1, outer // 2 + 1):
        steps.append([k] if 2 * k == outer else [k, outer - k])
    columns = [[along_outer(own, k) for k in step] for step in steps]
    arrived = along_inner(own)
    before = []
    for step, blocks in zip(steps, columns):
        arrived += before + blocks
        before = []
        for k, block in zip(step, blocks):
            before += along_inner(block)
    arrived += before

    stages = [[own]]
    stages += [arrived[i : min(i + 3, len(arrived) - 1)] for i in range(0, len(arrived) - 1, 3)]
    stages += [arrived[-1:]] if arrived else []
    state = None
    for index, blocks in enumerate(stages):
        state = attend(
            block_order, queries, blocks, state, index == len(stages) - 1, kv_heads
        )
    attended = state[0]

    share = out_weight.shape[1] // n_tp
    cores = math.gcd(n_tp, 2)
    groups = n_tp // cores
    core, group = tp % cores, tp // cores

    def to_core(x):
        pairs = [(t, t // cores * cores + (t + 1) % cores) for t in range(n_tp)]
        return lax.ppermute(x, "tp", pairs)

    def to_group(x, r):
        pairs = [(t, (t + r * cores) % n_tp) for t in range(n_tp)]
        return lax.ppermute(x, "tp", pairs)

    def projected(r, at, width, after):
        to = (group + r) % groups * cores
        return project(
            attended,
            out_weight,
            (to + (core + 1) % cores) * share + at,
            (to + core) * share + at,
            width,
            after,
        )

    cuts = 2 if groups == 2 else 1
    width = share // cuts
    after = ()
    partial = []
    for cut in range(cuts):
        for r in range(1, groups):
            send, keep = projected(r, cut * width, width, after)
            after = (send,)
            partial.append((cut, r, to_core(send) if cores > 1 else None, keep))
    arriving = [[] for _ in range(cuts)]
    for cut, r, other, keep in partial:
        if other is not None:
            keep = keep + other.astype(jnp.float32)
        summed = keep.astype(jnp.bfloat16)
        after += (summed,)
        arriving[cut].append(to_group(summed, r))
    send, mine = projected(0, 0, share, after)
    if cores > 1:
        mine = mine + to_core(send).astype(jnp.float32)
    result = []
    for cut in range(cuts):
        total = mine[:, cut * width : (cut + 1) * width]
        for x in arriving[cut]:
            total = total + x.astype(jnp.float32)
        result.append(total.astype(jnp.bfloat16))
    return jnp.concatenate(result, axis=1)


def solution(mesh):
    in_specs = (P("ctx", "tp"), P("ctx", None), P("ctx", None), P("tp", None), P("ctx"))
    out_specs = P("ctx", "tp")

    def layer(*args):
        return shards(mesh.shape["ctx"], mesh.shape["tp"], *args)

    return jax.shard_map(
        layer, mesh=mesh, in_specs=in_specs, out_specs=out_specs, check_vma=False
    )
```

profile of v0, /device:TPU:0, one launch (start us, length us, event | category | flops | bytes accessed | tf_op | source)
XLA Modules:
  0.0 85.2 jit_solution(10909100735187296351)
XLA Ops:
  2.1 3.1 %collective-permute-start.2 = (bf16[272,512]{1,0:T(8,128)(2,1)S(1)}, bf16[272,512]{1,0:T(8,128)(2,1)S(1)}, u32[]{:S(2)}, u32[]{:S(2)}) collective-permute-start(bf16[272,512]{1,0:T(8,128)(2,1)S(1)} %maximum_maximum_fusion.refs_2_), channel_id=1, source_target_pairs={{0,8},{4,12},{8,16},{12,20},{16,24},{20,28},{24,0},{28,4},{1,9},{5... | collective-permute-start | bytes 835592 | tf_op jit(solution)/shard_map/ppermute | solution.py:208
  5.2 2.1 %collective-permute-start.4 = (bf16[272,512]{1,0:T(8,128)(2,1)S(1)}, bf16[272,512]{1,0:T(8,128)(2,1)S(1)}, u32[]{:S(2)}, u32[]{:S(2)}) collective-permute-start(bf16[272,512]{1,0:T(8,128)(2,1)S(1)} %maximum_maximum_fusion.refs_2_), channel_id=1, source_target_pairs={{0,24},{4,28},{8,0},{12,4},{16,8},{20,12},{24,16},{28,20},{1,25},{... | collective-permute-start | bytes 835592 | tf_op jit(solution)/shard_map/ppermute | solution.py:208
  8.2 1.5 %collective-permute-start.6 = (bf16[272,512]{1,0:T(8,128)(2,1)S(1)}, bf16[272,512]{1,0:T(8,128)(2,1)S(1)}, u32[]{:S(2)}, u32[]{:S(2)}) collective-permute-start(bf16[272,512]{1,0:T(8,128)(2,1)S(1)} %maximum_maximum_fusion.refs_2_), channel_id=1, source_target_pairs={{0,4},{4,0},{8,12},{12,8},{16,20},{20,16},{24,28},{28,24},{1,5},{5... | collective-permute-start | bytes 835592 | tf_op jit(solution)/shard_map/ppermute | solution.py:218
  9.7 5.0 %collective-permute-done.2.refs_3_ = bf16[272,512]{1,0:T(8,128)(2,1)S(1)} collective-permute-done((bf16[272,512]{1,0:T(8,128)(2,1)S(1)}, bf16[272,512]{1,0:T(8,128)(2,1)S(1)}, u32[]{:S(2)}, u32[]{:S(2)}) %collective-permute-start.2) | collective-permute-done | bytes 278560 | tf_op jit(solution)/shard_map/ppermute | solution.py:208
  14.7 1.7 %collective-permute-start.3 = (bf16[272,512]{1,0:T(8,128)(2,1)S(1)}, bf16[272,512]{1,0:T(8,128)(2,1)S(1)}, u32[]{:S(2)}, u32[]{:S(2)}) collective-permute-start(bf16[272,512]{1,0:T(8,128)(2,1)S(1)} %collective-permute-done.2.refs_3_), channel_id=1, source_target_pairs={{0,4},{4,0},{8,12},{12,8},{16,20},{20,16},{24,28},{28,24},{1,5},{5... | collective-permute-start | bytes 835592 | tf_op jit(solution)/shard_map/ppermute | solution.py:218
  16.5 2.8 %collective-permute-done.4.refs_4_ = bf16[272,512]{1,0:T(8,128)(2,1)S(1)} collective-permute-done((bf16[272,512]{1,0:T(8,128)(2,1)S(1)}, bf16[272,512]{1,0:T(8,128)(2,1)S(1)}, u32[]{:S(2)}, u32[]{:S(2)}) %collective-permute-start.4) | collective-permute-done | bytes 278560 | tf_op jit(solution)/shard_map/ppermute | solution.py:208
  19.3 1.5 %collective-permute-start.5 = (bf16[272,512]{1,0:T(8,128)(2,1)S(1)}, bf16[272,512]{1,0:T(8,128)(2,1)S(1)}, u32[]{:S(2)}, u32[]{:S(2)}) collective-permute-start(bf16[272,512]{1,0:T(8,128)(2,1)S(1)} %collective-permute-done.4.refs_4_), channel_id=1, source_target_pairs={{0,4},{4,0},{8,12},{12,8},{16,20},{20,16},{24,28},{28,24},{1,5},{5... | collective-permute-start | bytes 835592 | tf_op jit(solution)/shard_map/ppermute | solution.py:218
  22.6 2.6 %shard_map.55 = (f32[4,1,1024]{2,1,0:T(1,128)S(1)}, f32[4,1,1024]{2,1,0:T(1,128)S(1)}, f32[4,128,1024]{2,1,0:T(8,128)S(1)}) custom-call(s32[2]{0:T(128)S(1)} %copy-done.4, bf16[256,2048]{1,0:T(8,128)(2,1)S(1)} %copy-done.2, bf16[272,512]{1,0:T(8,128)(2,1)S(1)} %maximum_maximum_fusion.refs_2_), custom_call_target="tpu_custom_call" | custom-call | flops 536870912 | bytes 4194304 | tf_op jit(solution)/shard_map/pallas_call | solution.py:132
  25.3 1.3 %copy-done.6 = f32[4,128,1024]{2,1,0:T(8,128)} copy-done((f32[4,128,1024]{2,1,0:T(8,128)}, f32[4,128,1024]{2,1,0:T(8,128)S(1)}, u32[]{:S(2)}) %copy-start.6) | copy-done | bytes 2097176
  26.7 5.1 %collective-permute-done.refs_4_ = bf16[272,512]{1,0:T(8,128)(2,1)S(1)} collective-permute-done((bf16[272,512]{1,0:T(8,128)(2,1)S(1)}, bf16[272,512]{1,0:T(8,128)(2,1)S(1)}, u32[]{:S(2)}, u32[]{:S(2)}) %collective-permute-start) | collective-permute-done | bytes 278560 | tf_op jit(solution)/shard_map/ppermute | solution.py:208
  31.8 1.5 %collective-permute-start.1 = (bf16[272,512]{1,0:T(8,128)(2,1)S(1)}, bf16[272,512]{1,0:T(8,128)(2,1)S(1)}, u32[]{:S(2)}, u32[]{:S(2)}) collective-permute-start(bf16[272,512]{1,0:T(8,128)(2,1)S(1)} %collective-permute-done.refs_4_), channel_id=1, source_target_pairs={{0,4},{4,0},{8,12},{12,8},{16,20},{20,16},{24,28},{28,24},{1,5},{5... | collective-permute-start | bytes 835592 | tf_op jit(solution)/shard_map/ppermute | solution.py:218
  33.3 1.6 %copy-done.7 = f32[4,128,1024]{2,1,0:T(8,128)S(1)} copy-done((f32[4,128,1024]{2,1,0:T(8,128)S(1)}, f32[4,128,1024]{2,1,0:T(8,128)}, u32[]{:S(2)}) %copy-start.7) | copy-done | bytes 2097176
  34.9 5.0 %shard_map.56 = (f32[4,1,1024]{2,1,0:T(1,128)S(1)}, f32[4,1,1024]{2,1,0:T(1,128)S(1)}, f32[4,128,1024]{2,1,0:T(8,128)S(1)}) custom-call(s32[2]{0:T(128)S(1)} %copy-done.5, bf16[256,2048]{1,0:T(8,128)(2,1)S(1)} %copy-done.3, bf16[272,512]{1,0:T(8,128)(2,1)S(1)} %collective-permute-done.6.refs_2_, bf16[272,512]{1,0:T(8,128)(2,1)S(1)} %collective-permute-done.2.refs_3_, ...), custom_call_target="tpu_custom_call" | custom-call | flops 1610612736 | bytes 12582912 | tf_op jit(solution)/shard_map/pallas_call | solution.py:132
  39.9 5.1 %shard_map.57 = (f32[4,1,1024]{2,1,0:T(1,128)S(1)}, f32[4,1,1024]{2,1,0:T(1,128)S(1)}, f32[4,128,1024]{2,1,0:T(8,128)S(1)}) custom-call(s32[2]{0:T(128)S(1)} %copy-done.5, bf16[256,2048]{1,0:T(8,128)(2,1)S(1)} %copy-done.3, bf16[272,512]{1,0:T(8,128)(2,1)S(1)} %collective-permute-done.3.refs_2_, bf16[272,512]{1,0:T(8,128)(2,1)S(1)} %collective-permute-done.5.refs_3_, ...), custom_call_target="tpu_custom_call" | custom-call | flops 1610612736 | bytes 12582912 | tf_op jit(solution)/shard_map/pallas_call | solution.py:132
  45.0 2.9 %shard_map.58.a_ref = bf16[256,2048]{1,0:T(8,128)(2,1)S(1)} custom-call(s32[2]{0:T(128)S(1)} %copy-done.5, bf16[256,2048]{1,0:T(8,128)(2,1)S(1)} %copy-done.3, bf16[272,512]{1,0:T(8,128)(2,1)S(1)} %collective-permute-done.1.refs_2_, f32[4,1,1024]{2,1,0:T(1,128)S(1)} %get-tuple-element.26.refs_3_, f32[4,1,1024]{2,1,0:T(1,128)S(1)} %get-tuple-element.27.refs_4_, ...), custom_call_target="tpu_custom_call" | custom-call | flops 536870912 | bytes 4194304 | tf_op jit(solution)/shard_map/pallas_call | solution.py:132
  48.0 5.8 %copy-done = bf16[2048,4096]{1,0:T(8,128)(2,1)S(1)} copy-done((bf16[2048,4096]{1,0:T(8,128)(2,1)S(1)}, bf16[2048,4096]{1,0:T(8,128)(2,1)}, u32[]{:S(2)}) %copy-start) | copy-done | bytes 16777240
  53.7 1.8 %shard_map.59 = (bf16[256,512]{1,0:T(8,128)(2,1)S(1)}, f32[256,512]{1,0:T(8,128)S(1)}) custom-call(s32[2]{0:T(128)S(1)} %get-tuple-element.44.at_ref, bf16[256,2048]{1,0:T(8,128)(2,1)S(1)} %shard_map.58.a_ref, bf16[2048,4096]{1,0:T(8,128)(2,1)S(1)} %copy-done), custom_call_target="tpu_custom_call" | custom-call | flops 1073741824 | bytes 4194304 | tf_op jit(solution)/shard_map/pallas_call | solution.py:165
  55.9 1.3 %slice-done.3 = s8[4194304]{0:T(1024)(128)(4,1)S(1)} async-done(((s8[16777216]{0:T(1024)(128)(4,1)}), s8[4194304]{0:T(1024)(128)(4,1)S(1)}, s32[]{:S(2)}) %slice-start.3) | async-done | bytes 4194328
  57.2 1.8 %shard_map.60 = (bf16[256,512]{1,0:T(8,128)(2,1)S(1)}, f32[256,512]{1,0:T(8,128)S(1)}) custom-call(s32[2]{0:T(128)S(1)} %get-tuple-element.43.at_ref, bf16[256,2048]{1,0:T(8,128)(2,1)S(1)} %shard_map.58.a_ref, bf16[2048,4096]{1,0:T(8,128)(2,1)S(1)} %bitcast.11, bf16[256,512]{1,0:T(8,128)(2,1)S(1)} %get-tuple-element.29.refs_0_), custom_call_target="tpu_custom_call" | custom-call | flops 1073741824 | bytes 4194304 | tf_op jit(solution)/shard_map/pallas_call | solution.py:165
  61.1 5.8 %copy-done.1 = bf16[2048,4096]{1,0:T(8,128)(2,1)S(1)} copy-done((bf16[2048,4096]{1,0:T(8,128)(2,1)S(1)}, bf16[2048,4096]{1,0:T(8,128)(2,1)}, u32[]{:S(2)}) %copy-start.1) | copy-done | bytes 16777240
  66.9 2.9 %shard_map.61 = (bf16[256,1024]{1,0:T(8,128)(2,1)S(1)}, f32[256,1024]{1,0:T(8,128)S(1)}) custom-call(s32[2]{0:T(128)S(1)} %pad_add_fusion.at_ref, bf16[256,2048]{1,0:T(8,128)(2,1)S(1)} %shard_map.58.a_ref, bf16[2048,4096]{1,0:T(8,128)(2,1)S(1)} %copy-done.1, bf16[256,512]{1,0:T(8,128)(2,1)S(1)} %get-tuple-element.30.refs_0_, ...), custom_call_target="tpu_custom_call" | custom-call | flops 2147483648 | bytes 8388608 | tf_op jit(solution)/shard_map/pallas_call | solution.py:165
  70.0 1.5 %collective-permute-start.11 = (bf16[256,512]{1,0:T(8,128)(2,1)S(1)}, bf16[256,512]{1,0:T(8,128)(2,1)S(1)}, u32[]{:S(2)}, u32[]{:S(2)}) collective-permute-start(bf16[256,512]{1,0:T(8,128)(2,1)S(1)} %add_convert_fusion.refs_2_), channel_id=1, source_target_pairs={{0,2},{1,3},{2,0},{3,1},{4,6},{5,7},{6,4},{7,5},{8,10},{9,11},{10,... | collective-permute-start | bytes 786440 | tf_op jit(solution)/shard_map/ppermute | solution.py:255
  72.2 7.0 %collective-permute-done.11 = bf16[256,512]{1,0:T(8,128)(2,1)S(1)} collective-permute-done((bf16[256,512]{1,0:T(8,128)(2,1)S(1)}, bf16[256,512]{1,0:T(8,128)(2,1)S(1)}, u32[]{:S(2)}, u32[]{:S(2)}) %collective-permute-start.11) | collective-permute-done | bytes 262176 | tf_op jit(solution)/shard_map/ppermute | solution.py:255
  79.2 5.0 %collective-permute-done.10 = bf16[256,512]{1,0:T(8,128)(2,1)S(1)} collective-permute-done((bf16[256,512]{1,0:T(8,128)(2,1)S(1)}, bf16[256,512]{1,0:T(8,128)(2,1)S(1)}, u32[]{:S(2)}, u32[]{:S(2)}) %collective-permute-start.10) | collective-permute-done | bytes 262176 | tf_op jit(solution)/shard_map/ppermute | solution.py:255
  (46 shorter events, 9.2 us)
Async XLA Ops:
  0.0 33.2 %copy-start.5 = (s32[2]{0:T(128)S(1)}, s32[2]{0:T(128)}, u32[]{:S(2)}) copy-start(s32[2]{0:T(128)} %refs_0_.7) | copy-start | bytes 28
  0.0 33.3 %copy-start.3 = (bf16[256,2048]{1,0:T(8,128)(2,1)S(1)}, bf16[256,2048]{1,0:T(8,128)(2,1)}, u32[]{:S(2)}) copy-start(bf16[256,2048]{1,0:T(8,128)(2,1)} %refs_1_.7) | copy-start | bytes 3145732
  2.1 12.7 %collective-permute-start.2 = (bf16[272,512]{1,0:T(8,128)(2,1)S(1)}, bf16[272,512]{1,0:T(8,128)(2,1)S(1)}, u32[]{:S(2)}, u32[]{:S(2)}) collective-permute-start(bf16[272,512]{1,0:T(8,128)(2,1)S(1)} %maximum_maximum_fusion.refs_2_), channel_id=1, source_target_pairs={{0,8},{4,12},{8,16},{12,20},{16,24},{20,28},{24,0},{28,4},{1,9},{5... | collective-permute-start | bytes 835592 | tf_op jit(solution)/shard_map/ppermute | solution.py:208
  5.2 14.1 %collective-permute-start.4 = (bf16[272,512]{1,0:T(8,128)(2,1)S(1)}, bf16[272,512]{1,0:T(8,128)(2,1)S(1)}, u32[]{:S(2)}, u32[]{:S(2)}) collective-permute-start(bf16[272,512]{1,0:T(8,128)(2,1)S(1)} %maximum_maximum_fusion.refs_2_), channel_id=1, source_target_pairs={{0,24},{4,28},{8,0},{12,4},{16,8},{20,12},{24,16},{28,20},{1,25},{... | collective-permute-start | bytes 835592 | tf_op jit(solution)/shard_map/ppermute | solution.py:208
  7.3 24.5 %collective-permute-start = (bf16[272,512]{1,0:T(8,128)(2,1)S(1)}, bf16[272,512]{1,0:T(8,128)(2,1)S(1)}, u32[]{:S(2)}, u32[]{:S(2)}) collective-permute-start(bf16[272,512]{1,0:T(8,128)(2,1)S(1)} %maximum_maximum_fusion.refs_2_), channel_id=1, source_target_pairs={{0,16},{4,20},{8,24},{12,28},{16,0},{20,4},{24,8},{28,12},{1,17},{... | collective-permute-start | bytes 835592 | tf_op jit(solution)/shard_map/ppermute | solution.py:208
  8.2 25.0 %collective-permute-start.6 = (bf16[272,512]{1,0:T(8,128)(2,1)S(1)}, bf16[272,512]{1,0:T(8,128)(2,1)S(1)}, u32[]{:S(2)}, u32[]{:S(2)}) collective-permute-start(bf16[272,512]{1,0:T(8,128)(2,1)S(1)} %maximum_maximum_fusion.refs_2_), channel_id=1, source_target_pairs={{0,4},{4,0},{8,12},{12,8},{16,20},{20,16},{24,28},{28,24},{1,5},{5... | collective-permute-start | bytes 835592 | tf_op jit(solution)/shard_map/ppermute | solution.py:218
  14.7 25.2 %collective-permute-start.3 = (bf16[272,512]{1,0:T(8,128)(2,1)S(1)}, bf16[272,512]{1,0:T(8,128)(2,1)S(1)}, u32[]{:S(2)}, u32[]{:S(2)}) collective-permute-start(bf16[272,512]{1,0:T(8,128)(2,1)S(1)} %collective-permute-done.2.refs_3_), channel_id=1, source_target_pairs={{0,4},{4,0},{8,12},{12,8},{16,20},{20,16},{24,28},{28,24},{1,5},{5... | collective-permute-start | bytes 835592 | tf_op jit(solution)/shard_map/ppermute | solution.py:218
  19.3 20.7 %collective-permute-start.5 = (bf16[272,512]{1,0:T(8,128)(2,1)S(1)}, bf16[272,512]{1,0:T(8,128)(2,1)S(1)}, u32[]{:S(2)}, u32[]{:S(2)}) collective-permute-start(bf16[272,512]{1,0:T(8,128)(2,1)S(1)} %collective-permute-done.4.refs_4_), channel_id=1, source_target_pairs={{0,4},{4,0},{8,12},{12,8},{16,20},{20,16},{24,28},{28,24},{1,5},{5... | collective-permute-start | bytes 835592 | tf_op jit(solution)/shard_map/ppermute | solution.py:218
  20.7 1.2 %copy-start.2 = (bf16[256,2048]{1,0:T(8,128)(2,1)S(1)}, bf16[256,2048]{1,0:T(8,128)(2,1)}, u32[]{:S(2)}) copy-start(bf16[256,2048]{1,0:T(8,128)(2,1)} %refs_1_.7) | copy-start | bytes 3145732
  22.0 0.7 copy-start.4
  25.3 1.4 %copy-start.6 = (f32[4,128,1024]{2,1,0:T(8,128)}, f32[4,128,1024]{2,1,0:T(8,128)S(1)}, u32[]{:S(2)}) copy-start(f32[4,128,1024]{2,1,0:T(8,128)S(1)} %get-tuple-element.22.refs_7_) | copy-start | bytes 6291460
  31.8 13.2 %collective-permute-start.1 = (bf16[272,512]{1,0:T(8,128)(2,1)S(1)}, bf16[272,512]{1,0:T(8,128)(2,1)S(1)}, u32[]{:S(2)}, u32[]{:S(2)}) collective-permute-start(bf16[272,512]{1,0:T(8,128)(2,1)S(1)} %collective-permute-done.refs_4_), channel_id=1, source_target_pairs={{0,4},{4,0},{8,12},{12,8},{16,20},{20,16},{24,28},{28,24},{1,5},{5... | collective-permute-start | bytes 835592 | tf_op jit(solution)/shard_map/ppermute | solution.py:218
  33.3 1.6 %copy-start.7 = (f32[4,128,1024]{2,1,0:T(8,128)S(1)}, f32[4,128,1024]{2,1,0:T(8,128)}, u32[]{:S(2)}) copy-start(f32[4,128,1024]{2,1,0:T(8,128)} %copy-done.6) | copy-start | bytes 6291460
  34.8 20.7 %slice-start = ((s8[16777216]{0:T(1024)(128)(4,1)}), s8[4194304]{0:T(1024)(128)(4,1)S(1)}, s32[]{:S(2)}) async-start(s8[16777216]{0:T(1024)(128)(4,1)} %bitcast.10), calls=%async_computation | async-start | bytes 8388608
  39.9 15.7 %slice-start.1 = ((s8[16777216]{0:T(1024)(128)(4,1)}), s8[4194304]{0:T(1024)(128)(4,1)S(1)}, s32[]{:S(2)}) async-start(s8[16777216]{0:T(1024)(128)(4,1)} %bitcast.10), calls=%async_computation.1 | async-start | bytes 8388608
  47.9 5.8 %copy-start = (bf16[2048,4096]{1,0:T(8,128)(2,1)S(1)}, bf16[2048,4096]{1,0:T(8,128)(2,1)}, u32[]{:S(2)}) copy-start(bf16[2048,4096]{1,0:T(8,128)(2,1)} %w_ref.5) | copy-start | bytes 50331652
  53.7 2.2 %slice-start.2 = ((s8[16777216]{0:T(1024)(128)(4,1)}), s8[4194304]{0:T(1024)(128)(4,1)S(1)}, s32[]{:S(2)}) async-start(s8[16777216]{0:T(1024)(128)(4,1)} %bitcast.10), calls=%async_computation.2 | async-start | bytes 8388608
  53.7 3.5 %slice-start.3 = ((s8[16777216]{0:T(1024)(128)(4,1)}), s8[4194304]{0:T(1024)(128)(4,1)S(1)}, s32[]{:S(2)}) async-start(s8[16777216]{0:T(1024)(128)(4,1)} %bitcast.10), calls=%async_computation.3 | async-start | bytes 8388608
  59.0 1.6 %collective-permute-start.8 = (bf16[256,512]{1,0:T(8,128)(2,1)S(1)}, bf16[256,512]{1,0:T(8,128)(2,1)S(1)}, u32[]{:S(2)}, u32[]{:S(2)}) collective-permute-start(bf16[256,512]{1,0:T(8,128)(2,1)S(1)} %get-tuple-element.30.refs_0_), channel_id=1, source_target_pairs={{0,1},{1,0},{2,3},{3,2},{4,5},{5,4},{6,7},{7,6},{8,9},{9,8},{10,11... | collective-permute-start | bytes 786440 | tf_op jit(solution)/shard_map/ppermute | solution.py:251
  59.1 1.9 %collective-permute-start.7 = (bf16[256,512]{1,0:T(8,128)(2,1)S(1)}, bf16[256,512]{1,0:T(8,128)(2,1)S(1)}, u32[]{:S(2)}, u32[]{:S(2)}) collective-permute-start(bf16[256,512]{1,0:T(8,128)(2,1)S(1)} %get-tuple-element.29.refs_0_), channel_id=1, source_target_pairs={{0,1},{1,0},{2,3},{3,2},{4,5},{5,4},{6,7},{7,6},{8,9},{9,8},{10,11... | collective-permute-start | bytes 786440 | tf_op jit(solution)/shard_map/ppermute | solution.py:251
  61.1 5.8 %copy-start.1 = (bf16[2048,4096]{1,0:T(8,128)(2,1)S(1)}, bf16[2048,4096]{1,0:T(8,128)(2,1)}, u32[]{:S(2)}) copy-start(bf16[2048,4096]{1,0:T(8,128)(2,1)} %w_ref.5) | copy-start | bytes 50331652
  69.8 2.2 %collective-permute-start.9 = (bf16[256,1024]{1,0:T(8,128)(2,1)S(1)}, bf16[256,1024]{1,0:T(8,128)(2,1)S(1)}, u32[]{:S(2)}, u32[]{:S(2)}) collective-permute-start(bf16[256,1024]{1,0:T(8,128)(2,1)S(1)} %get-tuple-element.34), channel_id=1, source_target_pairs={{0,1},{1,0},{2,3},{3,2},{4,5},{5,4},{6,7},{7,6},{8,9},{9,8},{10,11... | collective-permute-start | bytes 1572872 | tf_op jit(solution)/shard_map/ppermute | solution.py:251
  70.0 9.2 %collective-permute-start.11 = (bf16[256,512]{1,0:T(8,128)(2,1)S(1)}, bf16[256,512]{1,0:T(8,128)(2,1)S(1)}, u32[]{:S(2)}, u32[]{:S(2)}) collective-permute-start(bf16[256,512]{1,0:T(8,128)(2,1)S(1)} %add_convert_fusion.refs_2_), channel_id=1, source_target_pairs={{0,2},{1,3},{2,0},{3,1},{4,6},{5,7},{6,4},{7,5},{8,10},{9,11},{10,... | collective-permute-start | bytes 786440 | tf_op jit(solution)/shard_map/ppermute | solution.py:255
  71.5 12.7 %collective-permute-start.10 = (bf16[256,512]{1,0:T(8,128)(2,1)S(1)}, bf16[256,512]{1,0:T(8,128)(2,1)S(1)}, u32[]{:S(2)}, u32[]{:S(2)}) collective-permute-start(bf16[256,512]{1,0:T(8,128)(2,1)S(1)} %add_convert_fusion.1.refs_1_), channel_id=1, source_target_pairs={{0,2},{1,3},{2,0},{3,1},{4,6},{5,7},{6,4},{7,5},{8,10},{9,11},{10,... | collective-permute-start | bytes 786440 | tf_op jit(solution)/shard_map/ppermute | solution.py:255
where the time goes:
time: 85.6 us; the launch traced here: 85.2 us
  waiting for transfers between devices  26.1 us (30%)
  Pallas kernels  22.3 us (26%)
  local copies, waits for them, and re-layouts  19.1 us (22%)
  starting transfers between devices  15.1 us (18%)
  other arithmetic  2.39 us (3%)
    unnamed x24, local copies, waits for them, and re-layouts  18 us
    pallas_call x4, Pallas kernels, attend(): pl.pallas_call(functools.partial(attend_kernel, len(blocks), first, last,...  15.7 us
    ppermute x3, waiting for transfers between devices, along_outer(): return lax.ppermute(block, 'ctx', pairs)  12.9 us
    ppermute x2, waiting for transfers between devices, to_group(): return lax.ppermute(x, 'tp', pairs)  12 us
    pallas_call x3, Pallas kernels, project(): pl.pallas_call(project_kernel, in_specs=[pl.BlockSpec(memory_space=pltpu....  6.6 us
    ppermute x4, starting transfers between devices, along_inner(): found.append(lax.ppermute(block, 'ctx', pairs))  6.18 us
    ppermute x3, starting transfers between devices, along_outer(): return lax.ppermute(block, 'ctx', pairs)  6.14 us
    ppermute x2, starting transfers between devices, to_group(): return lax.ppermute(x, 'tp', pairs)  2.03 us
  transfers between devices with their start and end apart: 12, of which 7 were waited for; matrix products, arithmetic and copies ran while one was open for 0% of the time, Pallas kernels for 15%

commit v1 on v0

--- a/solution.py
+++ b/solution.py
@@ -16,6 +16,35 @@
 DIGIT = 128
 NT = (((1,), (1,)), ((), ()))
 VMEM_LIMIT = 16 << 20
+WIDE_LIMIT = 48 << 20
+
+
+def fetch_columns(at_ref, weight_ref, buffer, sem, counts):
+    wide = buffer.shape[2]
+    copies = []
+    for run, count in enumerate(counts):
+        for tile in range(count):
+            column = pl.multiple_of(at_ref[run] + tile * wide, wide)
+            n = len(copies)
+            copies.append(
+                pltpu.make_async_copy(
+                    weight_ref.at[:, pl.ds(column, wide)], buffer.at[n], sem.at[n]
+                )
+            )
+            copies[-1].start()
+    return copies
+
+
+def multiply_columns(rows_ref, buffer, copies, outs):
+    wide = buffer.shape[2]
+    n = 0
+    for out in outs:
+        for tile in range(out.shape[1] // wide):
+            copies[n].wait()
+            out[:, tile * wide : (tile + 1) * wide] = jnp.dot(
+                rows_ref[...], buffer[n], preferred_element_type=jnp.float32
+            ).astype(out.dtype)
+            n += 1
 
 
 def attend_kernel(n_blocks, first, last, scale, kv_heads, span, *refs):
@@ -25,7 +54,13 @@
     if not first:
         old_top, old_total, old_acc = refs[:3]
         refs = refs[3:]
-    outs = refs[: 1 if last else 3]
+    if last:
+        at_ref, weight_ref = refs[:2]
+        buffer, sem = refs[-2:]
+        refs = refs[2:-2]
+        counts = [out.shape[1] // buffer.shape[2] for out in refs[1:3]]
+        copies = fetch_columns(at_ref, weight_ref, buffer, sem, counts)
+    outs = refs[:3]
     bias_ref, flip_ref = refs[-6:-4]
     score_refs, weight_refs = refs[-4:-2], refs[-2:]
     parts = order_ref.shape[0]
@@ -110,74 +145,96 @@
             spread(t - 2)
         if 1 <= t <= len(pieces):
             weigh(t - 1)
-
-
-def attend(order, queries, blocks, state, last, kv_heads):
+    if last:
+        multiply_columns(outs[0], buffer, copies, outs[1:3])
+
+
+def product_shapes(tokens, columns):
+    return [
+        jax.ShapeDtypeStruct((tokens, columns), jnp.bfloat16),
+        jax.ShapeDtypeStruct((tokens, columns), jnp.float32),
+    ]
+
+
+def column_scratch(depth, columns):
+    wide = math.gcd(columns, 256)
+    tiles = 2 * columns // wide
+    return [pltpu.VMEM((tiles, depth, wide), jnp.bfloat16), pltpu.SemaphoreType.DMA((tiles,))]
+
+
+def attend(order, queries, blocks, state, kv_heads, then=None):
     tokens, width = queries.shape
     parts = order.shape[0]
     rows = tokens // parts
     heads = width // kv_heads // HEAD_SIZE
     span = math.gcd(heads, 2) * rows
     scale = math.log2(math.e) / math.sqrt(HEAD_SIZE)
-    first = state is None
+    first, last = state is None, then is not None
     seen = sum(block.shape[0] - TAIL for block in blocks)
     pairs = tokens * width // HEAD_SIZE * seen
     whole = pl.BlockSpec(memory_space=pltpu.VMEM)
+    scalars = pl.BlockSpec(memory_space=pltpu.SMEM)
     combos = kv_heads * parts
-    state_shape = [
-        jax.ShapeDtypeStruct((combos, 1, heads * rows), jnp.float32),
-        jax.ShapeDtypeStruct((combos, 1, heads * rows), jnp.float32),
-        jax.ShapeDtypeStruct((combos, HEAD_SIZE, heads * rows), jnp.float32),
+    operands = [order, queries, *blocks, *(() if first else state)]
+    in_specs = [scalars] + [whole] * (len(operands) - 1)
+    scratch = [
+        pltpu.VMEM((parts, seen, rows), jnp.float32),
+        pltpu.VMEM((kv_heads, HEAD_SIZE, seen), jnp.bfloat16),
     ]
+    scratch += [pltpu.VMEM((seen, span), jnp.float32)] * 2
+    scratch += [pltpu.VMEM((seen, span), jnp.bfloat16)] * 2
+    flops = 4 * pairs * HEAD_SIZE
+    if last:
+        at, weight, columns = then
+        operands += [at, weight]
+        in_specs += [scalars, pl.BlockSpec(memory_space=pl.ANY)]
+        out_shape = [jax.ShapeDtypeStruct(queries.shape, jnp.bfloat16)]
+        out_shape += product_shapes(tokens, columns)
+        scratch += column_scratch(width, columns)
+        flops += 4 * tokens * width * columns
+    else:
+        out_shape = [
+            jax.ShapeDtypeStruct((combos, 1, heads * rows), jnp.float32),
+            jax.ShapeDtypeStruct((combos, 1, heads * rows), jnp.float32),
+            jax.ShapeDtypeStruct((combos, HEAD_SIZE, heads * rows), jnp.float32),
+        ]
     return pl.pallas_call(
         functools.partial(attend_kernel, len(blocks), first, last, scale, kv_heads, span),
-        in_specs=[pl.BlockSpec(memory_space=pltpu.SMEM)]
-        + [whole] * (1 + len(blocks) + (0 if first else 3)),
-        out_specs=[whole] if last else [whole] * 3,
-        out_shape=[jax.ShapeDtypeStruct(queries.shape, jnp.bfloat16)] if last else state_shape,
-        scratch_shapes=[
-            pltpu.VMEM((parts, seen, rows), jnp.float32),
-            pltpu.VMEM((kv_heads, HEAD_SIZE, seen), jnp.bfloat16),
-        ]
-        + [pltpu.VMEM((seen, span), jnp.float32)] * 2
-        + [pltpu.VMEM((seen, span), jnp.bfloat16)] * 2,
-        compiler_params=pltpu.CompilerParams(vmem_limit_bytes=VMEM_LIMIT),
+        in_specs=in_specs,
+        out_specs=[whole] * len(out_shape),
+        out_shape=out_shape,
+        scratch_shapes=scratch,
+        compiler_params=pltpu.CompilerParams(vmem_limit_bytes=WIDE_LIMIT if last else VMEM_LIMIT),
         cost_estimate=pl.CostEstimate(
-            flops=4 * pairs * HEAD_SIZE, bytes_accessed=4 * pairs, transcendentals=pairs
+            flops=flops, bytes_accessed=4 * pairs, transcendentals=pairs
         ),
-    )(order, queries, *blocks, *(() if first else state))
-
-
-def project_kernel(at_ref, a_ref, w_ref, *refs):
-    send_ref, keep_ref = refs[-2:]
-    wide = math.gcd(send_ref.shape[1], 256)
-    for out, which in ((send_ref, 0), (keep_ref, 1)):
-        for tile in range(out.shape[1] // wide):
-            column = pl.multiple_of(at_ref[which] + tile * wide, wide)
-            out[:, tile * wide : (tile + 1) * wide] = jnp.dot(
-                a_ref[...], w_ref[:, pl.ds(column, wide)], preferred_element_type=jnp.float32
-            ).astype(out.dtype)
-
-
-def project(attended, weight, send_at, keep_at, columns, after):
+    )(*operands)
+
+
+def project_kernel(at_ref, rows_ref, weight_ref, *refs):
+    send_ref, keep_ref, buffer, sem = refs[-4:]
+    counts = [out.shape[1] // buffer.shape[2] for out in (send_ref, keep_ref)]
+    copies = fetch_columns(at_ref, weight_ref, buffer, sem, counts)
+    multiply_columns(rows_ref, buffer, copies, (send_ref, keep_ref))
+
+
+def project(at, attended, weight, columns, after):
     tokens, depth = attended.shape
     whole = pl.BlockSpec(memory_space=pltpu.VMEM)
+    unread = pl.BlockSpec(memory_space=pl.ANY)
     return pl.pallas_call(
         project_kernel,
-        in_specs=[pl.BlockSpec(memory_space=pltpu.SMEM), whole, whole]
-        + [pl.BlockSpec(memory_space=pl.ANY)] * len(after),
+        in_specs=[pl.BlockSpec(memory_space=pltpu.SMEM), whole, unread] + [unread] * len(after),
         out_specs=[whole] * 2,
-        out_shape=[
-            jax.ShapeDtypeStruct((tokens, columns), jnp.bfloat16),
-            jax.ShapeDtypeStruct((tokens, columns), jnp.float32),
-        ],
-        compiler_params=pltpu.CompilerParams(vmem_limit_bytes=VMEM_LIMIT),
+        out_shape=product_shapes(tokens, columns),
+        scratch_shapes=column_scratch(depth, columns),
+        compiler_params=pltpu.CompilerParams(vmem_limit_bytes=WIDE_LIMIT),
         cost_estimate=pl.CostEstimate(
             flops=4 * tokens * depth * columns,
             bytes_accessed=4 * depth * columns,
             transcendentals=0,
         ),
-    )(jnp.stack([send_at, keep_at]).astype(jnp.int32), attended, weight, *after)
+    )(at, attended, weight, *after)
 
 
 def shards(n_ctx, n_tp, queries, keys, values, out_weight, block_order):
@@ -234,17 +291,18 @@
     stages = [[own]]
     stages += [arrived[i : min(i + 3, len(arrived) - 1)] for i in range(0, len(arrived) - 1, 3)]
     stages += [arrived[-1:]] if arrived else []
-    state = None
-    for index, blocks in enumerate(stages):
-        state = attend(
-            block_order, queries, blocks, state, index == len(stages) - 1, kv_heads
-        )
-    attended = state[0]
-
     share = out_weight.shape[1] // n_tp
     cores = math.gcd(n_tp, 2)
     groups = n_tp // cores
     core, group = tp % cores, tp // cores
+    cuts = 2 if groups == 2 else 1
+    width = share // cuts
+    jobs = [(cut, r) for cut in range(cuts) for r in range(1, groups)]
+
+    def begins(cut, r):
+        to = (group + r) % groups * cores
+        at = jnp.stack([to + (core + 1) % cores, to + core]) * share + cut * width
+        return at.astype(jnp.int32)
 
     def to_core(x):
         pairs = [(t, t // cores * cores + (t + 1) % cores) for t in range(n_tp)]
@@ -254,34 +312,33 @@
         pairs = [(t, (t + r * cores) % n_tp) for t in range(n_tp)]
         return lax.ppermute(x, "tp", pairs)
 
-    def projected(r, at, width, after):
-        to = (group + r) % groups * cores
-        return project(
-            attended,
-            out_weight,
-            (to + (core + 1) % cores) * share + at,
-            (to + core) * share + at,
-            width,
-            after,
-        )
-
-    cuts = 2 if groups == 2 else 1
-    width = share // cuts
-    after = ()
+    state = None
+    for blocks in stages[:-1]:
+        state = attend(block_order, queries, blocks, state, kv_heads)
+    first = jobs[0] if jobs else (0, 0)
+    attended, send, keep = attend(
+        block_order,
+        queries,
+        stages[-1],
+        state,
+        kv_heads,
+        (begins(*first), out_weight, width),
+    )
+
     partial = []
-    for cut in range(cuts):
-        for r in range(1, groups):
-            send, keep = projected(r, cut * width, width, after)
-            after = (send,)
-            partial.append((cut, r, to_core(send) if cores > 1 else None, keep))
+    for name, (cut, r) in enumerate(jobs):
+        if name > 0:
+            send, keep = project(begins(cut, r), attended, out_weight, width, (send,))
+        partial.append((to_core(send) if cores > 1 else None, keep))
     arriving = [[] for _ in range(cuts)]
-    for cut, r, other, keep in partial:
+    after = (send,)
+    for (cut, r), (other, keep) in zip(jobs, partial):
         if other is not None:
             keep = keep + other.astype(jnp.float32)
         summed = keep.astype(jnp.bfloat16)
         after += (summed,)
         arriving[cut].append(to_group(summed, r))
-    send, mine = projected(0, 0, share, after)
+    send, mine = project(begins(0, 0), attended, out_weight, share, after)
     if cores > 1:
         mine = mine + to_core(send).astype(jnp.float32)
     result = []

time: 85.6 us -> 81.4 us (0.951)
  local copies, waits for them, and re-layouts: 19.1 us -> 5.95 us
  Pallas kernels: 22.3 us -> 31.3 us
    unnamed x24 -> x12, local copies, waits for them, and re-layouts: 18 us -> 4.8 us
    pallas_call x3 -> x2, Pallas kernels: 6.6 us -> 11.9 us  [project(): pl.pallas_call(project_kernel, in_specs=[pl.BlockSpec(memory_space=pltpu....]
    pallas_call x4, Pallas kernels: 15.7 us -> 19.4 us  [attend(): pl.pallas_call(functools.partial(attend_kernel, len(blocks), first, last,...]
  transfers between devices with their start and end apart: 12 -> 12, of which waited for: 7 -> 7; matrix products, arithmetic and copies ran while one was open for 0% -> 0% of each run, Pallas kernels for 15% -> 16%
where the time goes in v1:
time: 81.4 us; the launch traced here: 81.1 us
  Pallas kernels  31.3 us (38%)
  waiting for transfers between devices  26.2 us (32%)
  starting transfers between devices  15.1 us (19%)
  local copies, waits for them, and re-layouts  5.95 us (7%)
  other arithmetic  2.38 us (3%)
    pallas_call x4, Pallas kernels, attend(): pl.pallas_call(functools.partial(attend_kernel, len(blocks), first, last,...  19.4 us
    ppermute x3, waiting for transfers between devices, along_outer(): return lax.ppermute(block, 'ctx', pairs)  12.9 us
    ppermute x2, waiting for transfers between devices, to_group(): return lax.ppermute(x, 'tp', pairs)  12 us
    pallas_call x2, Pallas kernels, project(): pl.pallas_call(project_kernel, in_specs=[pl.BlockSpec(memory_space=pltpu....  11.9 us
    ppermute x4, starting transfers between devices, along_inner(): found.append(lax.ppermute(block, 'ctx', pairs))  6.18 us
    ppermute x3, starting transfers between devices, along_outer(): return lax.ppermute(block, 'ctx', pairs)  6.14 us
    unnamed x12, local copies, waits for them, and re-layouts  4.8 us
    ppermute x2, starting transfers between devices, to_group(): return lax.ppermute(x, 'tp', pairs)  2.03 us
  transfers between devices with their start and end apart: 12, of which 7 were waited for; matrix products, arithmetic and copies ran while one was open for 0% of the time, Pallas kernels for 16%

profile of v1, /device:TPU:0, one launch (start us, length us, event | category | flops | bytes accessed | tf_op | source)
XLA Modules:
  0.0 81.1 jit_solution(8633224275022041551)
XLA Ops:
  1.0 1.0 %constant_dynamic-slice_fusion = (bf16[256,128]{1,0:T(8,128)(2,1)S(1)}, bf16[256,128]{1,0:T(8,128)(2,1)S(1)}, bf16[256,128]{1,0:T(8,128)(2,1)S(1)}, bf16[256,128]{1,0:T(8,128)(2,1)S(1)}) fusion(bf16[256,1024]{1,0:T(8,128)(2,1)} %param.7, s32[]{:T(128)S(6)} %select_n.52, s32[]{:T(128)S(6)} %add.92, bf16[256,1024]{1,0:T(8,128)(2,1)} %param.6), kind=kLoop, calls=%fused_computation.16 | loop fusion | bytes 524296 | tf_op jit(solution)/shard_map/slice | solution.py:251
  2.1 3.1 %collective-permute-start.2 = (bf16[272,512]{1,0:T(8,128)(2,1)S(1)}, bf16[272,512]{1,0:T(8,128)(2,1)S(1)}, u32[]{:S(2)}, u32[]{:S(2)}) collective-permute-start(bf16[272,512]{1,0:T(8,128)(2,1)S(1)} %maximum_maximum_fusion.refs_2_), channel_id=1, source_target_pairs={{0,8},{4,12},{8,16},{12,20},{16,24},{20,28},{24,0},{28,4},{1,9},{5... | collective-permute-start | bytes 835592 | tf_op jit(solution)/shard_map/ppermute | solution.py:265
  5.2 2.1 %collective-permute-start.4 = (bf16[272,512]{1,0:T(8,128)(2,1)S(1)}, bf16[272,512]{1,0:T(8,128)(2,1)S(1)}, u32[]{:S(2)}, u32[]{:S(2)}) collective-permute-start(bf16[272,512]{1,0:T(8,128)(2,1)S(1)} %maximum_maximum_fusion.refs_2_), channel_id=1, source_target_pairs={{0,24},{4,28},{8,0},{12,4},{16,8},{20,12},{24,16},{28,20},{1,25},{... | collective-permute-start | bytes 835592 | tf_op jit(solution)/shard_map/ppermute | solution.py:265
  7.3 0.9 %collective-permute-start = (bf16[272,512]{1,0:T(8,128)(2,1)S(1)}, bf16[272,512]{1,0:T(8,128)(2,1)S(1)}, u32[]{:S(2)}, u32[]{:S(2)}) collective-permute-start(bf16[272,512]{1,0:T(8,128)(2,1)S(1)} %maximum_maximum_fusion.refs_2_), channel_id=1, source_target_pairs={{0,16},{4,20},{8,24},{12,28},{16,0},{20,4},{24,8},{28,12},{1,17},{... | collective-permute-start | bytes 835592 | tf_op jit(solution)/shard_map/ppermute | solution.py:265
  8.2 1.5 %collective-permute-start.6 = (bf16[272,512]{1,0:T(8,128)(2,1)S(1)}, bf16[272,512]{1,0:T(8,128)(2,1)S(1)}, u32[]{:S(2)}, u32[]{:S(2)}) collective-permute-start(bf16[272,512]{1,0:T(8,128)(2,1)S(1)} %maximum_maximum_fusion.refs_2_), channel_id=1, source_target_pairs={{0,4},{4,0},{8,12},{12,8},{16,20},{20,16},{24,28},{28,24},{1,5},{5... | collective-permute-start | bytes 835592 | tf_op jit(solution)/shard_map/ppermute | solution.py:275
  9.7 5.0 %collective-permute-done.2.refs_3_ = bf16[272,512]{1,0:T(8,128)(2,1)S(1)} collective-permute-done((bf16[272,512]{1,0:T(8,128)(2,1)S(1)}, bf16[272,512]{1,0:T(8,128)(2,1)S(1)}, u32[]{:S(2)}, u32[]{:S(2)}) %collective-permute-start.2) | collective-permute-done | bytes 278560 | tf_op jit(solution)/shard_map/ppermute | solution.py:265
  14.7 1.7 %collective-permute-start.3 = (bf16[272,512]{1,0:T(8,128)(2,1)S(1)}, bf16[272,512]{1,0:T(8,128)(2,1)S(1)}, u32[]{:S(2)}, u32[]{:S(2)}) collective-permute-start(bf16[272,512]{1,0:T(8,128)(2,1)S(1)} %collective-permute-done.2.refs_3_), channel_id=1, source_target_pairs={{0,4},{4,0},{8,12},{12,8},{16,20},{20,16},{24,28},{28,24},{1,5},{5... | collective-permute-start | bytes 835592 | tf_op jit(solution)/shard_map/ppermute | solution.py:275
  16.5 2.8 %collective-permute-done.4.refs_4_ = bf16[272,512]{1,0:T(8,128)(2,1)S(1)} collective-permute-done((bf16[272,512]{1,0:T(8,128)(2,1)S(1)}, bf16[272,512]{1,0:T(8,128)(2,1)S(1)}, u32[]{:S(2)}, u32[]{:S(2)}) %collective-permute-start.4) | collective-permute-done | bytes 278560 | tf_op jit(solution)/shard_map/ppermute | solution.py:265
  19.3 1.5 %collective-permute-start.5 = (bf16[272,512]{1,0:T(8,128)(2,1)S(1)}, bf16[272,512]{1,0:T(8,128)(2,1)S(1)}, u32[]{:S(2)}, u32[]{:S(2)}) collective-permute-start(bf16[272,512]{1,0:T(8,128)(2,1)S(1)} %collective-permute-done.4.refs_4_), channel_id=1, source_target_pairs={{0,4},{4,0},{8,12},{12,8},{16,20},{20,16},{24,28},{28,24},{1,5},{5... | collective-permute-start | bytes 835592 | tf_op jit(solution)/shard_map/ppermute | solution.py:275
  20.7 1.2 %copy-done = bf16[256,2048]{1,0:T(8,128)(2,1)S(1)} copy-done((bf16[256,2048]{1,0:T(8,128)(2,1)S(1)}, bf16[256,2048]{1,0:T(8,128)(2,1)}, u32[]{:S(2)}) %copy-start) | copy-done | bytes 1048600
  22.6 2.6 %shard_map.55 = (f32[4,1,1024]{2,1,0:T(1,128)S(1)}, f32[4,1,1024]{2,1,0:T(1,128)S(1)}, f32[4,128,1024]{2,1,0:T(8,128)S(1)}) custom-call(s32[2]{0:T(128)S(1)} %copy-done.2, bf16[256,2048]{1,0:T(8,128)(2,1)S(1)} %copy-done, bf16[272,512]{1,0:T(8,128)(2,1)S(1)} %maximum_maximum_fusion.refs_2_), custom_call_target="tpu_custom_call" | custom-call | flops 536870912 | bytes 4194304 | tf_op jit(solution)/shard_map/pallas_call | solution.py:201
  25.3 1.3 %copy-done.4 = f32[4,128,1024]{2,1,0:T(8,128)} copy-done((f32[4,128,1024]{2,1,0:T(8,128)}, f32[4,128,1024]{2,1,0:T(8,128)S(1)}, u32[]{:S(2)}) %copy-start.4) | copy-done | bytes 2097176
  26.7 5.1 %collective-permute-done.refs_4_ = bf16[272,512]{1,0:T(8,128)(2,1)S(1)} collective-permute-done((bf16[272,512]{1,0:T(8,128)(2,1)S(1)}, bf16[272,512]{1,0:T(8,128)(2,1)S(1)}, u32[]{:S(2)}, u32[]{:S(2)}) %collective-permute-start) | collective-permute-done | bytes 278560 | tf_op jit(solution)/shard_map/ppermute | solution.py:265
  31.8 1.5 %collective-permute-start.1 = (bf16[272,512]{1,0:T(8,128)(2,1)S(1)}, bf16[272,512]{1,0:T(8,128)(2,1)S(1)}, u32[]{:S(2)}, u32[]{:S(2)}) collective-permute-start(bf16[272,512]{1,0:T(8,128)(2,1)S(1)} %collective-permute-done.refs_4_), channel_id=1, source_target_pairs={{0,4},{4,0},{8,12},{12,8},{16,20},{20,16},{24,28},{28,24},{1,5},{5... | collective-permute-start | bytes 835592 | tf_op jit(solution)/shard_map/ppermute | solution.py:275
  33.3 1.6 %copy-done.5 = f32[4,128,1024]{2,1,0:T(8,128)S(1)} copy-done((f32[4,128,1024]{2,1,0:T(8,128)S(1)}, f32[4,128,1024]{2,1,0:T(8,128)}, u32[]{:S(2)}) %copy-start.5) | copy-done | bytes 2097176
  34.8 5.1 %shard_map.56 = (f32[4,1,1024]{2,1,0:T(1,128)S(1)}, f32[4,1,1024]{2,1,0:T(1,128)S(1)}, f32[4,128,1024]{2,1,0:T(8,128)S(1)}) custom-call(s32[2]{0:T(128)S(1)} %copy-done.3, bf16[256,2048]{1,0:T(8,128)(2,1)S(1)} %copy-done.1, bf16[272,512]{1,0:T(8,128)(2,1)S(1)} %collective-permute-done.6.refs_2_, bf16[272,512]{1,0:T(8,128)(2,1)S(1)} %collective-permute-done.2.refs_3_, ...), custom_call_target="tpu_custom_call" | custom-call | flops 1610612736 | bytes 12582912 | tf_op jit(solution)/shard_map/pallas_call | solution.py:201
  40.0 5.1 %shard_map.57 = (f32[4,1,1024]{2,1,0:T(1,128)S(1)}, f32[4,1,1024]{2,1,0:T(1,128)S(1)}, f32[4,128,1024]{2,1,0:T(8,128)S(1)}) custom-call(s32[2]{0:T(128)S(1)} %copy-done.3, bf16[256,2048]{1,0:T(8,128)(2,1)S(1)} %copy-done.1, bf16[272,512]{1,0:T(8,128)(2,1)S(1)} %collective-permute-done.3.refs_2_, bf16[272,512]{1,0:T(8,128)(2,1)S(1)} %collective-permute-done.5.refs_3_, ...), custom_call_target="tpu_custom_call" | custom-call | flops 1610612736 | bytes 12582912 | tf_op jit(solution)/shard_map/pallas_call | solution.py:201
  45.1 6.5 %shard_map.58 = (bf16[256,2048]{1,0:T(8,128)(2,1)S(1)}, bf16[256,512]{1,0:T(8,128)(2,1)S(1)}, f32[256,512]{1,0:T(8,128)S(1)}) custom-call(s32[2]{0:T(128)S(1)} %copy-done.3, bf16[256,2048]{1,0:T(8,128)(2,1)S(1)} %copy-done.1, bf16[272,512]{1,0:T(8,128)(2,1)S(1)} %collective-permute-done.1.refs_2_, f32[4,1,1024]{2,1,0:T(1,128)S(1)} %get-tuple-element.27.refs_3_, ...), custom_call_target="tpu_custom_call" | custom-call | flops 1610612736 | bytes 4194304 | tf_op jit(solution)/shard_map/pallas_call | solution.py:201
  51.7 4.6 %shard_map.59 = (bf16[256,512]{1,0:T(8,128)(2,1)S(1)}, f32[256,512]{1,0:T(8,128)S(1)}) custom-call(s32[2]{0:T(128)S(1)} %get-tuple-element.37.at_ref, bf16[256,2048]{1,0:T(8,128)(2,1)S(1)} %get-tuple-element.30.rows_ref, bf16[2048,4096]{1,0:T(8,128)(2,1)} %weight_ref.3, bf16[256,512]{1,0:T(8,128)(2,1)S(1)} %get-tuple-element.31.refs_0_), custom_call_target="tpu_custom_call" | custom-call | flops 1073741824 | bytes 4194304 | tf_op jit(solution)/shard_map/pallas_call | solution.py:225
  56.9 0.9 %collective-permute-done.8 = bf16[256,512]{1,0:T(8,128)(2,1)S(1)} collective-permute-done((bf16[256,512]{1,0:T(8,128)(2,1)S(1)}, bf16[256,512]{1,0:T(8,128)(2,1)S(1)}, u32[]{:S(2)}, u32[]{:S(2)}) %collective-permute-start.8) | collective-permute-done | bytes 262176 | tf_op jit(solution)/shard_map/ppermute | solution.py:309
  58.3 7.4 %shard_map.60 = (bf16[256,1024]{1,0:T(8,128)(2,1)S(1)}, f32[256,1024]{1,0:T(8,128)S(1)}) custom-call(s32[2]{0:T(128)S(1)} %add_multiply_fusion.at_ref, bf16[256,2048]{1,0:T(8,128)(2,1)S(1)} %get-tuple-element.30.rows_ref, bf16[2048,4096]{1,0:T(8,128)(2,1)} %weight_ref.3, bf16[256,512]{1,0:T(8,128)(2,1)S(1)} %get-tuple-element.32.refs_0_, ...), custom_call_target="tpu_custom_call" | custom-call | flops 2147483648 | bytes 8388608 | tf_op jit(solution)/shard_map/pallas_call | solution.py:225
  65.9 1.5 %collective-permute-start.11 = (bf16[256,512]{1,0:T(8,128)(2,1)S(1)}, bf16[256,512]{1,0:T(8,128)(2,1)S(1)}, u32[]{:S(2)}, u32[]{:S(2)}) collective-permute-start(bf16[256,512]{1,0:T(8,128)(2,1)S(1)} %add_convert_fusion.refs_2_), channel_id=1, source_target_pairs={{0,2},{1,3},{2,0},{3,1},{4,6},{5,7},{6,4},{7,5},{8,10},{9,11},{10,... | collective-permute-start | bytes 786440 | tf_op jit(solution)/shard_map/ppermute | solution.py:313
  68.1 7.0 %collective-permute-done.11 = bf16[256,512]{1,0:T(8,128)(2,1)S(1)} collective-permute-done((bf16[256,512]{1,0:T(8,128)(2,1)S(1)}, bf16[256,512]{1,0:T(8,128)(2,1)S(1)}, u32[]{:S(2)}, u32[]{:S(2)}) %collective-permute-start.11) | collective-permute-done | bytes 262176 | tf_op jit(solution)/shard_map/ppermute | solution.py:313
  75.1 5.0 %collective-permute-done.10 = bf16[256,512]{1,0:T(8,128)(2,1)S(1)} collective-permute-done((bf16[256,512]{1,0:T(8,128)(2,1)S(1)}, bf16[256,512]{1,0:T(8,128)(2,1)S(1)}, u32[]{:S(2)}, u32[]{:S(2)}) %collective-permute-start.10) | collective-permute-done | bytes 262176 | tf_op jit(solution)/shard_map/ppermute | solution.py:313
  (32 shorter events, 4.8 us)
Async XLA Ops:
  0.0 33.2 %copy-start.3 = (s32[2]{0:T(128)S(1)}, s32[2]{0:T(128)}, u32[]{:S(2)}) copy-start(s32[2]{0:T(128)} %refs_0_.7) | copy-start | bytes 28
  0.0 33.3 %copy-start.1 = (bf16[256,2048]{1,0:T(8,128)(2,1)S(1)}, bf16[256,2048]{1,0:T(8,128)(2,1)}, u32[]{:S(2)}) copy-start(bf16[256,2048]{1,0:T(8,128)(2,1)} %refs_1_.7) | copy-start | bytes 3145732
  2.1 12.7 %collective-permute-start.2 = (bf16[272,512]{1,0:T(8,128)(2,1)S(1)}, bf16[272,512]{1,0:T(8,128)(2,1)S(1)}, u32[]{:S(2)}, u32[]{:S(2)}) collective-permute-start(bf16[272,512]{1,0:T(8,128)(2,1)S(1)} %maximum_maximum_fusion.refs_2_), channel_id=1, source_target_pairs={{0,8},{4,12},{8,16},{12,20},{16,24},{20,28},{24,0},{28,4},{1,9},{5... | collective-permute-start | bytes 835592 | tf_op jit(solution)/shard_map/ppermute | solution.py:265
  5.2 14.1 %collective-permute-start.4 = (bf16[272,512]{1,0:T(8,128)(2,1)S(1)}, bf16[272,512]{1,0:T(8,128)(2,1)S(1)}, u32[]{:S(2)}, u32[]{:S(2)}) collective-permute-start(bf16[272,512]{1,0:T(8,128)(2,1)S(1)} %maximum_maximum_fusion.refs_2_), channel_id=1, source_target_pairs={{0,24},{4,28},{8,0},{12,4},{16,8},{20,12},{24,16},{28,20},{1,25},{... | collective-permute-start | bytes 835592 | tf_op jit(solution)/shard_map/ppermute | solution.py:265
  7.3 24.5 %collective-permute-start = (bf16[272,512]{1,0:T(8,128)(2,1)S(1)}, bf16[272,512]{1,0:T(8,128)(2,1)S(1)}, u32[]{:S(2)}, u32[]{:S(2)}) collective-permute-start(bf16[272,512]{1,0:T(8,128)(2,1)S(1)} %maximum_maximum_fusion.refs_2_), channel_id=1, source_target_pairs={{0,16},{4,20},{8,24},{12,28},{16,0},{20,4},{24,8},{28,12},{1,17},{... | collective-permute-start | bytes 835592 | tf_op jit(solution)/shard_map/ppermute | solution.py:265
  8.2 25.0 %collective-permute-start.6 = (bf16[272,512]{1,0:T(8,128)(2,1)S(1)}, bf16[272,512]{1,0:T(8,128)(2,1)S(1)}, u32[]{:S(2)}, u32[]{:S(2)}) collective-permute-start(bf16[272,512]{1,0:T(8,128)(2,1)S(1)} %maximum_maximum_fusion.refs_2_), channel_id=1, source_target_pairs={{0,4},{4,0},{8,12},{12,8},{16,20},{20,16},{24,28},{28,24},{1,5},{5... | collective-permute-start | bytes 835592 | tf_op jit(solution)/shard_map/ppermute | solution.py:275
  14.7 25.2 %collective-permute-start.3 = (bf16[272,512]{1,0:T(8,128)(2,1)S(1)}, bf16[272,512]{1,0:T(8,128)(2,1)S(1)}, u32[]{:S(2)}, u32[]{:S(2)}) collective-permute-start(bf16[272,512]{1,0:T(8,128)(2,1)S(1)} %collective-permute-done.2.refs_3_), channel_id=1, source_target_pairs={{0,4},{4,0},{8,12},{12,8},{16,20},{20,16},{24,28},{28,24},{1,5},{5... | collective-permute-start | bytes 835592 | tf_op jit(solution)/shard_map/ppermute | solution.py:275
  19.3 20.7 %collective-permute-start.5 = (bf16[272,512]{1,0:T(8,128)(2,1)S(1)}, bf16[272,512]{1,0:T(8,128)(2,1)S(1)}, u32[]{:S(2)}, u32[]{:S(2)}) collective-permute-start(bf16[272,512]{1,0:T(8,128)(2,1)S(1)} %collective-permute-done.4.refs_4_), channel_id=1, source_target_pairs={{0,4},{4,0},{8,12},{12,8},{16,20},{20,16},{24,28},{28,24},{1,5},{5... | collective-permute-start | bytes 835592 | tf_op jit(solution)/shard_map/ppermute | solution.py:275
  20.7 1.2 %copy-start = (bf16[256,2048]{1,0:T(8,128)(2,1)S(1)}, bf16[256,2048]{1,0:T(8,128)(2,1)}, u32[]{:S(2)}) copy-start(bf16[256,2048]{1,0:T(8,128)(2,1)} %refs_1_.7) | copy-start | bytes 3145732
  22.0 0.7 copy-start.2
  25.3 1.3 %copy-start.4 = (f32[4,128,1024]{2,1,0:T(8,128)}, f32[4,128,1024]{2,1,0:T(8,128)S(1)}, u32[]{:S(2)}) copy-start(f32[4,128,1024]{2,1,0:T(8,128)S(1)} %get-tuple-element.23.refs_7_) | copy-start | bytes 6291460
  31.8 13.4 %collective-permute-start.1 = (bf16[272,512]{1,0:T(8,128)(2,1)S(1)}, bf16[272,512]{1,0:T(8,128)(2,1)S(1)}, u32[]{:S(2)}, u32[]{:S(2)}) collective-permute-start(bf16[272,512]{1,0:T(8,128)(2,1)S(1)} %collective-permute-done.refs_4_), channel_id=1, source_target_pairs={{0,4},{4,0},{8,12},{12,8},{16,20},{20,16},{24,28},{28,24},{1,5},{5... | collective-permute-start | bytes 835592 | tf_op jit(solution)/shard_map/ppermute | solution.py:275
  33.3 1.6 %copy-start.5 = (f32[4,128,1024]{2,1,0:T(8,128)S(1)}, f32[4,128,1024]{2,1,0:T(8,128)}, u32[]{:S(2)}) copy-start(f32[4,128,1024]{2,1,0:T(8,128)} %copy-done.4) | copy-start | bytes 6291460
  56.3 1.6 %collective-permute-start.8 = (bf16[256,512]{1,0:T(8,128)(2,1)S(1)}, bf16[256,512]{1,0:T(8,128)(2,1)S(1)}, u32[]{:S(2)}, u32[]{:S(2)}) collective-permute-start(bf16[256,512]{1,0:T(8,128)(2,1)S(1)} %get-tuple-element.32.refs_0_), channel_id=1, source_target_pairs={{0,1},{1,0},{2,3},{3,2},{4,5},{5,4},{6,7},{7,6},{8,9},{9,8},{10,11... | collective-permute-start | bytes 786440 | tf_op jit(solution)/shard_map/ppermute | solution.py:309
  56.4 1.9 %collective-permute-start.7 = (bf16[256,512]{1,0:T(8,128)(2,1)S(1)}, bf16[256,512]{1,0:T(8,128)(2,1)S(1)}, u32[]{:S(2)}, u32[]{:S(2)}) collective-permute-start(bf16[256,512]{1,0:T(8,128)(2,1)S(1)} %get-tuple-element.31.refs_0_), channel_id=1, source_target_pairs={{0,1},{1,0},{2,3},{3,2},{4,5},{5,4},{6,7},{7,6},{8,9},{9,8},{10,11... | collective-permute-start | bytes 786440 | tf_op jit(solution)/shard_map/ppermute | solution.py:309
  65.7 2.2 %collective-permute-start.9 = (bf16[256,1024]{1,0:T(8,128)(2,1)S(1)}, bf16[256,1024]{1,0:T(8,128)(2,1)S(1)}, u32[]{:S(2)}, u32[]{:S(2)}) collective-permute-start(bf16[256,1024]{1,0:T(8,128)(2,1)S(1)} %get-tuple-element.36), channel_id=1, source_target_pairs={{0,1},{1,0},{2,3},{3,2},{4,5},{5,4},{6,7},{7,6},{8,9},{9,8},{10,11... | collective-permute-start | bytes 1572872 | tf_op jit(solution)/shard_map/ppermute | solution.py:309
  65.9 9.2 %collective-permute-start.11 = (bf16[256,512]{1,0:T(8,128)(2,1)S(1)}, bf16[256,512]{1,0:T(8,128)(2,1)S(1)}, u32[]{:S(2)}, u32[]{:S(2)}) collective-permute-start(bf16[256,512]{1,0:T(8,128)(2,1)S(1)} %add_convert_fusion.refs_2_), channel_id=1, source_target_pairs={{0,2},{1,3},{2,0},{3,1},{4,6},{5,7},{6,4},{7,5},{8,10},{9,11},{10,... | collective-permute-start | bytes 786440 | tf_op jit(solution)/shard_map/ppermute | solution.py:313
  67.4 12.7 %collective-permute-start.10 = (bf16[256,512]{1,0:T(8,128)(2,1)S(1)}, bf16[256,512]{1,0:T(8,128)(2,1)S(1)}, u32[]{:S(2)}, u32[]{:S(2)}) collective-permute-start(bf16[256,512]{1,0:T(8,128)(2,1)S(1)} %add_convert_fusion.1.refs_1_), channel_id=1, source_target_pairs={{0,2},{1,3},{2,0},{3,1},{4,6},{5,7},{6,4},{7,5},{8,10},{9,11},{10,... | collective-permute-start | bytes 786440 | tf_op jit(solution)/shard_map/ppermute | solution.py:313

commit v2 on v0

v2 whole, which is shorter than its diff:
```python
import functools
import math

import jax
import jax.numpy as jnp
from jax import lax
from jax.experimental import pallas as pl
from jax.experimental.pallas import tpu as pltpu
from jax.sharding import PartitionSpec as P

QUERY_HEADS = 64
KEY_VALUE_HEADS = 8
HEAD_SIZE = 128
HIDDEN = -1e30
TAIL = 16
DIGIT = 128
NT = (((1,), (1,)), ((), ()))
DEPTH = 3
VMEM_LIMIT = 16 << 20
WIDE_LIMIT = 48 << 20


WHOLE = pl.BlockSpec(memory_space=pltpu.VMEM)
SCALARS = pl.BlockSpec(memory_space=pltpu.SMEM)
UNREAD = pl.BlockSpec(memory_space=pl.ANY)


def lanes(n):
    return slice(n * HEAD_SIZE, (n + 1) * HEAD_SIZE)


def pack_kernel(kv_heads, at_ref, order_ref, keys_ref, values_ref, whole_ref, *head_refs):
    tokens = keys_ref.shape[0]
    line = lax.broadcasted_iota(jnp.int32, (TAIL, HEAD_SIZE), 0)
    tail = jnp.zeros((TAIL, HEAD_SIZE), jnp.int32)
    for part in range(order_ref.shape[0]):
        number = order_ref[part]
        tail = jnp.where(line == 2 * part, number // DIGIT, tail)
        tail = jnp.where(line == 2 * part + 1, number % DIGIT, tail)
    tail = tail.astype(jnp.float32).astype(jnp.bfloat16)
    for k in range(kv_heads):
        column = pl.multiple_of(at_ref[0] + k * HEAD_SIZE, HEAD_SIZE)
        for n, ref in enumerate((keys_ref, values_ref)):
            part = ref[:, pl.ds(column, HEAD_SIZE)]
            outs = [(whole_ref, 2 * k + n)] + [(ref, n) for ref in head_refs[k : k + 1]]
            for out, place in outs:
                out[0:tokens, lanes(place)] = part
                out[tokens : tokens + TAIL, lanes(place)] = tail


def pack(at, order, keys, values, kv_heads):
    rows = keys.shape[0] + TAIL
    out_shape = [jax.ShapeDtypeStruct((rows, 2 * kv_heads * HEAD_SIZE), jnp.bfloat16)]
    if kv_heads > 1:
        out_shape += [jax.ShapeDtypeStruct((rows, 2 * HEAD_SIZE), jnp.bfloat16)] * kv_heads
    found = pl.pallas_call(
        functools.partial(pack_kernel, kv_heads),
        in_specs=[SCALARS, SCALARS, WHOLE, WHOLE],
        out_specs=[WHOLE] * len(out_shape),
        out_shape=out_shape,
        compiler_params=pltpu.CompilerParams(vmem_limit_bytes=VMEM_LIMIT),
        cost_estimate=pl.CostEstimate(
            flops=rows * 4096, bytes_accessed=4 * rows * 1024, transcendentals=0
        ),
    )(at, order, keys, values)
    return found[0], found[1:] if kv_heads > 1 else found


class Columns:
    def __init__(self, at_ref, weight_ref, buffer, sem, outs):
        wide = buffer.shape[2]
        self.buffer = buffer
        self.copies, self.places = [], []
        for run, out in enumerate(outs):
            for tile in range(out.shape[1] // wide):
                column = pl.multiple_of(at_ref[run] + tile * wide, wide)
                n = len(self.copies)
                source = weight_ref.at[:, pl.ds(column, wide)]
                self.copies.append(pltpu.make_async_copy(source, buffer.at[n], sem.at[n]))
                self.places.append((out, slice(tile * wide, (tile + 1) * wide)))
        for copy in self.copies[:DEPTH]:
            copy.start()

    def multiply(self, rows_refs):
        for n, (copy, (out, at)) in enumerate(zip(self.copies, self.places)):
            copy.wait()
            if n + DEPTH < len(self.copies):
                self.copies[n + DEPTH].start()
            product, depth = None, 0
            for ref in rows_refs:
                held = self.buffer[n, depth : depth + ref.shape[1], :]
                part = jnp.dot(ref[...], held, preferred_element_type=jnp.float32)
                product = part if product is None else product + part
                depth += ref.shape[1]
            out[:, at] = product.astype(out.dtype)


def product_shapes(tokens, columns):
    return [
        jax.ShapeDtypeStruct((tokens, columns), jnp.bfloat16),
        jax.ShapeDtypeStruct((tokens, columns), jnp.float32),
    ]


def column_scratch(depth, columns):
    wide = math.gcd(columns, 256)
    tiles = 2 * columns // wide
    return [pltpu.VMEM((tiles, depth, wide), jnp.bfloat16), pltpu.SemaphoreType.DMA((tiles,))]


def attend_kernel(head, heads, places, first, last, earlier, scale, span, *refs):
    order_ref, q_ref = refs[:2]
    blocks = refs[2 : 2 + len(places)]
    refs = refs[2 + len(places) :]
    if not first:
        old_top, old_total, old_acc = refs[:3]
        refs = refs[3:]
    columns = None
    if earlier is not None:
        at_ref, weight_ref = refs[:2]
        earlier_refs = refs[2 : 2 + earlier]
        buffer, sem = refs[-2:]
        refs = refs[2 + earlier : -2]
        columns = Columns(at_ref, weight_ref, buffer, sem, refs[1:3])
    outs = refs[:-6]
    bias_ref, flip_ref = refs[-6:-4]
    score_refs, weight_refs = refs[-4:-2], refs[-2:]
    parts = order_ref.shape[0]
    rows = q_ref.shape[0] // parts
    pair = span // rows
    lengths = [block.shape[0] - TAIL for block in blocks]
    offsets = [sum(lengths[:b]) for b in range(len(blocks))]

    key_at = lax.broadcasted_iota(jnp.int32, (rows, rows), 0).astype(jnp.float32)
    query_iota = lax.broadcasted_iota(jnp.int32, (rows, rows), 1)
    for block, place, length, offset in zip(blocks, places, lengths, offsets):
        tail = block[length : length + TAIL, lanes(0)].astype(jnp.float32)
        for part in range(length // rows):
            high, low = tail[2 * part : 2 * part + 1, :], tail[2 * part + 1 : 2 * part + 2, :]
            key_pos = (high * DIGIT + low)[:, 0:rows] * float(rows) + key_at
            at = slice(offset + part * rows, offset + (part + 1) * rows)
            for i in range(parts):
                query_pos = (query_iota + order_ref[i] * rows).astype(jnp.float32)
                bias_ref[i, at, :] = jnp.where(key_pos > query_pos, HIDDEN, 0.0)
        flip_ref[:, offset : offset + length] = block[0:length, lanes(2 * place + 1)].T

    pieces = [(i, p) for i in range(parts) for p in range(heads // pair)]
    tops, totals = {}, {}

    def score(t):
        i, p = pieces[t]
        found = [
            q_ref[i * rows : (i + 1) * rows, lanes(head * heads + p * pair + j)]
            for j in range(pair)
        ]
        q = jnp.concatenate(found, axis=0)
        top = None
        for block, place, length, offset in zip(blocks, places, lengths, offsets):
            key = block[0:length, lanes(2 * place)]
            tile = bias_ref[i, offset : offset + length, :]
            scores = lax.dot_general(key, q, NT, preferred_element_type=jnp.float32)
            scores = scores * scale + jnp.concatenate([tile] * pair, axis=1)
            score_refs[t % 2][offset : offset + length, :] = scores
            part = jnp.max(scores, axis=0, keepdims=True)
            top = part if top is None else jnp.maximum(top, part)
        if not first:
            top = jnp.maximum(top, old_top[i, :, p * span : (p + 1) * span])
        tops[t] = top

    def weigh(t):
        weights = jnp.exp2(score_refs[t % 2][...] - tops[t])
        totals[t] = jnp.sum(weights, axis=0, keepdims=True)
        weight_refs[t % 2][...] = weights.astype(jnp.bfloat16)

    def spread(t):
        i, p = pieces[t]
        at = slice(p * span, (p + 1) * span)
        acc = jnp.dot(flip_ref[...], weight_refs[t % 2][...], preferred_element_type=jnp.float32)
        total = totals[t]
        if not first:
            factor = jnp.exp2(old_top[i, :, at] - tops[t])
            total = total + old_total[i, :, at] * factor
            acc = acc + old_acc[i, :, at] * factor
        if last:
            done = (acc * (1.0 / total)).T.astype(jnp.bfloat16)
            for j in range(pair):
                outs[0][i * rows : (i + 1) * rows, lanes(p * pair + j)] = done[
                    j * rows : (j + 1) * rows, :
                ]
        else:
            outs[0][i, :, at] = tops[t]
            outs[1][i, :, at] = total
            outs[2][i, :, at] = acc

    for t in range(len(pieces) + 2):
        if t < len(pieces):
            score(t)
        if t >= 2:
            spread(t - 2)
        if 1 <= t <= len(pieces):
            weigh(t - 1)
    if columns is not None:
        columns.multiply((*earlier_refs, outs[0]))


def attend(order, queries, kv_heads, head, blocks, state, last=False, then=None):
    tokens, width = queries.shape
    parts = order.shape[0]
    rows = tokens // parts
    heads = width // kv_heads // HEAD_SIZE
    span = math.gcd(heads, 2) * rows
    scale = math.log2(math.e) / math.sqrt(HEAD_SIZE)
    first = state is None
    arrays = [array for array, _ in blocks]
    places = [place for _, place in blocks]
    seen = sum(array.shape[0] - TAIL for array in arrays)
    pairs = tokens * heads * seen
    operands = [order, queries, *arrays, *(() if first else state)]
    in_specs = [SCALARS] + [WHOLE] * (len(operands) - 1)
    scratch = [
        pltpu.VMEM((parts, seen, rows), jnp.float32),
        pltpu.VMEM((HEAD_SIZE, seen), jnp.bfloat16),
    ]
    scratch += [pltpu.VMEM((seen, span), jnp.float32)] * 2
    scratch += [pltpu.VMEM((seen, span), jnp.bfloat16)] * 2
    flops = 4 * pairs * HEAD_SIZE
    if last:
        out_shape = [jax.ShapeDtypeStruct((tokens, heads * HEAD_SIZE), jnp.bfloat16)]
    else:
        out_shape = [
            jax.ShapeDtypeStruct((parts, 1, heads * rows), jnp.float32),
            jax.ShapeDtypeStruct((parts, 1, heads * rows), jnp.float32),
            jax.ShapeDtypeStruct((parts, HEAD_SIZE, heads * rows), jnp.float32),
        ]
    earlier = None
    if then is not None:
        at, weight, columns, done = then
        earlier = len(done)
        operands += [at, weight, *done]
        in_specs += [SCALARS, UNREAD] + [WHOLE] * earlier
        out_shape += product_shapes(tokens, columns)
        scratch += column_scratch(width, columns)
        flops += 4 * tokens * width * columns
    return pl.pallas_call(
        functools.partial(
            attend_kernel, head, heads, places, first, last, earlier, scale, span
        ),
        in_specs=in_specs,
        out_specs=[WHOLE] * len(out_shape),
        out_shape=out_shape,
        scratch_shapes=scratch,
        compiler_params=pltpu.CompilerParams(
            vmem_limit_bytes=VMEM_LIMIT if then is None else WIDE_LIMIT,
        ),
        cost_estimate=pl.CostEstimate(
            flops=flops, bytes_accessed=4 * pairs, transcendentals=pairs
        ),
    )(*operands)


def project_kernel(n_rows, at_ref, weight_ref, *refs):
    send_ref, keep_ref, buffer, sem = refs[-4:]
    columns = Columns(at_ref, weight_ref, buffer, sem, (send_ref, keep_ref))
    columns.multiply(refs[:n_rows])


def project(at, attended, weight, columns, after):
    tokens, depth = attended[0].shape[0], weight.shape[0]
    return pl.pallas_call(
        functools.partial(project_kernel, len(attended)),
        in_specs=[SCALARS, UNREAD] + [WHOLE] * len(attended) + [UNREAD] * len(after),
        out_specs=[WHOLE] * 2,
        out_shape=product_shapes(tokens, columns),
        scratch_shapes=column_scratch(depth, columns),
        compiler_params=pltpu.CompilerParams(vmem_limit_bytes=WIDE_LIMIT),
        cost_estimate=pl.CostEstimate(
            flops=4 * tokens * depth * columns,
            bytes_accessed=4 * depth * columns,
            transcendentals=0,
        ),
    )(at, weight, *attended, *after)


def shards(n_ctx, n_tp, queries, keys, values, out_weight, block_order):
    heads_dev = queries.shape[1] // HEAD_SIZE
    group_size = QUERY_HEADS // KEY_VALUE_HEADS
    kv_heads = max(1, heads_dev // group_size)
    tp = lax.axis_index("tp")
    start = (tp * heads_dev // group_size * HEAD_SIZE).astype(jnp.int32)
    own, own_heads = pack(start[None], block_order, keys, values, kv_heads)

    inner = math.gcd(n_ctx, 2)
    outer = n_ctx // inner

    def along_outer(block, k):
        pairs = [
            (o * inner + i, (o + k) % outer * inner + i) for o in range(outer) for i in range(inner)
        ]
        return lax.ppermute(block, "ctx", pairs)

    def along_inner(block):
        found = []
        for k in range(1, inner):
            pairs = [
                (o * inner + i, o * inner + (i + k) % inner)
                for o in range(outer)
                for i in range(inner)
            ]
            found.append(lax.ppermute(block, "ctx", pairs))
        return found

    half = outer // 2
    moved = {}
    for k in range(1, half):
        for shift in (k, outer - k):
            moved[shift] = along_outer(own, shift)
    split = [along_outer(x, half) for x in own_heads] if half else []
    arrived = along_inner(own)
    before = []
    for k in range(1, half):
        for shift in (k, outer - k):
            arrived.append(moved[shift])
        arrived += before
        before = []
        for shift in (k, outer - k):
            before += along_inner(moved[shift])
    arrived += before
    final = [along_inner(x) for x in split]

    share = out_weight.shape[1] // n_tp
    cores = math.gcd(n_tp, 2)
    groups = n_tp // cores
    core, group = tp % cores, tp // cores
    cuts = [0, share // 4, share] if groups == 2 else [0, share]
    jobs = [(cut, r) for cut in range(len(cuts) - 1) for r in range(1, groups)]

    def begins(cut, r):
        to = (group + r) % groups * cores
        at = jnp.stack([to + (core + 1) % cores, to + core]) * share + cuts[cut]
        return at.astype(jnp.int32)

    def to_core(x):
        pairs = [(t, t // cores * cores + (t + 1) % cores) for t in range(n_tp)]
        return lax.ppermute(x, "tp", pairs)

    def to_group(x, r):
        pairs = [(t, (t + r * cores) % n_tp) for t in range(n_tp)]
        return lax.ppermute(x, "tp", pairs)

    tail, tail_at = (jobs[0], cuts[jobs[0][0] + 1] - cuts[jobs[0][0]]) if jobs else ((0, 0), share)
    attended = []
    batch = 3
    for head in range(kv_heads):
        stages = [[(own, head)]]
        stages += [
            [(x, head) for x in arrived[i : i + batch]] for i in range(0, len(arrived), batch)
        ]
        if split:
            if len(stages[-1]) < batch:
                stages[-1] = stages[-1] + [(split[head], 0)]
            else:
                stages.append([(split[head], 0)])
            stages += [[(x, 0)] for x in final[head]]
        state = None
        for index, blocks in enumerate(stages):
            last = index == len(stages) - 1
            then = None
            if last and head == kv_heads - 1:
                then = (begins(*tail), out_weight, tail_at, attended)
            state = attend(block_order, queries, kv_heads, head, blocks, state, last, then)
        attended = attended + [state[0]]
    send, keep = state[1:]

    partial = []
    for name, (cut, r) in enumerate(jobs):
        if name > 0:
            send, keep = project(
                begins(cut, r), attended, out_weight, cuts[cut + 1] - cuts[cut], (send,)
            )
        partial.append((to_core(send) if cores > 1 else None, keep))
    arriving = [[] for _ in cuts[1:]]
    after = (send,)
    for (cut, r), (other, keep) in zip(jobs, partial):
        if other is not None:
            keep = keep + other.astype(jnp.float32)
        summed = keep.astype(jnp.bfloat16)
        after += (summed,)
        arriving[cut].append(to_group(summed, r))
    if jobs:
        send, keep = project(begins(0, 0), attended, out_weight, share, after)
    mine = keep
    if cores > 1:
        mine = mine + to_core(send).astype(jnp.float32)
    result = []
    for cut, others in enumerate(arriving):
        total = mine[:, cuts[cut] : cuts[cut + 1]]
        for x in others:
            total = total + x.astype(jnp.float32)
        result.append(total.astype(jnp.bfloat16))
    return jnp.concatenate(result, axis=1)


def solution(mesh):
    in_specs = (P("ctx", "tp"), P("ctx", None), P("ctx", None), P("tp", None), P("ctx"))
    out_specs = P("ctx", "tp")

    def layer(*args):
        return shards(mesh.shape["ctx"], mesh.shape["tp"], *args)

    return jax.shard_map(
        layer, mesh=mesh, in_specs=in_specs, out_specs=out_specs, check_vma=False
    )
```

time: 85.6 us -> 86.7 us (1.013)
  Pallas kernels: 22.3 us -> 37 us
  local copies, waits for them, and re-layouts: 19.1 us -> 7.82 us
  waiting for transfers between devices: 26.1 us -> 21.9 us
  starting transfers between devices: 15.1 us -> 18 us
  other arithmetic: 2.39 us -> 1.38 us
    pallas_call x7 -> x11, Pallas kernels: 22.3 us -> 37 us  [the longest x8 22.4 us: attend(): pl.pallas_call(functools.partial(attend_kernel, head, heads, places, firs...]
    unnamed x24 -> x20, local copies, waits for them, and re-layouts: 18 us -> 7.82 us
    ppermute x3 -> x4, waiting for transfers between devices: 12.9 us -> 8.66 us  [along_outer(): return lax.ppermute(block, 'ctx', pairs)]
    ppermute x3 -> x4, starting transfers between devices: 6.14 us -> 8 us  [along_outer(): return lax.ppermute(block, 'ctx', pairs)]
    ppermute x4 -> x5, starting transfers between devices: 6.18 us -> 7.18 us  [along_inner(): found.append(lax.ppermute(block, 'ctx', pairs))]
    slice x1 -> x0, local copies, waits for them, and re-layouts: 0.96 us -> none  [shards(): pieces += [own_keys[:, at], own_values[:, at]]]
    another operation x4 -> x0, other arithmetic: 0.92 us -> none  [the longest x2 0.77 us: shards(): jnp.stack([block_order // DIGIT, block_order % DIGIT], axis=1).reshape(-1)]
  transfers between devices with their start and end apart: 12 -> 14, of which waited for: 7 -> 6; matrix products, arithmetic and copies ran while one was open for 0% -> 0% of each run, Pallas kernels for 15% -> 21%
where the time goes in v2:
time: 86.7 us; the launch traced here: 86.3 us
  Pallas kernels  37 us (43%)
  waiting for transfers between devices  21.9 us (25%)
  starting transfers between devices  18 us (21%)
  local copies, waits for them, and re-layouts  7.82 us (9%)
  other arithmetic  1.38 us (2%)
    pallas_call x8, Pallas kernels, attend(): pl.pallas_call(functools.partial(attend_kernel, head, heads, places, firs...  22.4 us
    pallas_call x2, Pallas kernels, project(): pl.pallas_call(functools.partial(project_kernel, len(attended)), in_specs...  13.3 us
    ppermute x2, waiting for transfers between devices, to_group(): return lax.ppermute(x, 'tp', pairs)  11.9 us
    ppermute x4, waiting for transfers between devices, along_outer(): return lax.ppermute(block, 'ctx', pairs)  8.66 us
    ppermute x4, starting transfers between devices, along_outer(): return lax.ppermute(block, 'ctx', pairs)  8 us
    unnamed x20, local copies, waits for them, and re-layouts  7.82 us
    ppermute x5, starting transfers between devices, along_inner(): found.append(lax.ppermute(block, 'ctx', pairs))  7.18 us
    ppermute x2, starting transfers between devices, to_group(): return lax.ppermute(x, 'tp', pairs)  2.03 us
  transfers between devices with their start and end apart: 14, of which 6 were waited for; matrix products, arithmetic and copies ran while one was open for 0% of the time, Pallas kernels for 21%

profile of v2, /device:TPU:0, one launch (start us, length us, event | category | flops | bytes accessed | tf_op | source)
XLA Modules:
  0.0 86.3 jit_solution(11761824672648727847)
XLA Ops:
  4.1 3.1 %collective-permute-start.2 = (bf16[272,512]{1,0:T(8,128)(2,1)S(1)}, bf16[272,512]{1,0:T(8,128)(2,1)S(1)}, u32[]{:S(2)}, u32[]{:S(2)}) collective-permute-start(bf16[272,512]{1,0:T(8,128)(2,1)S(1)} %get-tuple-element.34.refs_2_), channel_id=1, source_target_pairs={{0,8},{4,12},{8,16},{12,20},{16,24},{20,28},{24,0},{28,4},{1,9},{5... | collective-permute-start | bytes 835592 | tf_op jit(solution)/shard_map/ppermute | solution.py:299
  7.2 2.0 %collective-permute-start.4 = (bf16[272,512]{1,0:T(8,128)(2,1)S(1)}, bf16[272,512]{1,0:T(8,128)(2,1)S(1)}, u32[]{:S(2)}, u32[]{:S(2)}) collective-permute-start(bf16[272,512]{1,0:T(8,128)(2,1)S(1)} %get-tuple-element.34.refs_2_), channel_id=1, source_target_pairs={{0,24},{4,28},{8,0},{12,4},{16,8},{20,12},{24,16},{28,20},{1,25},{... | collective-permute-start | bytes 835592 | tf_op jit(solution)/shard_map/ppermute | solution.py:299
  9.2 1.7 %collective-permute-start.6 = (bf16[272,512]{1,0:T(8,128)(2,1)S(1)}, bf16[272,512]{1,0:T(8,128)(2,1)}, u32[]{:S(2)}, u32[]{:S(2)}) collective-permute-start(bf16[272,512]{1,0:T(8,128)(2,1)S(1)} %get-tuple-element.34.refs_2_), channel_id=1, source_target_pairs={{0,4},{4,0},{8,12},{12,8},{16,20},{20,16},{24,28},{28,24},{1,5},{5... | collective-permute-start | bytes 835592 | tf_op jit(solution)/shard_map/ppermute | solution.py:309
  11.7 2.1 %collective-permute-start.7 = (bf16[272,256]{1,0:T(8,128)(2,1)S(1)}, bf16[272,256]{1,0:T(8,128)(2,1)S(1)}, u32[]{:S(2)}, u32[]{:S(2)}) collective-permute-start(bf16[272,256]{1,0:T(8,128)(2,1)S(1)} %get-tuple-element.44), channel_id=1, source_target_pairs={{0,16},{4,20},{8,24},{12,28},{16,0},{20,4},{24,8},{28,12},{1,17},{... | collective-permute-start | bytes 417800 | tf_op jit(solution)/shard_map/ppermute | solution.py:299
  15.7 1.7 %shard_map.56 = (f32[2,1,1024]{2,1,0:T(1,128)S(1)}, f32[2,1,1024]{2,1,0:T(1,128)S(1)}, f32[2,128,1024]{2,1,0:T(8,128)S(1)}) custom-call(s32[2]{0:T(128)S(1)} %copy-done.7, bf16[256,2048]{1,0:T(8,128)(2,1)S(1)} %copy-done, bf16[272,512]{1,0:T(8,128)(2,1)S(1)} %get-tuple-element.34.refs_2_), custom_call_target="tpu_custom_call" | custom-call | flops 268435456 | bytes 2097152 | tf_op jit(solution)/shard_map/pallas_call | solution.py:244
  18.4 2.8 %collective-permute-done.4.refs_4_ = bf16[272,512]{1,0:T(8,128)(2,1)S(1)} collective-permute-done((bf16[272,512]{1,0:T(8,128)(2,1)S(1)}, bf16[272,512]{1,0:T(8,128)(2,1)S(1)}, u32[]{:S(2)}, u32[]{:S(2)}) %collective-permute-start.4) | collective-permute-done | bytes 278560 | tf_op jit(solution)/shard_map/ppermute | solution.py:299
  21.2 1.5 %collective-permute-start.5 = (bf16[272,512]{1,0:T(8,128)(2,1)S(1)}, bf16[272,512]{1,0:T(8,128)(2,1)S(1)}, u32[]{:S(2)}, u32[]{:S(2)}) collective-permute-start(bf16[272,512]{1,0:T(8,128)(2,1)S(1)} %collective-permute-done.4.refs_4_), channel_id=1, source_target_pairs={{0,4},{4,0},{8,12},{12,8},{16,20},{20,16},{24,28},{28,24},{1,5},{5... | collective-permute-start | bytes 835592 | tf_op jit(solution)/shard_map/ppermute | solution.py:309
  24.6 1.7 %shard_map.60 = (f32[2,1,1024]{2,1,0:T(1,128)S(1)}, f32[2,1,1024]{2,1,0:T(1,128)S(1)}, f32[2,128,1024]{2,1,0:T(8,128)S(1)}) custom-call(s32[2]{0:T(128)S(1)} %copy-done.8, bf16[256,2048]{1,0:T(8,128)(2,1)S(1)} %copy-done.1, bf16[272,512]{1,0:T(8,128)(2,1)S(1)} %get-tuple-element.34.refs_2_), custom_call_target="tpu_custom_call" | custom-call | flops 268435456 | bytes 2097152 | tf_op jit(solution)/shard_map/pallas_call | solution.py:244
  26.4 4.5 %collective-permute-done.refs_4_ = bf16[272,256]{1,0:T(8,128)(2,1)S(1)} collective-permute-done((bf16[272,256]{1,0:T(8,128)(2,1)}, bf16[272,256]{1,0:T(8,128)(2,1)S(1)}, u32[]{:S(2)}, u32[]{:S(2)}) %collective-permute-start) | collective-permute-done | bytes 139296 | tf_op jit(solution)/shard_map/ppermute | solution.py:299
  30.9 1.5 %collective-permute-start.1 = (bf16[272,256]{1,0:T(8,128)(2,1)S(1)}, bf16[272,256]{1,0:T(8,128)(2,1)S(1)}, u32[]{:S(2)}, u32[]{:S(2)}) collective-permute-start(bf16[272,256]{1,0:T(8,128)(2,1)S(1)} %collective-permute-done.refs_4_), channel_id=1, source_target_pairs={{0,4},{4,0},{8,12},{12,8},{16,20},{20,16},{24,28},{28,24},{1,5},{5... | collective-permute-start | bytes 417800 | tf_op jit(solution)/shard_map/ppermute | solution.py:309
  32.3 1.4 %collective-permute-done.7.refs_4_ = bf16[272,256]{1,0:T(8,128)(2,1)S(1)} collective-permute-done((bf16[272,256]{1,0:T(8,128)(2,1)S(1)}, bf16[272,256]{1,0:T(8,128)(2,1)S(1)}, u32[]{:S(2)}, u32[]{:S(2)}) %collective-permute-start.7) | collective-permute-done | bytes 139296 | tf_op jit(solution)/shard_map/ppermute | solution.py:299
  33.7 1.5 %collective-permute-start.8 = (bf16[272,256]{1,0:T(8,128)(2,1)S(1)}, bf16[272,256]{1,0:T(8,128)(2,1)S(1)}, u32[]{:S(2)}, u32[]{:S(2)}) collective-permute-start(bf16[272,256]{1,0:T(8,128)(2,1)S(1)} %collective-permute-done.7.refs_4_), channel_id=1, source_target_pairs={{0,4},{4,0},{8,12},{12,8},{16,20},{20,16},{24,28},{28,24},{1,5},{5... | collective-permute-start | bytes 417800 | tf_op jit(solution)/shard_map/ppermute | solution.py:309
  36.5 3.4 %shard_map.57 = (f32[2,1,1024]{2,1,0:T(1,128)S(1)}, f32[2,1,1024]{2,1,0:T(1,128)S(1)}, f32[2,128,1024]{2,1,0:T(8,128)S(1)}) custom-call(s32[2]{0:T(128)S(1)} %copy-done.8, bf16[256,2048]{1,0:T(8,128)(2,1)S(1)} %copy-done.2, bf16[272,512]{1,0:T(8,128)(2,1)} %collective-permute-done.6.refs_2_, bf16[272,512]{1,0:T(8,128)(2,1)S(1)} %collective-permute-done.2.refs_3_, ...), custom_call_target="tpu_custom_call" | custom-call | flops 805306368 | bytes 6291456 | tf_op jit(solution)/shard_map/pallas_call | solution.py:244
  39.9 3.4 %shard_map.61 = (f32[2,1,1024]{2,1,0:T(1,128)S(1)}, f32[2,1,1024]{2,1,0:T(1,128)S(1)}, f32[2,128,1024]{2,1,0:T(8,128)S(1)}) custom-call(s32[2]{0:T(128)S(1)} %copy-done.8, bf16[256,2048]{1,0:T(8,128)(2,1)S(1)} %copy-done.2, bf16[272,512]{1,0:T(8,128)(2,1)} %collective-permute-done.6.refs_2_, bf16[272,512]{1,0:T(8,128)(2,1)S(1)} %collective-permute-done.2.refs_3_, ...), custom_call_target="tpu_custom_call" | custom-call | flops 805306368 | bytes 6291456 | tf_op jit(solution)/shard_map/pallas_call | solution.py:244
  43.3 3.0 %shard_map.58 = (f32[2,1,1024]{2,1,0:T(1,128)S(1)}, f32[2,1,1024]{2,1,0:T(1,128)S(1)}, f32[2,128,1024]{2,1,0:T(8,128)S(1)}) custom-call(s32[2]{0:T(128)S(1)} %copy-done.8, bf16[256,2048]{1,0:T(8,128)(2,1)S(1)} %copy-done.2, bf16[272,512]{1,0:T(8,128)(2,1)S(1)} %collective-permute-done.3.refs_2_, bf16[272,512]{1,0:T(8,128)(2,1)S(1)} %collective-permute-done.5.refs_3_, ...), custom_call_target="tpu_custom_call" | custom-call | flops 805306368 | bytes 6291456 | tf_op jit(solution)/shard_map/pallas_call | solution.py:244
  46.4 1.8 %shard_map.59.refs_8_.refs_0_ = bf16[256,1024]{1,0:T(8,128)(2,1)S(1)} custom-call(s32[2]{0:T(128)S(1)} %copy-done.8, bf16[256,2048]{1,0:T(8,128)(2,1)S(1)} %copy-done.2, bf16[272,256]{1,0:T(8,128)(2,1)S(1)} %collective-permute-done.1.refs_2_, f32[2,1,1024]{2,1,0:T(1,128)S(1)} %get-tuple-element.41.refs_3_, f32[2,1,1024]{2,1,0:T(1,128)S(1)} %get-tuple-element.42.refs_4_, ...), custom_call_target="tpu_custom_call" | custom-call | flops 268435456 | bytes 2097152 | tf_op jit(solution)/shard_map/pallas_call | solution.py:244
  48.1 3.2 %shard_map.62 = (f32[2,1,1024]{2,1,0:T(1,128)S(1)}, f32[2,1,1024]{2,1,0:T(1,128)S(1)}, f32[2,128,1024]{2,1,0:T(8,128)S(1)}) custom-call(s32[2]{0:T(128)S(1)} %copy-done.8, bf16[256,2048]{1,0:T(8,128)(2,1)S(1)} %copy-done.2, bf16[272,512]{1,0:T(8,128)(2,1)S(1)} %collective-permute-done.3.refs_2_, bf16[272,512]{1,0:T(8,128)(2,1)S(1)} %collective-permute-done.5.refs_3_, ...), custom_call_target="tpu_custom_call" | custom-call | flops 805306368 | bytes 6291456 | tf_op jit(solution)/shard_map/pallas_call | solution.py:244
  51.3 4.2 %shard_map.63 = (bf16[256,1024]{1,0:T(8,128)(2,1)S(1)}, bf16[256,256]{1,0:T(8,128)(2,1)S(1)}, f32[256,256]{1,0:T(8,128)S(1)}) custom-call(s32[2]{0:T(128)S(1)} %copy-done.9, bf16[256,2048]{1,0:T(8,128)(2,1)S(1)} %copy-done.3, bf16[272,256]{1,0:T(8,128)(2,1)S(1)} %collective-permute-done.8.refs_2_, f32[2,1,1024]{2,1,0:T(1,128)S(1)} %get-tuple-element.51.refs_3_, ...), custom_call_target="tpu_custom_call" | custom-call | flops 805306368 | bytes 2097152 | tf_op jit(solution)/shard_map/pallas_call | solution.py:244
  55.6 6.0 %shard_map.64 = (bf16[256,768]{1,0:T(8,128)(2,1)S(1)}, f32[256,768]{1,0:T(8,128)S(1)}) custom-call(s32[2]{0:T(128)S(1)} %get-tuple-element.61.at_ref, bf16[2048,4096]{1,0:T(8,128)(2,1)} %weight_ref.3, bf16[256,1024]{1,0:T(8,128)(2,1)S(1)} %shard_map.59.refs_8_.refs_0_, bf16[256,1024]{1,0:T(8,128)(2,1)S(1)} %get-tuple-element.54.refs_1_, ...), custom_call_target="tpu_custom_call" | custom-call | flops 1610612736 | bytes 6291456 | tf_op jit(solution)/shard_map/pallas_call | solution.py:269
  62.2 1.3 %collective-permute-done.9 = bf16[256,256]{1,0:T(8,128)(2,1)S(1)} collective-permute-done((bf16[256,256]{1,0:T(8,128)(2,1)S(1)}, bf16[256,256]{1,0:T(8,128)(2,1)S(1)}, u32[]{:S(2)}, u32[]{:S(2)}) %collective-permute-start.9) | collective-permute-done | bytes 131104 | tf_op jit(solution)/shard_map/ppermute | solution.py:344
  63.6 7.4 %shard_map.65 = (bf16[256,1024]{1,0:T(8,128)(2,1)S(1)}, f32[256,1024]{1,0:T(8,128)S(1)}) custom-call(s32[2]{0:T(128)S(1)} %add_multiply_fusion.at_ref, bf16[2048,4096]{1,0:T(8,128)(2,1)} %weight_ref.3, bf16[256,1024]{1,0:T(8,128)(2,1)S(1)} %shard_map.59.refs_8_.refs_0_, bf16[256,1024]{1,0:T(8,128)(2,1)S(1)} %get-tuple-element.54.refs_1_, ...), custom_call_target="tpu_custom_call" | custom-call | flops 2147483648 | bytes 8388608 | tf_op jit(solution)/shard_map/pallas_call | solution.py:269
  71.2 1.5 %collective-permute-start.13 = (bf16[256,768]{1,0:T(8,128)(2,1)S(1)}, bf16[256,768]{1,0:T(8,128)(2,1)S(1)}, u32[]{:S(2)}, u32[]{:S(2)}) collective-permute-start(bf16[256,768]{1,0:T(8,128)(2,1)S(1)} %add_convert_fusion.refs_4_), channel_id=1, source_target_pairs={{0,2},{1,3},{2,0},{3,1},{4,6},{5,7},{6,4},{7,5},{8,10},{9,11},{10,... | collective-permute-start | bytes 1179656 | tf_op jit(solution)/shard_map/ppermute | solution.py:348
  73.4 9.8 %collective-permute-done.13 = bf16[256,768]{1,0:T(8,128)(2,1)S(1)} collective-permute-done((bf16[256,768]{1,0:T(8,128)(2,1)S(1)}, bf16[256,768]{1,0:T(8,128)(2,1)S(1)}, u32[]{:S(2)}, u32[]{:S(2)}) %collective-permute-start.13) | collective-permute-done | bytes 393248 | tf_op jit(solution)/shard_map/ppermute | solution.py:348
  83.3 2.1 %collective-permute-done.12 = bf16[256,256]{1,0:T(8,128)(2,1)S(1)} collective-permute-done((bf16[256,256]{1,0:T(8,128)(2,1)S(1)}, bf16[256,256]{1,0:T(8,128)(2,1)S(1)}, u32[]{:S(2)}, u32[]{:S(2)}) %collective-permute-start.12) | collective-permute-done | bytes 131104 | tf_op jit(solution)/shard_map/ppermute | solution.py:348
  (43 shorter events, 13.6 us)
Async XLA Ops:
  0.0 51.3 %copy-start.3 = (bf16[256,2048]{1,0:T(8,128)(2,1)S(1)}, bf16[256,2048]{1,0:T(8,128)(2,1)}, u32[]{:S(2)}) copy-start(bf16[256,2048]{1,0:T(8,128)(2,1)} %refs_1_.15) | copy-start | bytes 3145732
  0.0 1.1 %copy-start.4 = (bf16[256,1024]{1,0:T(8,128)(2,1)S(1)}, bf16[256,1024]{1,0:T(8,128)(2,1)}, u32[]{:S(2)}) copy-start(bf16[256,1024]{1,0:T(8,128)(2,1)} %keys_ref.1) | copy-start | bytes 1572868
  1.1 1.0 %copy-start.5 = (bf16[256,1024]{1,0:T(8,128)(2,1)S(1)}, bf16[256,1024]{1,0:T(8,128)(2,1)}, u32[]{:S(2)}) copy-start(bf16[256,1024]{1,0:T(8,128)(2,1)} %values_ref.1) | copy-start | bytes 1572868
  2.2 0.7 copy-start.6
  2.8 48.5 %copy-start.9 = (s32[2]{0:T(128)S(1)}, s32[2]{0:T(128)}, u32[]{:S(2)}) copy-start(s32[2]{0:T(128)} %refs_0_.15) | copy-start | bytes 28
  4.1 13.3 %collective-permute-start.2 = (bf16[272,512]{1,0:T(8,128)(2,1)S(1)}, bf16[272,512]{1,0:T(8,128)(2,1)S(1)}, u32[]{:S(2)}, u32[]{:S(2)}) collective-permute-start(bf16[272,512]{1,0:T(8,128)(2,1)S(1)} %get-tuple-element.34.refs_2_), channel_id=1, source_target_pairs={{0,8},{4,12},{8,16},{12,20},{16,24},{20,28},{24,0},{28,4},{1,9},{5... | collective-permute-start | bytes 835592 | tf_op jit(solution)/shard_map/ppermute | solution.py:299
  7.2 14.1 %collective-permute-start.4 = (bf16[272,512]{1,0:T(8,128)(2,1)S(1)}, bf16[272,512]{1,0:T(8,128)(2,1)S(1)}, u32[]{:S(2)}, u32[]{:S(2)}) collective-permute-start(bf16[272,512]{1,0:T(8,128)(2,1)S(1)} %get-tuple-element.34.refs_2_), channel_id=1, source_target_pairs={{0,24},{4,28},{8,0},{12,4},{16,8},{20,12},{24,16},{28,20},{1,25},{... | collective-permute-start | bytes 835592 | tf_op jit(solution)/shard_map/ppermute | solution.py:299
  9.2 26.1 %collective-permute-start.6 = (bf16[272,512]{1,0:T(8,128)(2,1)S(1)}, bf16[272,512]{1,0:T(8,128)(2,1)}, u32[]{:S(2)}, u32[]{:S(2)}) collective-permute-start(bf16[272,512]{1,0:T(8,128)(2,1)S(1)} %get-tuple-element.34.refs_2_), channel_id=1, source_target_pairs={{0,4},{4,0},{8,12},{12,8},{16,20},{20,16},{24,28},{28,24},{1,5},{5... | collective-permute-start | bytes 835592 | tf_op jit(solution)/shard_map/ppermute | solution.py:309
  10.9 20.0 %collective-permute-start = (bf16[272,256]{1,0:T(8,128)(2,1)}, bf16[272,256]{1,0:T(8,128)(2,1)S(1)}, u32[]{:S(2)}, u32[]{:S(2)}) collective-permute-start(bf16[272,256]{1,0:T(8,128)(2,1)} %get-tuple-element.33), channel_id=1, source_target_pairs={{0,16},{4,20},{8,24},{12,28},{16,0},{20,4},{24,8},{28,12},{1,17},{... | collective-permute-start | bytes 417800 | tf_op jit(solution)/shard_map/ppermute | solution.py:299
  11.7 22.1 %collective-permute-start.7 = (bf16[272,256]{1,0:T(8,128)(2,1)S(1)}, bf16[272,256]{1,0:T(8,128)(2,1)S(1)}, u32[]{:S(2)}, u32[]{:S(2)}) collective-permute-start(bf16[272,256]{1,0:T(8,128)(2,1)S(1)} %get-tuple-element.44), channel_id=1, source_target_pairs={{0,16},{4,20},{8,24},{12,28},{16,0},{20,4},{24,8},{28,12},{1,17},{... | collective-permute-start | bytes 417800 | tf_op jit(solution)/shard_map/ppermute | solution.py:299
  13.8 1.2 %copy-start = (bf16[256,2048]{1,0:T(8,128)(2,1)S(1)}, bf16[256,2048]{1,0:T(8,128)(2,1)}, u32[]{:S(2)}) copy-start(bf16[256,2048]{1,0:T(8,128)(2,1)} %refs_1_.15) | copy-start | bytes 3145732
  15.1 0.7 copy-start.7
  17.5 25.8 %collective-permute-start.3 = (bf16[272,512]{1,0:T(8,128)(2,1)S(1)}, bf16[272,512]{1,0:T(8,128)(2,1)S(1)}, u32[]{:S(2)}, u32[]{:S(2)}) collective-permute-start(bf16[272,512]{1,0:T(8,128)(2,1)S(1)} %collective-permute-done.2.refs_3_), channel_id=1, source_target_pairs={{0,4},{4,0},{8,12},{12,8},{16,20},{20,16},{24,28},{28,24},{1,5},{5... | collective-permute-start | bytes 835592 | tf_op jit(solution)/shard_map/ppermute | solution.py:309
  21.2 22.1 %collective-permute-start.5 = (bf16[272,512]{1,0:T(8,128)(2,1)S(1)}, bf16[272,512]{1,0:T(8,128)(2,1)S(1)}, u32[]{:S(2)}, u32[]{:S(2)}) collective-permute-start(bf16[272,512]{1,0:T(8,128)(2,1)S(1)} %collective-permute-done.4.refs_4_), channel_id=1, source_target_pairs={{0,4},{4,0},{8,12},{12,8},{16,20},{20,16},{24,28},{28,24},{1,5},{5... | collective-permute-start | bytes 835592 | tf_op jit(solution)/shard_map/ppermute | solution.py:309
  22.7 1.2 %copy-start.1 = (bf16[256,2048]{1,0:T(8,128)(2,1)S(1)}, bf16[256,2048]{1,0:T(8,128)(2,1)}, u32[]{:S(2)}) copy-start(bf16[256,2048]{1,0:T(8,128)(2,1)} %refs_1_.15) | copy-start | bytes 3145732
  24.0 0.7 copy-start.8
  30.9 15.5 %collective-permute-start.1 = (bf16[272,256]{1,0:T(8,128)(2,1)S(1)}, bf16[272,256]{1,0:T(8,128)(2,1)S(1)}, u32[]{:S(2)}, u32[]{:S(2)}) collective-permute-start(bf16[272,256]{1,0:T(8,128)(2,1)S(1)} %collective-permute-done.refs_4_), channel_id=1, source_target_pairs={{0,4},{4,0},{8,12},{12,8},{16,20},{20,16},{24,28},{28,24},{1,5},{5... | collective-permute-start | bytes 417800 | tf_op jit(solution)/shard_map/ppermute | solution.py:309
  33.7 17.6 %collective-permute-start.8 = (bf16[272,256]{1,0:T(8,128)(2,1)S(1)}, bf16[272,256]{1,0:T(8,128)(2,1)S(1)}, u32[]{:S(2)}, u32[]{:S(2)}) collective-permute-start(bf16[272,256]{1,0:T(8,128)(2,1)S(1)} %collective-permute-done.7.refs_4_), channel_id=1, source_target_pairs={{0,4},{4,0},{8,12},{12,8},{16,20},{20,16},{24,28},{28,24},{1,5},{5... | collective-permute-start | bytes 417800 | tf_op jit(solution)/shard_map/ppermute | solution.py:309
  35.2 1.2 %copy-start.2 = (bf16[256,2048]{1,0:T(8,128)(2,1)S(1)}, bf16[256,2048]{1,0:T(8,128)(2,1)}, u32[]{:S(2)}) copy-start(bf16[256,2048]{1,0:T(8,128)(2,1)} %refs_1_.15) | copy-start | bytes 3145732
  61.5 2.0 %collective-permute-start.10 = (bf16[256,768]{1,0:T(8,128)(2,1)S(1)}, bf16[256,768]{1,0:T(8,128)(2,1)S(1)}, u32[]{:S(2)}, u32[]{:S(2)}) collective-permute-start(bf16[256,768]{1,0:T(8,128)(2,1)S(1)} %get-tuple-element.56.refs_2_), channel_id=1, source_target_pairs={{0,1},{1,0},{2,3},{3,2},{4,5},{5,4},{6,7},{7,6},{8,9},{9,8},{10,11... | collective-permute-start | bytes 1179656 | tf_op jit(solution)/shard_map/ppermute | solution.py:344
  61.6 1.9 %collective-permute-start.9 = (bf16[256,256]{1,0:T(8,128)(2,1)S(1)}, bf16[256,256]{1,0:T(8,128)(2,1)S(1)}, u32[]{:S(2)}, u32[]{:S(2)}) collective-permute-start(bf16[256,256]{1,0:T(8,128)(2,1)S(1)} %get-tuple-element.55.refs_2_), channel_id=1, source_target_pairs={{0,1},{1,0},{2,3},{3,2},{4,5},{5,4},{6,7},{7,6},{8,9},{9,8},{10,11... | collective-permute-start | bytes 393224 | tf_op jit(solution)/shard_map/ppermute | solution.py:344
  71.0 2.2 %collective-permute-start.11 = (bf16[256,1024]{1,0:T(8,128)(2,1)S(1)}, bf16[256,1024]{1,0:T(8,128)(2,1)S(1)}, u32[]{:S(2)}, u32[]{:S(2)}) collective-permute-start(bf16[256,1024]{1,0:T(8,128)(2,1)S(1)} %get-tuple-element.60), channel_id=1, source_target_pairs={{0,1},{1,0},{2,3},{3,2},{4,5},{5,4},{6,7},{7,6},{8,9},{9,8},{10,11... | collective-permute-start | bytes 1572872 | tf_op jit(solution)/shard_map/ppermute | solution.py:344
  71.2 12.0 %collective-permute-start.13 = (bf16[256,768]{1,0:T(8,128)(2,1)S(1)}, bf16[256,768]{1,0:T(8,128)(2,1)S(1)}, u32[]{:S(2)}, u32[]{:S(2)}) collective-permute-start(bf16[256,768]{1,0:T(8,128)(2,1)S(1)} %add_convert_fusion.refs_4_), channel_id=1, source_target_pairs={{0,2},{1,3},{2,0},{3,1},{4,6},{5,7},{6,4},{7,5},{8,10},{9,11},{10,... | collective-permute-start | bytes 1179656 | tf_op jit(solution)/shard_map/ppermute | solution.py:348
  72.7 12.7 %collective-permute-start.12 = (bf16[256,256]{1,0:T(8,128)(2,1)S(1)}, bf16[256,256]{1,0:T(8,128)(2,1)S(1)}, u32[]{:S(2)}, u32[]{:S(2)}) collective-permute-start(bf16[256,256]{1,0:T(8,128)(2,1)S(1)} %add_convert_fusion.1.refs_3_), channel_id=1, source_target_pairs={{0,2},{1,3},{2,0},{3,1},{4,6},{5,7},{6,4},{7,5},{8,10},{9,11},{10,... | collective-permute-start | bytes 393224 | tf_op jit(solution)/shard_map/ppermute | solution.py:348

commit v3 on v1

--- a/solution.py
+++ b/solution.py
@@ -15,11 +15,12 @@
 TAIL = 16
 DIGIT = 128
 NT = (((1,), (1,)), ((), ()))
+DEPTH = 3
 VMEM_LIMIT = 16 << 20
 WIDE_LIMIT = 48 << 20
 
 
-def fetch_columns(at_ref, weight_ref, buffer, sem, counts):
+def fetch_columns(at_ref, weight_ref, buffer, sem, counts, started=None):
     wide = buffer.shape[2]
     copies = []
     for run, count in enumerate(counts):
@@ -31,7 +32,8 @@
                     weight_ref.at[:, pl.ds(column, wide)], buffer.at[n], sem.at[n]
                 )
             )
-            copies[-1].start()
+    for copy in copies[:started]:
+        copy.start()
     return copies
 
 
@@ -40,17 +42,23 @@
     n = 0
     for out in outs:
         for tile in range(out.shape[1] // wide):
-            copies[n].wait()
+            if copies is not None:
+                copies[n].wait()
+                if n + DEPTH < len(copies):
+                    copies[n + DEPTH].start()
             out[:, tile * wide : (tile + 1) * wide] = jnp.dot(
                 rows_ref[...], buffer[n], preferred_element_type=jnp.float32
             ).astype(out.dtype)
             n += 1
 
 
-def attend_kernel(n_blocks, first, last, scale, kv_heads, span, *refs):
+def attend_kernel(halves, first, last, scale, kv_heads, span, *refs):
+    n_blocks = len(halves)
     order_ref, q_ref = refs[:2]
-    blocks = refs[2 : 2 + n_blocks]
-    refs = refs[2 + n_blocks :]
+    blocks, refs = [], refs[2:]
+    for count in halves:
+        blocks.append(refs[:count])
+        refs = refs[count:]
     if not first:
         old_top, old_total, old_acc = refs[:3]
         refs = refs[3:]
@@ -58,15 +66,22 @@
         at_ref, weight_ref = refs[:2]
         buffer, sem = refs[-2:]
         refs = refs[2:-2]
-        counts = [out.shape[1] // buffer.shape[2] for out in refs[1:3]]
+        products = refs[1:-7]
+        counts = [out.shape[1] // buffer.shape[2] for out in products]
         copies = fetch_columns(at_ref, weight_ref, buffer, sem, counts)
     outs = refs[:3]
-    bias_ref, flip_ref = refs[-6:-4]
+    merged_ref, bias_ref, flip_ref = refs[-7:-4]
     score_refs, weight_refs = refs[-4:-2], refs[-2:]
     parts = order_ref.shape[0]
     rows = q_ref.shape[0] // parts
     heads = q_ref.shape[1] // kv_heads // HEAD_SIZE
     pair = span // rows
+    for b, found in enumerate(blocks):
+        if len(found) == 2:
+            merged_ref[...] = found[0][...] + found[1][...]
+            blocks[b] = merged_ref
+        else:
+            blocks[b] = found[0]
     lengths = [block.shape[0] - TAIL for block in blocks]
     offsets = [sum(lengths[:b]) for b in range(n_blocks)]
 
@@ -146,19 +161,22 @@
         if 1 <= t <= len(pieces):
             weigh(t - 1)
     if last:
-        multiply_columns(outs[0], buffer, copies, outs[1:3])
-
-
-def product_shapes(tokens, columns):
-    return [
-        jax.ShapeDtypeStruct((tokens, columns), jnp.bfloat16),
-        jax.ShapeDtypeStruct((tokens, columns), jnp.float32),
-    ]
-
-
-def column_scratch(depth, columns):
-    wide = math.gcd(columns, 256)
-    tiles = 2 * columns // wide
+        for copy in copies:
+            copy.wait()
+        multiply_columns(outs[0], buffer, None, products)
+
+
+def product_shapes(tokens, widths):
+    found = []
+    for width in widths:
+        found.append(jax.ShapeDtypeStruct((tokens, width), jnp.bfloat16))
+        found.append(jax.ShapeDtypeStruct((tokens, width), jnp.float32))
+    return found
+
+
+def column_scratch(depth, widths):
+    wide = math.gcd(256, *widths)
+    tiles = 2 * sum(widths) // wide
     return [pltpu.VMEM((tiles, depth, wide), jnp.bfloat16), pltpu.SemaphoreType.DMA((tiles,))]
 
 
@@ -170,14 +188,17 @@
     span = math.gcd(heads, 2) * rows
     scale = math.log2(math.e) / math.sqrt(HEAD_SIZE)
     first, last = state is None, then is not None
-    seen = sum(block.shape[0] - TAIL for block in blocks)
+    seen = sum(block[0].shape[0] - TAIL for block in blocks)
     pairs = tokens * width // HEAD_SIZE * seen
     whole = pl.BlockSpec(memory_space=pltpu.VMEM)
     scalars = pl.BlockSpec(memory_space=pltpu.SMEM)
     combos = kv_heads * parts
-    operands = [order, queries, *blocks, *(() if first else state)]
+    halves = [len(block) for block in blocks]
+    arrays = [array for block in blocks for array in block]
+    operands = [order, queries, *arrays, *(() if first else state)]
     in_specs = [scalars] + [whole] * (len(operands) - 1)
     scratch = [
+        pltpu.VMEM(arrays[0].shape, arrays[0].dtype),
         pltpu.VMEM((parts, seen, rows), jnp.float32),
         pltpu.VMEM((kv_heads, HEAD_SIZE, seen), jnp.bfloat16),
     ]
@@ -185,13 +206,13 @@
     scratch += [pltpu.VMEM((seen, span), jnp.bfloat16)] * 2
     flops = 4 * pairs * HEAD_SIZE
     if last:
-        at, weight, columns = then
+        at, weight, widths = then
         operands += [at, weight]
         in_specs += [scalars, pl.BlockSpec(memory_space=pl.ANY)]
         out_shape = [jax.ShapeDtypeStruct(queries.shape, jnp.bfloat16)]
-        out_shape += product_shapes(tokens, columns)
-        scratch += column_scratch(width, columns)
-        flops += 4 * tokens * width * columns
+        out_shape += product_shapes(tokens, widths)
+        scratch += column_scratch(width, widths)
+        flops += 4 * tokens * width * sum(widths)
     else:
         out_shape = [
             jax.ShapeDtypeStruct((combos, 1, heads * rows), jnp.float32),
@@ -199,7 +220,7 @@
             jax.ShapeDtypeStruct((combos, HEAD_SIZE, heads * rows), jnp.float32),
         ]
     return pl.pallas_call(
-        functools.partial(attend_kernel, len(blocks), first, last, scale, kv_heads, span),
+        functools.partial(attend_kernel, halves, first, last, scale, kv_heads, span),
         in_specs=in_specs,
         out_specs=[whole] * len(out_shape),
         out_shape=out_shape,
@@ -214,7 +235,7 @@
 def project_kernel(at_ref, rows_ref, weight_ref, *refs):
     send_ref, keep_ref, buffer, sem = refs[-4:]
     counts = [out.shape[1] // buffer.shape[2] for out in (send_ref, keep_ref)]
-    copies = fetch_columns(at_ref, weight_ref, buffer, sem, counts)
+    copies = fetch_columns(at_ref, weight_ref, buffer, sem, counts, DEPTH)
     multiply_columns(rows_ref, buffer, copies, (send_ref, keep_ref))
 
 
@@ -226,8 +247,8 @@
         project_kernel,
         in_specs=[pl.BlockSpec(memory_space=pltpu.SMEM), whole, unread] + [unread] * len(after),
         out_specs=[whole] * 2,
-        out_shape=product_shapes(tokens, columns),
-        scratch_shapes=column_scratch(depth, columns),
+        out_shape=product_shapes(tokens, [columns]),
+        scratch_shapes=column_scratch(depth, [columns]),
         compiler_params=pltpu.CompilerParams(vmem_limit_bytes=WIDE_LIMIT),
         cost_estimate=pl.CostEstimate(
             flops=4 * tokens * depth * columns,
@@ -258,51 +279,60 @@
     inner = math.gcd(n_ctx, 2)
     outer = n_ctx // inner
 
-    def along_outer(block, k):
-        pairs = [
-            (o * inner + i, (o + k) % outer * inner + i) for o in range(outer) for i in range(inner)
-        ]
+    def move(block, target):
+        pairs = []
+        for o in range(outer):
+            for i in range(inner):
+                to = target(o, i)
+                if to is not None:
+                    pairs.append((o * inner + i, to[0] * inner + to[1]))
         return lax.ppermute(block, "ctx", pairs)
 
-    def along_inner(block):
+    def cross(block, among=None):
         found = []
         for k in range(1, inner):
-            pairs = [
-                (o * inner + i, o * inner + (i + k) % inner)
-                for o in range(outer)
-                for i in range(inner)
-            ]
-            found.append(lax.ppermute(block, "ctx", pairs))
+
+            def target(o, i):
+                return (o, (i + k) % inner) if among is None or o in among else None
+
+            found.append(move(block, target))
         return found
 
-    steps = []
-    for k in range(1, outer // 2 + 1):
-        steps.append([k] if 2 * k == outer else [k, outer - k])
-    columns = [[along_outer(own, k) for k in step] for step in steps]
-    arrived = along_inner(own)
-    before = []
-    for step, blocks in zip(steps, columns):
-        arrived += before + blocks
-        before = []
-        for k, block in zip(step, blocks):
-            before += along_inner(block)
-    arrived += before
-
-    stages = [[own]]
-    stages += [arrived[i : min(i + 3, len(arrived) - 1)] for i in range(0, len(arrived) - 1, 3)]
-    stages += [arrived[-1:]] if arrived else []
+    if outer == 4:
+        near = move(own, lambda o, i: (o ^ 1, i))
+        mirror = move(own, lambda o, i: (3 - o, i))
+        third = move(own, lambda o, i: {0: (2, i), 3: (1, i)}.get(o))
+        own_crossed = cross(own)
+        onward = move(mirror, lambda o, i: {2: (3, i), 1: (0, i)}.get(o))
+        stages = [[(own,)], [(near,), (mirror,)] + [(x,) for x in own_crossed]]
+        stages += [[(x,) for x in cross(near) + cross(mirror)]]
+        stages[-1].append((third, onward))
+        late = zip(cross(third, (1, 2)), cross(onward, (0, 3)))
+        stages += [[pair] for pair in late]
+    else:
+        blocks = [own]
+        for k in range(1, outer):
+            blocks.append(move(own, lambda o, i: ((o + k) % outer, i)))
+        arrived = blocks[1:]
+        for k, block in enumerate(blocks):
+            arrived += cross(block)
+        arrived = [(x,) for x in arrived]
+        stages = [[(own,)]]
+        stages += [arrived[i : min(i + 3, len(arrived) - 1)] for i in range(0, len(arrived) - 1, 3)]
+        stages += [arrived[-1:]] if arrived else []
+
     share = out_weight.shape[1] // n_tp
     cores = math.gcd(n_tp, 2)
     groups = n_tp // cores
     core, group = tp % cores, tp // cores
-    cuts = 2 if groups == 2 else 1
-    width = share // cuts
-    jobs = [(cut, r) for cut in range(cuts) for r in range(1, groups)]
-
-    def begins(cut, r):
+    cuts = [0, share // 4, share] if groups == 2 else [0, share]
+    widths = [b - a for a, b in zip(cuts, cuts[1:])]
+    jobs = [(cut, r) for r in range(1, groups) for cut in range(len(widths))]
+
+    def begins(r, numbers):
         to = (group + r) % groups * cores
-        at = jnp.stack([to + (core + 1) % cores, to + core]) * share + cut * width
-        return at.astype(jnp.int32)
+        firsts = jnp.stack([to + (core + 1) % cores, to + core]) * share
+        return jnp.concatenate([firsts + cuts[n] for n in numbers]).astype(jnp.int32)
 
     def to_core(x):
         pairs = [(t, t // cores * cores + (t + 1) % cores) for t in range(n_tp)]
@@ -315,36 +345,43 @@
     state = None
     for blocks in stages[:-1]:
         state = attend(block_order, queries, blocks, state, kv_heads)
-    first = jobs[0] if jobs else (0, 0)
-    attended, send, keep = attend(
+    together = list(range(len(widths)))
+    attended, *products = attend(
         block_order,
         queries,
         stages[-1],
         state,
         kv_heads,
-        (begins(*first), out_weight, width),
+        (begins(min(1, groups - 1), together), out_weight, widths),
     )
-
-    partial = []
+    for r in range(2, groups):
+        for cut in together:
+            products += project(
+                begins(r, [cut]), attended, out_weight, widths[cut], products[-2:-1]
+            )
+
+    arriving = [[] for _ in widths]
+    after = ()
+    others = [to_core(products[2 * n]) for n in range(len(jobs))] if cores > 1 else None
     for name, (cut, r) in enumerate(jobs):
-        if name > 0:
-            send, keep = project(begins(cut, r), attended, out_weight, width, (send,))
-        partial.append((to_core(send) if cores > 1 else None, keep))
-    arriving = [[] for _ in range(cuts)]
-    after = (send,)
-    for (cut, r), (other, keep) in zip(jobs, partial):
-        if other is not None:
-            keep = keep + other.astype(jnp.float32)
-        summed = keep.astype(jnp.bfloat16)
-        after += (summed,)
-        arriving[cut].append(to_group(summed, r))
-    send, mine = project(begins(0, 0), attended, out_weight, share, after)
-    if cores > 1:
-        mine = mine + to_core(send).astype(jnp.float32)
+        total = products[2 * name + 1]
+        if cores > 1:
+            total = total + others[name].astype(jnp.float32)
+        total = total.astype(jnp.bfloat16)
+        after += (total,)
+        arriving[cut].append(to_group(total, r))
+    if jobs:
+        send, mine = project(begins(0, [0]), attended, out_weight, share, after)
+        if cores > 1:
+            mine = mine + to_core(send).astype(jnp.float32)
+    else:
+        mine = products[1]
+        if cores > 1:
+            mine = mine + to_core(products[0]).astype(jnp.float32)
     result = []
-    for cut in range(cuts):
-        total = mine[:, cut * width : (cut + 1) * width]
-        for x in arriving[cut]:
+    for cut, found in enumerate(arriving):
+        total = mine[:, cuts[cut] : cuts[cut + 1]]
+        for x in found:
             total = total + x.astype(jnp.float32)
         result.append(total.astype(jnp.bfloat16))
     return jnp.concatenate(result, axis=1)

time: 81.4 us -> 80.7 us (level)
  the two profiles are of different devices: /device:TPU:0 before, /device:TPU:10 now
where the time goes in v3:
time: 80.7 us; the launch traced here: 80.4 us
  Pallas kernels  30 us (37%)
  waiting for transfers between devices  27.3 us (34%)
  starting transfers between devices  16.4 us (20%)
  local copies, waits for them, and re-layouts  4.36 us (5%)
  other arithmetic  2.26 us (3%)
    pallas_call x4, Pallas kernels, attend(): pl.pallas_call(functools.partial(attend_kernel, halves, first, last, scal...  22.6 us
    ppermute x9, waiting for transfers between devices, move(): return lax.ppermute(block, 'ctx', pairs)  13.9 us
    ppermute x9, starting transfers between devices, move(): return lax.ppermute(block, 'ctx', pairs)  13.6 us
    ppermute x2, waiting for transfers between devices, to_group(): return lax.ppermute(x, 'tp', pairs)  12 us
    pallas_call x1, Pallas kernels, project(): pl.pallas_call(project_kernel, in_specs=[pl.BlockSpec(memory_space=pltpu....  7.37 us
    unnamed x10, local copies, waits for them, and re-layouts  3.21 us
    ppermute x2, starting transfers between devices, to_group(): return lax.ppermute(x, 'tp', pairs)  2.03 us
  transfers between devices with their start and end apart: 14, of which 5 were waited for; matrix products, arithmetic and copies ran while one was open for 1% of the time, Pallas kernels for 16%

profile of v3, /device:TPU:10, one launch (start us, length us, event | category | flops | bytes accessed | tf_op | source)
XLA Modules:
  0.0 80.4 jit_solution(11275653740814571762)
XLA Ops:
  0.0 0.7 convert_bitcast_fusion
  0.9 1.0 %constant_dynamic-slice_fusion = (bf16[256,128]{1,0:T(8,128)(2,1)S(1)}, bf16[256,128]{1,0:T(8,128)(2,1)S(1)}, bf16[256,128]{1,0:T(8,128)(2,1)S(1)}, bf16[256,128]{1,0:T(8,128)(2,1)S(1)}) fusion(bf16[256,1024]{1,0:T(8,128)(2,1)} %param.7, s32[]{:T(128)S(6)} %select_n.48, s32[]{:T(128)S(6)} %add.87, bf16[256,1024]{1,0:T(8,128)(2,1)} %param.6), kind=kLoop, calls=%fused_computation.16 | loop fusion | bytes 524296 | tf_op jit(solution)/shard_map/slice | solution.py:272
  2.0 1.6 %collective-permute-start.2 = (bf16[272,512]{1,0:T(8,128)(2,1)S(1)}, bf16[272,512]{1,0:T(8,128)(2,1)S(1)}, u32[]{:S(2)}, u32[]{:S(2)}) collective-permute-start(bf16[272,512]{1,0:T(8,128)(2,1)S(1)} %maximum_maximum_fusion.refs_2_), channel_id=1, source_target_pairs={{0,24},{4,28},{8,16},{12,20},{16,8},{20,12},{24,0},{28,4},{1,25},{... | collective-permute-start | bytes 835592 | tf_op jit(solution)/shard_map/ppermute | solution.py:289
  3.6 2.5 %collective-permute-start.5 = (bf16[272,512]{1,0:T(8,128)(2,1)S(1)}, bf16[272,512]{1,0:T(8,128)(2,1)S(1)}, u32[]{:S(2)}, u32[]{:S(2)}) collective-permute-start(bf16[272,512]{1,0:T(8,128)(2,1)S(1)} %maximum_maximum_fusion.refs_2_), channel_id=1, source_target_pairs={{0,8},{4,12},{8,0},{12,4},{16,24},{20,28},{24,16},{28,20},{1,9},{5... | collective-permute-start | bytes 835592 | tf_op jit(solution)/shard_map/ppermute | solution.py:289
  6.1 1.3 %collective-permute-start = (bf16[272,512]{1,0:T(8,128)(2,1)S(1)}, bf16[272,512]{1,0:T(8,128)(2,1)S(1)}, u32[]{:S(2)}, u32[]{:S(2)}) collective-permute-start(bf16[272,512]{1,0:T(8,128)(2,1)S(1)} %maximum_maximum_fusion.refs_2_), channel_id=1, source_target_pairs={{0,16},{4,20},{24,8},{28,12},{1,17},{5,21},{25,9},{29,13},{2,18},{... | collective-permute-start | bytes 835592 | tf_op jit(solution)/shard_map/ppermute | solution.py:289
  7.4 9.1 %collective-permute-done.2.refs_3_ = bf16[272,512]{1,0:T(8,128)(2,1)S(1)} collective-permute-done((bf16[272,512]{1,0:T(8,128)(2,1)S(1)}, bf16[272,512]{1,0:T(8,128)(2,1)S(1)}, u32[]{:S(2)}, u32[]{:S(2)}) %collective-permute-start.2) | collective-permute-done | bytes 278560 | tf_op jit(solution)/shard_map/ppermute | solution.py:289
  16.5 1.3 %collective-permute-start.3 = (bf16[272,512]{1,0:T(8,128)(2,1)S(1)}, bf16[272,512]{1,0:T(8,128)(2,1)S(1)}, u32[]{:S(2)}, u32[]{:S(2)}) collective-permute-start(bf16[272,512]{1,0:T(8,128)(2,1)S(1)} %collective-permute-done.2.refs_3_), channel_id=1, source_target_pairs={{8,0},{12,4},{16,24},{20,28},{9,1},{13,5},{17,25},{21,29},{10,2},{... | collective-permute-start | bytes 835592 | tf_op jit(solution)/shard_map/ppermute | solution.py:289
  18.4 1.6 %collective-permute-start.7 = (bf16[272,512]{1,0:T(8,128)(2,1)S(1)}, bf16[272,512]{1,0:T(8,128)(2,1)S(1)}, u32[]{:S(2)}, u32[]{:S(2)}) collective-permute-start(bf16[272,512]{1,0:T(8,128)(2,1)S(1)} %collective-permute-done.2.refs_3_), channel_id=1, source_target_pairs={{0,4},{4,0},{8,12},{12,8},{16,20},{20,16},{24,28},{28,24},{1,5},{5... | collective-permute-start | bytes 835592 | tf_op jit(solution)/shard_map/ppermute | solution.py:289
  20.4 1.2 %copy-done.1 = bf16[256,2048]{1,0:T(8,128)(2,1)S(1)} copy-done((bf16[256,2048]{1,0:T(8,128)(2,1)S(1)}, bf16[256,2048]{1,0:T(8,128)(2,1)}, u32[]{:S(2)}) %copy-start.1) | copy-done | bytes 1048600
  21.6 0.7 copy-done.3
  22.3 2.6 %shard_map.55 = (f32[4,1,1024]{2,1,0:T(1,128)S(1)}, f32[4,1,1024]{2,1,0:T(1,128)S(1)}, f32[4,128,1024]{2,1,0:T(8,128)S(1)}) custom-call(s32[2]{0:T(128)S(1)} %copy-done.3, bf16[256,2048]{1,0:T(8,128)(2,1)S(1)} %copy-done.1, bf16[272,512]{1,0:T(8,128)(2,1)S(1)} %maximum_maximum_fusion.refs_2_), custom_call_target="tpu_custom_call" | custom-call | flops 536870912 | bytes 4194304 | tf_op jit(solution)/shard_map/pallas_call | solution.py:222
  25.0 3.5 %collective-permute-start.1 = (bf16[272,512]{1,0:T(8,128)(2,1)S(1)}, bf16[272,512]{1,0:T(8,128)(2,1)S(1)}, u32[]{:S(2)}, u32[]{:S(2)}) collective-permute-start(bf16[272,512]{1,0:T(8,128)(2,1)S(1)} %collective-permute-done.refs_4_), channel_id=1, source_target_pairs={{8,12},{12,8},{16,20},{20,16},{9,13},{13,9},{17,21},{21,17},{10,14... | collective-permute-start | bytes 835592 | tf_op jit(solution)/shard_map/ppermute | solution.py:289
  28.5 0.9 %collective-permute-start.4 = (bf16[272,512]{1,0:T(8,128)(2,1)S(1)}, bf16[272,512]{1,0:T(8,128)(2,1)S(1)}, u32[]{:S(2)}, u32[]{:S(2)}) collective-permute-start(bf16[272,512]{1,0:T(8,128)(2,1)S(1)} %collective-permute-done.3.refs_5_), channel_id=1, source_target_pairs={{0,4},{4,0},{24,28},{28,24},{1,5},{5,1},{25,29},{29,25},{2,6},{6,2... | collective-permute-start | bytes 835592 | tf_op jit(solution)/shard_map/ppermute | solution.py:289
  29.4 5.1 %shard_map.56 = (f32[4,1,1024]{2,1,0:T(1,128)S(1)}, f32[4,1,1024]{2,1,0:T(1,128)S(1)}, f32[4,128,1024]{2,1,0:T(8,128)S(1)}) custom-call(s32[2]{0:T(128)S(1)} %copy-done.3, bf16[256,2048]{1,0:T(8,128)(2,1)S(1)} %copy-done.1, bf16[272,512]{1,0:T(8,128)(2,1)S(1)} %collective-permute-done.5.refs_2_, bf16[272,512]{1,0:T(8,128)(2,1)S(1)} %collective-permute-done.2.refs_3_, ...), custom_call_target="tpu_custom_call" | custom-call | flops 1610612736 | bytes 12582912 | tf_op jit(solution)/shard_map/pallas_call | solution.py:222
  34.5 4.8 %collective-permute-done.6.refs_2_ = bf16[272,512]{1,0:T(8,128)(2,1)S(1)} collective-permute-done((bf16[272,512]{1,0:T(8,128)(2,1)S(1)}, bf16[272,512]{1,0:T(8,128)(2,1)S(1)}, u32[]{:S(2)}, u32[]{:S(2)}) %collective-permute-start.6) | collective-permute-done | bytes 278560 | tf_op jit(solution)/shard_map/ppermute | solution.py:289
  39.3 5.3 %shard_map.57 = (f32[4,1,1024]{2,1,0:T(1,128)S(1)}, f32[4,1,1024]{2,1,0:T(1,128)S(1)}, f32[4,128,1024]{2,1,0:T(8,128)S(1)}) custom-call(s32[2]{0:T(128)S(1)} %copy-done.3, bf16[256,2048]{1,0:T(8,128)(2,1)S(1)} %copy-done.1, bf16[272,512]{1,0:T(8,128)(2,1)S(1)} %collective-permute-done.6.refs_2_, bf16[272,512]{1,0:T(8,128)(2,1)S(1)} %collective-permute-done.7.refs_3_, ...), custom_call_target="tpu_custom_call" | custom-call | flops 1610612736 | bytes 12582912 | tf_op jit(solution)/shard_map/pallas_call | solution.py:222
  44.7 1.3 %copy-done = f32[4,128,1024]{2,1,0:T(8,128)} copy-done((f32[4,128,1024]{2,1,0:T(8,128)}, f32[4,128,1024]{2,1,0:T(8,128)S(1)}, u32[]{:S(2)}) %copy-start) | copy-done | bytes 2097176
  46.0 9.6 %shard_map.58 = (bf16[256,2048]{1,0:T(8,128)(2,1)S(1)}, bf16[256,256]{1,0:T(8,128)(2,1)S(1)}, f32[256,256]{1,0:T(8,128)S(1)}, bf16[256,768]{1,0:T(8,128)(2,1)S(1)}, f32[256,768]{1,0:T(8,128)S(1)}) custom-call(s32[2]{0:T(128)S(1)} %copy-done.4, bf16[256,2048]{1,0:T(8,128)(2,1)S(1)} %copy-done.2, bf16[272,512]{1,0:T(8,128)(2,1)S(1)} %collective-permute-done.1.refs_2_, ...), custom_call_target="tpu_custom_call" | custom-call | flops 2684354560 | bytes 4194304 | tf_op jit(solution)/shard_map/pallas_call | solution.py:222
  56.2 1.3 %collective-permute-done.9 = bf16[256,256]{1,0:T(8,128)(2,1)S(1)} collective-permute-done((bf16[256,256]{1,0:T(8,128)(2,1)S(1)}, bf16[256,256]{1,0:T(8,128)(2,1)S(1)}, u32[]{:S(2)}, u32[]{:S(2)}) %collective-permute-start.9) | collective-permute-done | bytes 131104 | tf_op jit(solution)/shard_map/ppermute | solution.py:339
  57.7 7.4 %shard_map.59 = (bf16[256,1024]{1,0:T(8,128)(2,1)S(1)}, f32[256,1024]{1,0:T(8,128)S(1)}) custom-call(s32[2]{0:T(128)S(1)} %add_multiply_fusion.at_ref, bf16[256,2048]{1,0:T(8,128)(2,1)S(1)} %get-tuple-element.30.rows_ref, bf16[2048,4096]{1,0:T(8,128)(2,1)} %weight_ref.1, bf16[256,256]{1,0:T(8,128)(2,1)S(1)} %add_convert_fusion.1.refs_0_, ...), custom_call_target="tpu_custom_call" | custom-call | flops 2147483648 | bytes 8388608 | tf_op jit(solution)/shard_map/pallas_call | solution.py:246
  65.3 1.5 %collective-permute-start.12 = (bf16[256,256]{1,0:T(8,128)(2,1)S(1)}, bf16[256,256]{1,0:T(8,128)(2,1)S(1)}, u32[]{:S(2)}, u32[]{:S(2)}) collective-permute-start(bf16[256,256]{1,0:T(8,128)(2,1)S(1)} %add_convert_fusion.1.refs_0_), channel_id=1, source_target_pairs={{0,2},{1,3},{2,0},{3,1},{4,6},{5,7},{6,4},{7,5},{8,10},{9,11},{10,... | collective-permute-start | bytes 393224 | tf_op jit(solution)/shard_map/ppermute | solution.py:343
  67.4 4.2 %collective-permute-done.12 = bf16[256,256]{1,0:T(8,128)(2,1)S(1)} collective-permute-done((bf16[256,256]{1,0:T(8,128)(2,1)S(1)}, bf16[256,256]{1,0:T(8,128)(2,1)S(1)}, u32[]{:S(2)}, u32[]{:S(2)}) %collective-permute-start.12) | collective-permute-done | bytes 131104 | tf_op jit(solution)/shard_map/ppermute | solution.py:343
  71.7 7.8 %collective-permute-done.13 = bf16[256,768]{1,0:T(8,128)(2,1)S(1)} collective-permute-done((bf16[256,768]{1,0:T(8,128)(2,1)S(1)}, bf16[256,768]{1,0:T(8,128)(2,1)S(1)}, u32[]{:S(2)}, u32[]{:S(2)}) %collective-permute-start.13) | collective-permute-done | bytes 393248 | tf_op jit(solution)/shard_map/ppermute | solution.py:343
  79.5 0.9 %pad_maximum_fusion = bf16[256,1024]{1,0:T(8,128)(2,1)} fusion(bf16[256,768]{1,0:T(8,128)(2,1)S(1)} %fusion, bf16[256,256]{1,0:T(8,128)(2,1)S(1)} %fusion.1), kind=kLoop, calls=%fused_computation.4 | loop fusion | flops 1048576 | bytes 1048576 | tf_op jit(solution)/shard_map/concatenate | solution.py:387
  (35 shorter events, 3.2 us)
Async XLA Ops:
  2.0 14.5 %collective-permute-start.2 = (bf16[272,512]{1,0:T(8,128)(2,1)S(1)}, bf16[272,512]{1,0:T(8,128)(2,1)S(1)}, u32[]{:S(2)}, u32[]{:S(2)}) collective-permute-start(bf16[272,512]{1,0:T(8,128)(2,1)S(1)} %maximum_maximum_fusion.refs_2_), channel_id=1, source_target_pairs={{0,24},{4,28},{8,16},{12,20},{16,8},{20,12},{24,0},{28,4},{1,25},{... | collective-permute-start | bytes 835592 | tf_op jit(solution)/shard_map/ppermute | solution.py:289
  3.6 16.4 %collective-permute-start.5 = (bf16[272,512]{1,0:T(8,128)(2,1)S(1)}, bf16[272,512]{1,0:T(8,128)(2,1)S(1)}, u32[]{:S(2)}, u32[]{:S(2)}) collective-permute-start(bf16[272,512]{1,0:T(8,128)(2,1)S(1)} %maximum_maximum_fusion.refs_2_), channel_id=1, source_target_pairs={{0,8},{4,12},{8,0},{12,4},{16,24},{20,28},{24,16},{28,20},{1,9},{5... | collective-permute-start | bytes 835592 | tf_op jit(solution)/shard_map/ppermute | solution.py:289
  6.1 18.9 %collective-permute-start = (bf16[272,512]{1,0:T(8,128)(2,1)S(1)}, bf16[272,512]{1,0:T(8,128)(2,1)S(1)}, u32[]{:S(2)}, u32[]{:S(2)}) collective-permute-start(bf16[272,512]{1,0:T(8,128)(2,1)S(1)} %maximum_maximum_fusion.refs_2_), channel_id=1, source_target_pairs={{0,16},{4,20},{24,8},{28,12},{1,17},{5,21},{25,9},{29,13},{2,18},{... | collective-permute-start | bytes 835592 | tf_op jit(solution)/shard_map/ppermute | solution.py:289
  16.5 12.0 %collective-permute-start.3 = (bf16[272,512]{1,0:T(8,128)(2,1)S(1)}, bf16[272,512]{1,0:T(8,128)(2,1)S(1)}, u32[]{:S(2)}, u32[]{:S(2)}) collective-permute-start(bf16[272,512]{1,0:T(8,128)(2,1)S(1)} %collective-permute-done.2.refs_3_), channel_id=1, source_target_pairs={{8,0},{12,4},{16,24},{20,28},{9,1},{13,5},{17,25},{21,29},{10,2},{... | collective-permute-start | bytes 835592 | tf_op jit(solution)/shard_map/ppermute | solution.py:289
  17.8 11.6 %collective-permute-start.8 = (bf16[272,512]{1,0:T(8,128)(2,1)S(1)}, bf16[272,512]{1,0:T(8,128)(2,1)S(1)}, u32[]{:S(2)}, u32[]{:S(2)}) collective-permute-start(bf16[272,512]{1,0:T(8,128)(2,1)S(1)} %maximum_maximum_fusion.refs_2_), channel_id=1, source_target_pairs={{0,4},{4,0},{8,12},{12,8},{16,20},{20,16},{24,28},{28,24},{1,5},{5... | collective-permute-start | bytes 835592 | tf_op jit(solution)/shard_map/ppermute | solution.py:289
  18.4 20.9 %collective-permute-start.7 = (bf16[272,512]{1,0:T(8,128)(2,1)S(1)}, bf16[272,512]{1,0:T(8,128)(2,1)S(1)}, u32[]{:S(2)}, u32[]{:S(2)}) collective-permute-start(bf16[272,512]{1,0:T(8,128)(2,1)S(1)} %collective-permute-done.2.refs_3_), channel_id=1, source_target_pairs={{0,4},{4,0},{8,12},{12,8},{16,20},{20,16},{24,28},{28,24},{1,5},{5... | collective-permute-start | bytes 835592 | tf_op jit(solution)/shard_map/ppermute | solution.py:289
  20.0 19.4 %collective-permute-start.6 = (bf16[272,512]{1,0:T(8,128)(2,1)S(1)}, bf16[272,512]{1,0:T(8,128)(2,1)S(1)}, u32[]{:S(2)}, u32[]{:S(2)}) collective-permute-start(bf16[272,512]{1,0:T(8,128)(2,1)S(1)} %collective-permute-done.5.refs_2_), channel_id=1, source_target_pairs={{0,4},{4,0},{8,12},{12,8},{16,20},{20,16},{24,28},{28,24},{1,5},{5... | collective-permute-start | bytes 835592 | tf_op jit(solution)/shard_map/ppermute | solution.py:289
  20.4 1.2 %copy-start.1 = (bf16[256,2048]{1,0:T(8,128)(2,1)S(1)}, bf16[256,2048]{1,0:T(8,128)(2,1)}, u32[]{:S(2)}) copy-start(bf16[256,2048]{1,0:T(8,128)(2,1)} %refs_1_.7) | copy-start | bytes 3145732
  21.6 0.7 copy-start.3
  25.0 21.0 %collective-permute-start.1 = (bf16[272,512]{1,0:T(8,128)(2,1)S(1)}, bf16[272,512]{1,0:T(8,128)(2,1)S(1)}, u32[]{:S(2)}, u32[]{:S(2)}) collective-permute-start(bf16[272,512]{1,0:T(8,128)(2,1)S(1)} %collective-permute-done.refs_4_), channel_id=1, source_target_pairs={{8,12},{12,8},{16,20},{20,16},{9,13},{13,9},{17,21},{21,17},{10,14... | collective-permute-start | bytes 835592 | tf_op jit(solution)/shard_map/ppermute | solution.py:289
  28.5 17.5 %collective-permute-start.4 = (bf16[272,512]{1,0:T(8,128)(2,1)S(1)}, bf16[272,512]{1,0:T(8,128)(2,1)S(1)}, u32[]{:S(2)}, u32[]{:S(2)}) collective-permute-start(bf16[272,512]{1,0:T(8,128)(2,1)S(1)} %collective-permute-done.3.refs_5_), channel_id=1, source_target_pairs={{0,4},{4,0},{24,28},{28,24},{1,5},{5,1},{25,29},{29,25},{2,6},{6,2... | collective-permute-start | bytes 835592 | tf_op jit(solution)/shard_map/ppermute | solution.py:289
  39.3 6.7 %copy-start.2 = (bf16[256,2048]{1,0:T(8,128)(2,1)S(1)}, bf16[256,2048]{1,0:T(8,128)(2,1)}, u32[]{:S(2)}) copy-start(bf16[256,2048]{1,0:T(8,128)(2,1)} %refs_1_.7) | copy-start | bytes 3145732
  39.3 6.7 %copy-start.4 = (s32[2]{0:T(128)S(1)}, s32[2]{0:T(128)}, u32[]{:S(2)}) copy-start(s32[2]{0:T(128)} %refs_0_.7) | copy-start | bytes 28
  44.6 1.3 %copy-start = (f32[4,128,1024]{2,1,0:T(8,128)}, f32[4,128,1024]{2,1,0:T(8,128)S(1)}, u32[]{:S(2)}) copy-start(f32[4,128,1024]{2,1,0:T(8,128)S(1)} %get-tuple-element.29.refs_6_) | copy-start | bytes 6291460
  55.6 2.0 %collective-permute-start.10 = (bf16[256,768]{1,0:T(8,128)(2,1)S(1)}, bf16[256,768]{1,0:T(8,128)(2,1)S(1)}, u32[]{:S(2)}, u32[]{:S(2)}) collective-permute-start(bf16[256,768]{1,0:T(8,128)(2,1)S(1)} %get-tuple-element.34), channel_id=1, source_target_pairs={{0,1},{1,0},{2,3},{3,2},{4,5},{5,4},{6,7},{7,6},{8,9},{9,8},{10,11... | collective-permute-start | bytes 1179656 | tf_op jit(solution)/shard_map/ppermute | solution.py:339
  55.7 1.9 %collective-permute-start.9 = (bf16[256,256]{1,0:T(8,128)(2,1)S(1)}, bf16[256,256]{1,0:T(8,128)(2,1)S(1)}, u32[]{:S(2)}, u32[]{:S(2)}) collective-permute-start(bf16[256,256]{1,0:T(8,128)(2,1)S(1)} %get-tuple-element.32), channel_id=1, source_target_pairs={{0,1},{1,0},{2,3},{3,2},{4,5},{5,4},{6,7},{7,6},{8,9},{9,8},{10,11... | collective-permute-start | bytes 393224 | tf_op jit(solution)/shard_map/ppermute | solution.py:339
  65.0 2.2 %collective-permute-start.11 = (bf16[256,1024]{1,0:T(8,128)(2,1)S(1)}, bf16[256,1024]{1,0:T(8,128)(2,1)S(1)}, u32[]{:S(2)}, u32[]{:S(2)}) collective-permute-start(bf16[256,1024]{1,0:T(8,128)(2,1)S(1)} %get-tuple-element.36), channel_id=1, source_target_pairs={{0,1},{1,0},{2,3},{3,2},{4,5},{5,4},{6,7},{7,6},{8,9},{9,8},{10,11... | collective-permute-start | bytes 1572872 | tf_op jit(solution)/shard_map/ppermute | solution.py:339
  65.3 6.4 %collective-permute-start.12 = (bf16[256,256]{1,0:T(8,128)(2,1)S(1)}, bf16[256,256]{1,0:T(8,128)(2,1)S(1)}, u32[]{:S(2)}, u32[]{:S(2)}) collective-permute-start(bf16[256,256]{1,0:T(8,128)(2,1)S(1)} %add_convert_fusion.1.refs_0_), channel_id=1, source_target_pairs={{0,2},{1,3},{2,0},{3,1},{4,6},{5,7},{6,4},{7,5},{8,10},{9,11},{10,... | collective-permute-start | bytes 393224 | tf_op jit(solution)/shard_map/ppermute | solution.py:343
  66.8 12.7 %collective-permute-start.13 = (bf16[256,768]{1,0:T(8,128)(2,1)S(1)}, bf16[256,768]{1,0:T(8,128)(2,1)S(1)}, u32[]{:S(2)}, u32[]{:S(2)}) collective-permute-start(bf16[256,768]{1,0:T(8,128)(2,1)S(1)} %add_convert_fusion.refs_1_), channel_id=1, source_target_pairs={{0,2},{1,3},{2,0},{3,1},{4,6},{5,7},{6,4},{7,5},{8,10},{9,11},{10,... | collective-permute-start | bytes 1179656 | tf_op jit(solution)/shard_map/ppermute | solution.py:343

commit v4 on v3

--- a/solution.py
+++ b/solution.py
@@ -14,8 +14,9 @@
 HIDDEN = -1e30
 TAIL = 16
 DIGIT = 128
+WHOLE = pl.BlockSpec(memory_space=pltpu.VMEM)
 NT = (((1,), (1,)), ((), ()))
-DEPTH = 3
+DEPTH = 4
 VMEM_LIMIT = 16 << 20
 WIDE_LIMIT = 48 << 20
 
@@ -78,8 +79,8 @@
     pair = span // rows
     for b, found in enumerate(blocks):
         if len(found) == 2:
-            merged_ref[...] = found[0][...] + found[1][...]
-            blocks[b] = merged_ref
+            merged_ref[b] = found[0][...] + found[1][...]
+            blocks[b] = merged_ref.at[b]
         else:
             blocks[b] = found[0]
     lengths = [block.shape[0] - TAIL for block in blocks]
@@ -175,7 +176,7 @@
 
 
 def column_scratch(depth, widths):
-    wide = math.gcd(256, *widths)
+    wide = math.gcd(512, *widths)
     tiles = 2 * sum(widths) // wide
     return [pltpu.VMEM((tiles, depth, wide), jnp.bfloat16), pltpu.SemaphoreType.DMA((tiles,))]
 
@@ -198,7 +199,7 @@
     operands = [order, queries, *arrays, *(() if first else state)]
     in_specs = [scalars] + [whole] * (len(operands) - 1)
     scratch = [
-        pltpu.VMEM(arrays[0].shape, arrays[0].dtype),
+        pltpu.VMEM((len(blocks), *arrays[0].shape), arrays[0].dtype),
         pltpu.VMEM((parts, seen, rows), jnp.float32),
         pltpu.VMEM((kv_heads, HEAD_SIZE, seen), jnp.bfloat16),
     ]
@@ -258,6 +259,34 @@
     )(at, attended, weight, *after)
 
 
+def add_up_kernel(cuts, n_swapped, mine_ref, *refs):
+    out_ref = refs[-1]
+    swapped, arrived = refs[:n_swapped], refs[n_swapped:-1]
+    each = len(arrived) // (len(cuts) - 1)
+    for cut in range(len(cuts) - 1):
+        at = slice(cuts[cut], cuts[cut + 1])
+        total = mine_ref[:, at]
+        for ref in swapped:
+            total = total + ref[:, at].astype(jnp.float32)
+        for ref in arrived[cut * each : (cut + 1) * each]:
+            total = total + ref[...].astype(jnp.float32)
+        out_ref[:, at] = total.astype(out_ref.dtype)
+
+
+def add_up(mine, swapped, arriving, cuts):
+    arrived = [x for found in arriving for x in found]
+    return pl.pallas_call(
+        functools.partial(add_up_kernel, cuts, len(swapped)),
+        in_specs=[WHOLE] * (1 + len(swapped) + len(arrived)),
+        out_specs=WHOLE,
+        out_shape=jax.ShapeDtypeStruct(mine.shape, jnp.bfloat16),
+        compiler_params=pltpu.CompilerParams(vmem_limit_bytes=VMEM_LIMIT),
+        cost_estimate=pl.CostEstimate(
+            flops=4 * mine.size, bytes_accessed=10 * mine.size, transcendentals=0
+        ),
+    )(mine, *swapped, *arrived)
+
+
 def shards(n_ctx, n_tp, queries, keys, values, out_weight, block_order):
     heads_dev = queries.shape[1] // HEAD_SIZE
     group_size = QUERY_HEADS // KEY_VALUE_HEADS
@@ -300,15 +329,18 @@
 
     if outer == 4:
         near = move(own, lambda o, i: (o ^ 1, i))
-        mirror = move(own, lambda o, i: (3 - o, i))
+        own_crossed = cross(own)
+        mid = move(own, lambda o, i: {1: (2, i), 2: (1, i)}.get(o))
+        far = move(own, lambda o, i: {0: (3, i), 3: (0, i)}.get(o))
         third = move(own, lambda o, i: {0: (2, i), 3: (1, i)}.get(o))
-        own_crossed = cross(own)
-        onward = move(mirror, lambda o, i: {2: (3, i), 1: (0, i)}.get(o))
-        stages = [[(own,)], [(near,), (mirror,)] + [(x,) for x in own_crossed]]
-        stages += [[(x,) for x in cross(near) + cross(mirror)]]
-        stages[-1].append((third, onward))
-        late = zip(cross(third, (1, 2)), cross(onward, (0, 3)))
-        stages += [[pair] for pair in late]
+        near_crossed = cross(near)
+        onward = move(mid, lambda o, i: {2: (3, i), 1: (0, i)}.get(o))
+        middle, ends = (1, 2), (0, 3)
+        stages = [[(own,), (near,)] + [(x,) for x in own_crossed]]
+        stages.append([(mid, far)] + [(x,) for x in near_crossed] + [(third, onward)])
+        for a, b in ((mid, far), (third, onward)):
+            crossed = zip(cross(a, middle), cross(b, ends))
+            stages += [[pair] for pair in crossed]
     else:
         blocks = [own]
         for k in range(1, outer):
@@ -372,19 +404,10 @@
         arriving[cut].append(to_group(total, r))
     if jobs:
         send, mine = project(begins(0, [0]), attended, out_weight, share, after)
-        if cores > 1:
-            mine = mine + to_core(send).astype(jnp.float32)
     else:
-        mine = products[1]
-        if cores > 1:
-            mine = mine + to_core(products[0]).astype(jnp.float32)
-    result = []
-    for cut, found in enumerate(arriving):
-        total = mine[:, cuts[cut] : cuts[cut + 1]]
-        for x in found:
-            total = total + x.astype(jnp.float32)
-        result.append(total.astype(jnp.bfloat16))
-    return jnp.concatenate(result, axis=1)
+        send, mine = products
+    swapped = [to_core(send)] if cores > 1 else []
+    return add_up(mine, swapped, arriving, cuts)
 
 
 def solution(mesh):

time: 80.7 us -> 79.7 us (0.988)
  the two profiles are of different devices: /device:TPU:10 before, /device:TPU:0 now
where the time goes in v4:
time: 79.7 us; the launch traced here: 79.3 us
  Pallas kernels  28.4 us (36%)
  starting transfers between devices  25.8 us (32%)
  waiting for transfers between devices  19.4 us (24%)
  local copies, waits for them, and re-layouts  4.38 us (5%)
  other arithmetic  1.13 us (1%)
    ppermute x11, starting transfers between devices, move(): return lax.ppermute(block, 'ctx', pairs)  23 us
    pallas_call x4, Pallas kernels, attend(): pl.pallas_call(functools.partial(attend_kernel, halves, first, last, scal...  22.4 us
    ppermute x2, waiting for transfers between devices, to_group(): return lax.ppermute(x, 'tp', pairs)  12.2 us
    ppermute x11, waiting for transfers between devices, move(): return lax.ppermute(block, 'ctx', pairs)  5.86 us
    pallas_call x1, Pallas kernels, project(): pl.pallas_call(project_kernel, in_specs=[pl.BlockSpec(memory_space=pltpu....  5 us
    unnamed x10, local copies, waits for them, and re-layouts  3.22 us
    ppermute x2, starting transfers between devices, to_group(): return lax.ppermute(x, 'tp', pairs)  2.03 us
  transfers between devices with their start and end apart: 16, of which 4 were waited for; matrix products, arithmetic and copies ran while one was open for 0% of the time, Pallas kernels for 16%

profile of v4, /device:TPU:0, one launch (start us, length us, event | category | flops | bytes accessed | tf_op | source)
XLA Modules:
  0.0 79.3 jit_solution(2163067392178318614)
XLA Ops:
  0.9 1.0 %constant_dynamic-slice_fusion = (bf16[256,128]{1,0:T(8,128)(2,1)S(1)}, bf16[256,128]{1,0:T(8,128)(2,1)S(1)}, bf16[256,128]{1,0:T(8,128)(2,1)S(1)}, bf16[256,128]{1,0:T(8,128)(2,1)S(1)}) fusion(bf16[256,1024]{1,0:T(8,128)(2,1)} %param.7, s32[]{:T(128)S(6)} %select_n.48, s32[]{:T(128)S(6)} %add.75, bf16[256,1024]{1,0:T(8,128)(2,1)} %param.6), kind=kLoop, calls=%fused_computation.10 | loop fusion | bytes 524296 | tf_op jit(solution)/shard_map/slice | solution.py:301
  2.0 0.7 collective-permute-start.2
  2.7 5.9 %collective-permute-start.8 = (bf16[272,512]{1,0:T(8,128)(2,1)S(1)}, bf16[272,512]{1,0:T(8,128)(2,1)S(1)}, u32[]{:S(2)}, u32[]{:S(2)}) collective-permute-start(bf16[272,512]{1,0:T(8,128)(2,1)S(1)} %maximum_maximum_fusion.refs_2_), channel_id=1, source_target_pairs={{0,8},{4,12},{8,0},{12,4},{16,24},{20,28},{24,16},{28,20},{1,9},{5... | collective-permute-start | bytes 835592 | tf_op jit(solution)/shard_map/ppermute | solution.py:318
  8.6 1.5 %collective-permute-start.10 = (bf16[272,512]{1,0:T(8,128)(2,1)S(1)}, bf16[272,512]{1,0:T(8,128)(2,1)S(1)}, u32[]{:S(2)}, u32[]{:S(2)}) collective-permute-start(bf16[272,512]{1,0:T(8,128)(2,1)S(1)} %maximum_maximum_fusion.refs_2_), channel_id=1, source_target_pairs={{0,4},{4,0},{8,12},{12,8},{16,20},{20,16},{24,28},{28,24},{1,5},{5... | collective-permute-start | bytes 835592 | tf_op jit(solution)/shard_map/ppermute | solution.py:318
  10.1 3.2 %collective-permute-start.6 = (bf16[272,512]{1,0:T(8,128)(2,1)S(1)}, bf16[272,512]{1,0:T(8,128)(2,1)S(1)}, u32[]{:S(2)}, u32[]{:S(2)}) collective-permute-start(bf16[272,512]{1,0:T(8,128)(2,1)S(1)} %maximum_maximum_fusion.refs_2_), channel_id=1, source_target_pairs={{0,24},{4,28},{24,0},{28,4},{1,25},{5,29},{25,1},{29,5},{2,26},{6,... | collective-permute-start | bytes 835592 | tf_op jit(solution)/shard_map/ppermute | solution.py:318
  13.3 1.3 %collective-permute-start = (bf16[272,512]{1,0:T(8,128)(2,1)S(1)}, bf16[272,512]{1,0:T(8,128)(2,1)S(1)}, u32[]{:S(2)}, u32[]{:S(2)}) collective-permute-start(bf16[272,512]{1,0:T(8,128)(2,1)S(1)} %maximum_maximum_fusion.refs_2_), channel_id=1, source_target_pairs={{0,16},{4,20},{24,8},{28,12},{1,17},{5,21},{25,9},{29,13},{2,18},{... | collective-permute-start | bytes 835592 | tf_op jit(solution)/shard_map/ppermute | solution.py:318
  14.6 1.3 %collective-permute-start.3 = (bf16[272,512]{1,0:T(8,128)(2,1)S(1)}, bf16[272,512]{1,0:T(8,128)(2,1)S(1)}, u32[]{:S(2)}, u32[]{:S(2)}) collective-permute-start(bf16[272,512]{1,0:T(8,128)(2,1)S(1)} %collective-permute-done.2.refs_2_), channel_id=1, source_target_pairs={{8,0},{12,4},{16,24},{20,28},{9,1},{13,5},{17,25},{21,29},{10,2},{... | collective-permute-start | bytes 835592 | tf_op jit(solution)/shard_map/ppermute | solution.py:318
  16.0 1.1 %collective-permute-start.9 = (bf16[272,512]{1,0:T(8,128)(2,1)S(1)}, bf16[272,512]{1,0:T(8,128)(2,1)S(1)}, u32[]{:S(2)}, u32[]{:S(2)}) collective-permute-start(bf16[272,512]{1,0:T(8,128)(2,1)S(1)} %collective-permute-done.8.refs_3_), channel_id=1, source_target_pairs={{0,4},{4,0},{8,12},{12,8},{16,20},{20,16},{24,28},{28,24},{1,5},{5... | collective-permute-start | bytes 835592 | tf_op jit(solution)/shard_map/ppermute | solution.py:318
  17.3 0.7 collective-permute-start.5
  17.9 5.4 %collective-permute-done.6.refs_3_ = bf16[272,512]{1,0:T(8,128)(2,1)S(1)} collective-permute-done((bf16[272,512]{1,0:T(8,128)(2,1)S(1)}, bf16[272,512]{1,0:T(8,128)(2,1)S(1)}, u32[]{:S(2)}, u32[]{:S(2)}) %collective-permute-start.6) | collective-permute-done | bytes 278560 | tf_op jit(solution)/shard_map/ppermute | solution.py:318
  23.3 3.5 %collective-permute-start.7 = (bf16[272,512]{1,0:T(8,128)(2,1)S(1)}, bf16[272,512]{1,0:T(8,128)(2,1)S(1)}, u32[]{:S(2)}, u32[]{:S(2)}) collective-permute-start(bf16[272,512]{1,0:T(8,128)(2,1)S(1)} %collective-permute-done.6.refs_3_), channel_id=1, source_target_pairs={{0,4},{4,0},{24,28},{28,24},{1,5},{5,1},{25,29},{29,25},{2,6},{6,2... | collective-permute-start | bytes 835592 | tf_op jit(solution)/shard_map/ppermute | solution.py:318
  26.8 0.7 collective-permute-start.1
  28.0 3.1 %collective-permute-start.4 = (bf16[272,512]{1,0:T(8,128)(2,1)S(1)}, bf16[272,512]{1,0:T(8,128)(2,1)S(1)}, u32[]{:S(2)}, u32[]{:S(2)}) collective-permute-start(bf16[272,512]{1,0:T(8,128)(2,1)S(1)} %collective-permute-done.3.refs_6_), channel_id=1, source_target_pairs={{0,4},{4,0},{24,28},{28,24},{1,5},{5,1},{25,29},{29,25},{2,6},{6,2... | collective-permute-start | bytes 835592 | tf_op jit(solution)/shard_map/ppermute | solution.py:318
  31.1 1.2 %copy-done = bf16[256,2048]{1,0:T(8,128)(2,1)S(1)} copy-done((bf16[256,2048]{1,0:T(8,128)(2,1)S(1)}, bf16[256,2048]{1,0:T(8,128)(2,1)}, u32[]{:S(2)}) %copy-start) | copy-done | bytes 1048600
  33.0 4.9 %shard_map.55 = (f32[4,1,1024]{2,1,0:T(1,128)S(1)}, f32[4,1,1024]{2,1,0:T(1,128)S(1)}, f32[4,128,1024]{2,1,0:T(8,128)S(1)}) custom-call(s32[2]{0:T(128)S(1)} %copy-done.3, bf16[256,2048]{1,0:T(8,128)(2,1)S(1)} %copy-done, bf16[272,512]{1,0:T(8,128)(2,1)S(1)} %maximum_maximum_fusion.refs_2_, bf16[272,512]{1,0:T(8,128)(2,1)S(1)} %collective-permute-done.8.refs_3_, ...), custom_call_target="tpu_custom_call" | custom-call | flops 1610612736 | bytes 12582912 | tf_op jit(solution)/shard_map/pallas_call | solution.py:223
  37.9 5.3 %shard_map.56 = (f32[4,1,1024]{2,1,0:T(1,128)S(1)}, f32[4,1,1024]{2,1,0:T(1,128)S(1)}, f32[4,128,1024]{2,1,0:T(8,128)S(1)}) custom-call(s32[2]{0:T(128)S(1)} %copy-done.3, bf16[256,2048]{1,0:T(8,128)(2,1)S(1)} %copy-done, bf16[272,512]{1,0:T(8,128)(2,1)S(1)} %collective-permute-done.2.refs_2_, bf16[272,512]{1,0:T(8,128)(2,1)S(1)} %collective-permute-done.6.refs_3_, ...), custom_call_target="tpu_custom_call" | custom-call | flops 1610612736 | bytes 12582912 | tf_op jit(solution)/shard_map/pallas_call | solution.py:223
  43.2 2.7 %shard_map.57 = (f32[4,1,1024]{2,1,0:T(1,128)S(1)}, f32[4,1,1024]{2,1,0:T(1,128)S(1)}, f32[4,128,1024]{2,1,0:T(8,128)S(1)}) custom-call(s32[2]{0:T(128)S(1)} %copy-done.3, bf16[256,2048]{1,0:T(8,128)(2,1)S(1)} %copy-done, bf16[272,512]{1,0:T(8,128)(2,1)S(1)} %collective-permute-done.5.refs_2_, bf16[272,512]{1,0:T(8,128)(2,1)S(1)} %collective-permute-done.7.refs_3_, ...), custom_call_target="tpu_custom_call" | custom-call | flops 536870912 | bytes 4194304 | tf_op jit(solution)/shard_map/pallas_call | solution.py:223
  45.9 1.3 %copy-done.2 = f32[4,128,1024]{2,1,0:T(8,128)} copy-done((f32[4,128,1024]{2,1,0:T(8,128)}, f32[4,128,1024]{2,1,0:T(8,128)S(1)}, u32[]{:S(2)}) %copy-start.2) | copy-done | bytes 2097176
  47.3 9.5 %shard_map.58 = (bf16[256,2048]{1,0:T(8,128)(2,1)S(1)}, bf16[256,256]{1,0:T(8,128)(2,1)S(1)}, f32[256,256]{1,0:T(8,128)S(1)}, bf16[256,768]{1,0:T(8,128)(2,1)S(1)}, f32[256,768]{1,0:T(8,128)S(1)}) custom-call(s32[2]{0:T(128)S(1)} %copy-done.4, bf16[256,2048]{1,0:T(8,128)(2,1)S(1)} %copy-done.1, bf16[272,512]{1,0:T(8,128)(2,1)S(1)} %collective-permute-done.1.refs_2_, ...), custom_call_target="tpu_custom_call" | custom-call | flops 2684354560 | bytes 4194304 | tf_op jit(solution)/shard_map/pallas_call | solution.py:223
  57.5 1.3 %collective-permute-done.11 = bf16[256,256]{1,0:T(8,128)(2,1)S(1)} collective-permute-done((bf16[256,256]{1,0:T(8,128)(2,1)S(1)}, bf16[256,256]{1,0:T(8,128)(2,1)S(1)}, u32[]{:S(2)}, u32[]{:S(2)}) %collective-permute-start.11) | collective-permute-done | bytes 131104 | tf_op jit(solution)/shard_map/ppermute | solution.py:371
  58.9 5.0 %shard_map.59 = (bf16[256,1024]{1,0:T(8,128)(2,1)S(1)}, f32[256,1024]{1,0:T(8,128)S(1)}) custom-call(s32[2]{0:T(128)S(1)} %add_multiply_fusion.at_ref, bf16[256,2048]{1,0:T(8,128)(2,1)S(1)} %get-tuple-element.30.rows_ref, bf16[2048,4096]{1,0:T(8,128)(2,1)} %weight_ref.1, bf16[256,256]{1,0:T(8,128)(2,1)S(1)} %add_convert_fusion.1.refs_0_, ...), custom_call_target="tpu_custom_call" | custom-call | flops 2147483648 | bytes 8388608 | tf_op jit(solution)/shard_map/pallas_call | solution.py:247
  64.1 1.5 %collective-permute-start.15 = (bf16[256,768]{1,0:T(8,128)(2,1)S(1)}, bf16[256,768]{1,0:T(8,128)(2,1)S(1)}, u32[]{:S(2)}, u32[]{:S(2)}) collective-permute-start(bf16[256,768]{1,0:T(8,128)(2,1)S(1)} %add_convert_fusion.refs_1_), channel_id=1, source_target_pairs={{0,2},{1,3},{2,0},{3,1},{4,6},{5,7},{6,4},{7,5},{8,10},{9,11},{10,... | collective-permute-start | bytes 1179656 | tf_op jit(solution)/shard_map/ppermute | solution.py:375
  66.2 12.2 %collective-permute-done.14.refs_1_ = bf16[256,256]{1,0:T(8,128)(2,1)S(1)} collective-permute-done((bf16[256,256]{1,0:T(8,128)(2,1)S(1)}, bf16[256,256]{1,0:T(8,128)(2,1)S(1)}, u32[]{:S(2)}, u32[]{:S(2)}) %collective-permute-start.14) | collective-permute-done | bytes 131104 | tf_op jit(solution)/shard_map/ppermute | solution.py:375
  78.3 1.0 %shard_map.60 = bf16[256,1024]{1,0:T(8,128)(2,1)} custom-call(f32[256,1024]{1,0:T(8,128)S(1)} %get-tuple-element.35.mine_ref, bf16[256,1024]{1,0:T(8,128)(2,1)S(1)} %collective-permute-done.13.refs_0_, bf16[256,256]{1,0:T(8,128)(2,1)S(1)} %collective-permute-done.14.refs_1_, bf16[256,768]{1,0:T(8,128)(2,1)S(1)} %collective-permute-done.15.refs_2_), custom_call_target="tpu_custom_call" | custom-call | flops 1048576 | bytes 2621440 | tf_op jit(solution)/shard_map/pallas_call | solution.py:278
  (36 shorter events, 3.8 us)
Async XLA Ops:
  2.0 12.7 %collective-permute-start.2 = (bf16[272,512]{1,0:T(8,128)(2,1)S(1)}, bf16[272,512]{1,0:T(8,128)(2,1)S(1)}, u32[]{:S(2)}, u32[]{:S(2)}) collective-permute-start(bf16[272,512]{1,0:T(8,128)(2,1)S(1)} %maximum_maximum_fusion.refs_2_), channel_id=1, source_target_pairs={{8,16},{12,20},{16,8},{20,12},{9,17},{13,21},{17,9},{21,13},{10,18... | collective-permute-start | bytes 835592 | tf_op jit(solution)/shard_map/ppermute | solution.py:318
  2.7 13.3 %collective-permute-start.8 = (bf16[272,512]{1,0:T(8,128)(2,1)S(1)}, bf16[272,512]{1,0:T(8,128)(2,1)S(1)}, u32[]{:S(2)}, u32[]{:S(2)}) collective-permute-start(bf16[272,512]{1,0:T(8,128)(2,1)S(1)} %maximum_maximum_fusion.refs_2_), channel_id=1, source_target_pairs={{0,8},{4,12},{8,0},{12,4},{16,24},{20,28},{24,16},{28,20},{1,9},{5... | collective-permute-start | bytes 835592 | tf_op jit(solution)/shard_map/ppermute | solution.py:318
  8.6 8.7 %collective-permute-start.10 = (bf16[272,512]{1,0:T(8,128)(2,1)S(1)}, bf16[272,512]{1,0:T(8,128)(2,1)S(1)}, u32[]{:S(2)}, u32[]{:S(2)}) collective-permute-start(bf16[272,512]{1,0:T(8,128)(2,1)S(1)} %maximum_maximum_fusion.refs_2_), channel_id=1, source_target_pairs={{0,4},{4,0},{8,12},{12,8},{16,20},{20,16},{24,28},{28,24},{1,5},{5... | collective-permute-start | bytes 835592 | tf_op jit(solution)/shard_map/ppermute | solution.py:318
  10.1 13.3 %collective-permute-start.6 = (bf16[272,512]{1,0:T(8,128)(2,1)S(1)}, bf16[272,512]{1,0:T(8,128)(2,1)S(1)}, u32[]{:S(2)}, u32[]{:S(2)}) collective-permute-start(bf16[272,512]{1,0:T(8,128)(2,1)S(1)} %maximum_maximum_fusion.refs_2_), channel_id=1, source_target_pairs={{0,24},{4,28},{24,0},{28,4},{1,25},{5,29},{25,1},{29,5},{2,26},{6,... | collective-permute-start | bytes 835592 | tf_op jit(solution)/shard_map/ppermute | solution.py:318
  13.3 13.5 %collective-permute-start = (bf16[272,512]{1,0:T(8,128)(2,1)S(1)}, bf16[272,512]{1,0:T(8,128)(2,1)S(1)}, u32[]{:S(2)}, u32[]{:S(2)}) collective-permute-start(bf16[272,512]{1,0:T(8,128)(2,1)S(1)} %maximum_maximum_fusion.refs_2_), channel_id=1, source_target_pairs={{0,16},{4,20},{24,8},{28,12},{1,17},{5,21},{25,9},{29,13},{2,18},{... | collective-permute-start | bytes 835592 | tf_op jit(solution)/shard_map/ppermute | solution.py:318
  14.6 13.3 %collective-permute-start.3 = (bf16[272,512]{1,0:T(8,128)(2,1)S(1)}, bf16[272,512]{1,0:T(8,128)(2,1)S(1)}, u32[]{:S(2)}, u32[]{:S(2)}) collective-permute-start(bf16[272,512]{1,0:T(8,128)(2,1)S(1)} %collective-permute-done.2.refs_2_), channel_id=1, source_target_pairs={{8,0},{12,4},{16,24},{20,28},{9,1},{13,5},{17,25},{21,29},{10,2},{... | collective-permute-start | bytes 835592 | tf_op jit(solution)/shard_map/ppermute | solution.py:318
  16.0 21.9 %collective-permute-start.9 = (bf16[272,512]{1,0:T(8,128)(2,1)S(1)}, bf16[272,512]{1,0:T(8,128)(2,1)S(1)}, u32[]{:S(2)}, u32[]{:S(2)}) collective-permute-start(bf16[272,512]{1,0:T(8,128)(2,1)S(1)} %collective-permute-done.8.refs_3_), channel_id=1, source_target_pairs={{0,4},{4,0},{8,12},{12,8},{16,20},{20,16},{24,28},{28,24},{1,5},{5... | collective-permute-start | bytes 835592 | tf_op jit(solution)/shard_map/ppermute | solution.py:318
  17.3 25.9 %collective-permute-start.5 = (bf16[272,512]{1,0:T(8,128)(2,1)S(1)}, bf16[272,512]{1,0:T(8,128)(2,1)S(1)}, u32[]{:S(2)}, u32[]{:S(2)}) collective-permute-start(bf16[272,512]{1,0:T(8,128)(2,1)S(1)} %collective-permute-done.2.refs_2_), channel_id=1, source_target_pairs={{8,12},{12,8},{16,20},{20,16},{9,13},{13,9},{17,21},{21,17},{10,14... | collective-permute-start | bytes 835592 | tf_op jit(solution)/shard_map/ppermute | solution.py:318
  23.3 19.9 %collective-permute-start.7 = (bf16[272,512]{1,0:T(8,128)(2,1)S(1)}, bf16[272,512]{1,0:T(8,128)(2,1)S(1)}, u32[]{:S(2)}, u32[]{:S(2)}) collective-permute-start(bf16[272,512]{1,0:T(8,128)(2,1)S(1)} %collective-permute-done.6.refs_3_), channel_id=1, source_target_pairs={{0,4},{4,0},{24,28},{28,24},{1,5},{5,1},{25,29},{29,25},{2,6},{6,2... | collective-permute-start | bytes 835592 | tf_op jit(solution)/shard_map/ppermute | solution.py:318
  26.8 20.5 %collective-permute-start.1 = (bf16[272,512]{1,0:T(8,128)(2,1)S(1)}, bf16[272,512]{1,0:T(8,128)(2,1)S(1)}, u32[]{:S(2)}, u32[]{:S(2)}) collective-permute-start(bf16[272,512]{1,0:T(8,128)(2,1)S(1)} %collective-permute-done.refs_5_), channel_id=1, source_target_pairs={{8,12},{12,8},{16,20},{20,16},{9,13},{13,9},{17,21},{21,17},{10,14... | collective-permute-start | bytes 835592 | tf_op jit(solution)/shard_map/ppermute | solution.py:318
  28.0 19.3 %collective-permute-start.4 = (bf16[272,512]{1,0:T(8,128)(2,1)S(1)}, bf16[272,512]{1,0:T(8,128)(2,1)S(1)}, u32[]{:S(2)}, u32[]{:S(2)}) collective-permute-start(bf16[272,512]{1,0:T(8,128)(2,1)S(1)} %collective-permute-done.3.refs_6_), channel_id=1, source_target_pairs={{0,4},{4,0},{24,28},{28,24},{1,5},{5,1},{25,29},{29,25},{2,6},{6,2... | collective-permute-start | bytes 835592 | tf_op jit(solution)/shard_map/ppermute | solution.py:318
  31.1 1.2 %copy-start = (bf16[256,2048]{1,0:T(8,128)(2,1)S(1)}, bf16[256,2048]{1,0:T(8,128)(2,1)}, u32[]{:S(2)}) copy-start(bf16[256,2048]{1,0:T(8,128)(2,1)} %refs_1_.7) | copy-start | bytes 3145732
  32.3 0.7 copy-start.3
  43.2 4.1 %copy-start.1 = (bf16[256,2048]{1,0:T(8,128)(2,1)S(1)}, bf16[256,2048]{1,0:T(8,128)(2,1)}, u32[]{:S(2)}) copy-start(bf16[256,2048]{1,0:T(8,128)(2,1)} %refs_1_.7) | copy-start | bytes 3145732
  43.2 4.1 %copy-start.4 = (s32[2]{0:T(128)S(1)}, s32[2]{0:T(128)}, u32[]{:S(2)}) copy-start(s32[2]{0:T(128)} %refs_0_.7) | copy-start | bytes 28
  45.9 1.3 %copy-start.2 = (f32[4,128,1024]{2,1,0:T(8,128)}, f32[4,128,1024]{2,1,0:T(8,128)S(1)}, u32[]{:S(2)}) copy-start(f32[4,128,1024]{2,1,0:T(8,128)S(1)} %get-tuple-element.29.refs_6_) | copy-start | bytes 6291460
  56.8 2.0 %collective-permute-start.12 = (bf16[256,768]{1,0:T(8,128)(2,1)S(1)}, bf16[256,768]{1,0:T(8,128)(2,1)S(1)}, u32[]{:S(2)}, u32[]{:S(2)}) collective-permute-start(bf16[256,768]{1,0:T(8,128)(2,1)S(1)} %get-tuple-element.34), channel_id=1, source_target_pairs={{0,1},{1,0},{2,3},{3,2},{4,5},{5,4},{6,7},{7,6},{8,9},{9,8},{10,11... | collective-permute-start | bytes 1179656 | tf_op jit(solution)/shard_map/ppermute | solution.py:371
  56.9 1.9 %collective-permute-start.11 = (bf16[256,256]{1,0:T(8,128)(2,1)S(1)}, bf16[256,256]{1,0:T(8,128)(2,1)S(1)}, u32[]{:S(2)}, u32[]{:S(2)}) collective-permute-start(bf16[256,256]{1,0:T(8,128)(2,1)S(1)} %get-tuple-element.32), channel_id=1, source_target_pairs={{0,1},{1,0},{2,3},{3,2},{4,5},{5,4},{6,7},{7,6},{8,9},{9,8},{10,11... | collective-permute-start | bytes 393224 | tf_op jit(solution)/shard_map/ppermute | solution.py:371
  63.9 14.4 %collective-permute-start.13 = (bf16[256,1024]{1,0:T(8,128)(2,1)S(1)}, bf16[256,1024]{1,0:T(8,128)(2,1)S(1)}, u32[]{:S(2)}, u32[]{:S(2)}) collective-permute-start(bf16[256,1024]{1,0:T(8,128)(2,1)S(1)} %get-tuple-element.36), channel_id=1, source_target_pairs={{0,1},{1,0},{2,3},{3,2},{4,5},{5,4},{6,7},{7,6},{8,9},{9,8},{10,11... | collective-permute-start | bytes 1572872 | tf_op jit(solution)/shard_map/ppermute | solution.py:371
  64.1 14.2 %collective-permute-start.15 = (bf16[256,768]{1,0:T(8,128)(2,1)S(1)}, bf16[256,768]{1,0:T(8,128)(2,1)S(1)}, u32[]{:S(2)}, u32[]{:S(2)}) collective-permute-start(bf16[256,768]{1,0:T(8,128)(2,1)S(1)} %add_convert_fusion.refs_1_), channel_id=1, source_target_pairs={{0,2},{1,3},{2,0},{3,1},{4,6},{5,7},{6,4},{7,5},{8,10},{9,11},{10,... | collective-permute-start | bytes 1179656 | tf_op jit(solution)/shard_map/ppermute | solution.py:375
  65.6 12.7 %collective-permute-start.14 = (bf16[256,256]{1,0:T(8,128)(2,1)S(1)}, bf16[256,256]{1,0:T(8,128)(2,1)S(1)}, u32[]{:S(2)}, u32[]{:S(2)}) collective-permute-start(bf16[256,256]{1,0:T(8,128)(2,1)S(1)} %add_convert_fusion.1.refs_0_), channel_id=1, source_target_pairs={{0,2},{1,3},{2,0},{3,1},{4,6},{5,7},{6,4},{7,5},{8,10},{9,11},{10,... | collective-permute-start | bytes 393224 | tf_op jit(solution)/shard_map/ppermute | solution.py:375

commit v5 on v4

--- a/solution.py
+++ b/solution.py
@@ -329,18 +329,19 @@
 
     if outer == 4:
         near = move(own, lambda o, i: (o ^ 1, i))
+        mid = move(own, lambda o, i: {1: (2, i), 2: (1, i)}.get(o))
         own_crossed = cross(own)
-        mid = move(own, lambda o, i: {1: (2, i), 2: (1, i)}.get(o))
-        far = move(own, lambda o, i: {0: (3, i), 3: (0, i)}.get(o))
+        onward = move(mid, lambda o, i: {2: (3, i), 1: (0, i)}.get(o))
         third = move(own, lambda o, i: {0: (2, i), 3: (1, i)}.get(o))
         near_crossed = cross(near)
-        onward = move(mid, lambda o, i: {2: (3, i), 1: (0, i)}.get(o))
-        middle, ends = (1, 2), (0, 3)
+        mid_crossed = cross(mid, (1, 2))
+        far = move(own, lambda o, i: {0: (3, i), 3: (0, i)}.get(o))
+        third_crossed = list(zip(cross(third, (1, 2)), cross(onward, (0, 3))))
+        far_crossed = cross(far, (0, 3))
         stages = [[(own,), (near,)] + [(x,) for x in own_crossed]]
-        stages.append([(mid, far)] + [(x,) for x in near_crossed] + [(third, onward)])
-        for a, b in ((mid, far), (third, onward)):
-            crossed = zip(cross(a, middle), cross(b, ends))
-            stages += [[pair] for pair in crossed]
+        stages.append([(third, onward)] + [(x,) for x in near_crossed])
+        stages.append([(mid, far)] + third_crossed)
+        stages += [[pair] for pair in zip(mid_crossed, far_crossed)]
     else:
         blocks = [own]
         for k in range(1, outer):

time: 79.7 us -> 82.9 us (1.040)
  waiting for transfers between devices: 19.4 us -> 22.8 us
    ppermute x11, waiting for transfers between devices: 5.86 us -> 9.31 us  [move(): return lax.ppermute(block, 'ctx', pairs)]
  transfers between devices with their start and end apart: 16 -> 16, of which waited for: 4 -> 4; matrix products, arithmetic and copies ran while one was open for 0% -> 0% of each run, Pallas kernels for 16% -> 15%
where the time goes in v5:
time: 82.9 us; the launch traced here: 82.5 us
  Pallas kernels  27.7 us (33%)
  starting transfers between devices  26.2 us (32%)
  waiting for transfers between devices  22.8 us (28%)
  local copies, waits for them, and re-layouts  4.38 us (5%)
  other arithmetic  1.12 us (1%)
    ppermute x11, starting transfers between devices, move(): return lax.ppermute(block, 'ctx', pairs)  23.4 us
    pallas_call x4, Pallas kernels, attend(): pl.pallas_call(functools.partial(attend_kernel, halves, first, last, scal...  21.8 us
    ppermute x2, waiting for transfers between devices, to_group(): return lax.ppermute(x, 'tp', pairs)  12.2 us
    ppermute x11, waiting for transfers between devices, move(): return lax.ppermute(block, 'ctx', pairs)  9.31 us
    pallas_call x1, Pallas kernels, project(): pl.pallas_call(project_kernel, in_specs=[pl.BlockSpec(memory_space=pltpu....  5 us
    unnamed x10, local copies, waits for them, and re-layouts  3.22 us
    ppermute x2, starting transfers between devices, to_group(): return lax.ppermute(x, 'tp', pairs)  2.03 us
  transfers between devices with their start and end apart: 16, of which 4 were waited for; matrix products, arithmetic and copies ran while one was open for 0% of the time, Pallas kernels for 15%

profile of v5, /device:TPU:0, one launch (start us, length us, event | category | flops | bytes accessed | tf_op | source)
XLA Modules:
  0.0 82.5 jit_solution(10812390792723432586)
XLA Ops:
  0.9 1.0 %constant_dynamic-slice_fusion = (bf16[256,128]{1,0:T(8,128)(2,1)S(1)}, bf16[256,128]{1,0:T(8,128)(2,1)S(1)}, bf16[256,128]{1,0:T(8,128)(2,1)S(1)}, bf16[256,128]{1,0:T(8,128)(2,1)S(1)}) fusion(bf16[256,1024]{1,0:T(8,128)(2,1)} %param.7, s32[]{:T(128)S(6)} %select_n.48, s32[]{:T(128)S(6)} %add.75, bf16[256,1024]{1,0:T(8,128)(2,1)} %param.6), kind=kLoop, calls=%fused_computation.10 | loop fusion | bytes 524296 | tf_op jit(solution)/shard_map/slice | solution.py:301
  2.0 0.7 collective-permute-start
  2.7 5.9 %collective-permute-start.8 = (bf16[272,512]{1,0:T(8,128)(2,1)S(1)}, bf16[272,512]{1,0:T(8,128)(2,1)S(1)}, u32[]{:S(2)}, u32[]{:S(2)}) collective-permute-start(bf16[272,512]{1,0:T(8,128)(2,1)S(1)} %maximum_maximum_fusion.refs_2_), channel_id=1, source_target_pairs={{0,8},{4,12},{8,0},{12,4},{16,24},{20,28},{24,16},{28,20},{1,9},{5... | collective-permute-start | bytes 835592 | tf_op jit(solution)/shard_map/ppermute | solution.py:318
  8.6 1.8 %collective-permute-start.4 = (bf16[272,512]{1,0:T(8,128)(2,1)S(1)}, bf16[272,512]{1,0:T(8,128)(2,1)S(1)}, u32[]{:S(2)}, u32[]{:S(2)}) collective-permute-start(bf16[272,512]{1,0:T(8,128)(2,1)S(1)} %maximum_maximum_fusion.refs_2_), channel_id=1, source_target_pairs={{0,16},{4,20},{24,8},{28,12},{1,17},{5,21},{25,9},{29,13},{2,18},{... | collective-permute-start | bytes 835592 | tf_op jit(solution)/shard_map/ppermute | solution.py:318
  10.4 1.3 %collective-permute-start.6 = (bf16[272,512]{1,0:T(8,128)(2,1)S(1)}, bf16[272,512]{1,0:T(8,128)(2,1)S(1)}, u32[]{:S(2)}, u32[]{:S(2)}) collective-permute-start(bf16[272,512]{1,0:T(8,128)(2,1)S(1)} %collective-permute-done.refs_2_), channel_id=1, source_target_pairs={{8,0},{12,4},{16,24},{20,28},{9,1},{13,5},{17,25},{21,29},{10,2},{... | collective-permute-start | bytes 835592 | tf_op jit(solution)/shard_map/ppermute | solution.py:318
  11.7 1.6 %collective-permute-start.10 = (bf16[272,512]{1,0:T(8,128)(2,1)S(1)}, bf16[272,512]{1,0:T(8,128)(2,1)S(1)}, u32[]{:S(2)}, u32[]{:S(2)}) collective-permute-start(bf16[272,512]{1,0:T(8,128)(2,1)S(1)} %maximum_maximum_fusion.refs_2_), channel_id=1, source_target_pairs={{0,4},{4,0},{8,12},{12,8},{16,20},{20,16},{24,28},{28,24},{1,5},{5... | collective-permute-start | bytes 835592 | tf_op jit(solution)/shard_map/ppermute | solution.py:318
  13.3 4.4 %collective-permute-start.2 = (bf16[272,512]{1,0:T(8,128)(2,1)S(1)}, bf16[272,512]{1,0:T(8,128)(2,1)S(1)}, u32[]{:S(2)}, u32[]{:S(2)}) collective-permute-start(bf16[272,512]{1,0:T(8,128)(2,1)S(1)} %maximum_maximum_fusion.refs_2_), channel_id=1, source_target_pairs={{0,24},{4,28},{24,0},{28,4},{1,25},{5,29},{25,1},{29,5},{2,26},{6,... | collective-permute-start | bytes 835592 | tf_op jit(solution)/shard_map/ppermute | solution.py:318
  18.4 3.2 %collective-permute-done.4.refs_2_ = bf16[272,512]{1,0:T(8,128)(2,1)S(1)} collective-permute-done((bf16[272,512]{1,0:T(8,128)(2,1)S(1)}, bf16[272,512]{1,0:T(8,128)(2,1)S(1)}, u32[]{:S(2)}, u32[]{:S(2)}) %collective-permute-start.4) | collective-permute-done | bytes 278560 | tf_op jit(solution)/shard_map/ppermute | solution.py:318
  21.6 0.7 collective-permute-start.5
  22.3 6.1 %collective-permute-done.6.refs_3_ = bf16[272,512]{1,0:T(8,128)(2,1)S(1)} collective-permute-done((bf16[272,512]{1,0:T(8,128)(2,1)S(1)}, bf16[272,512]{1,0:T(8,128)(2,1)S(1)}, u32[]{:S(2)}, u32[]{:S(2)}) %collective-permute-start.6) | collective-permute-done | bytes 278560 | tf_op jit(solution)/shard_map/ppermute | solution.py:318
  28.3 3.4 %collective-permute-start.7 = (bf16[272,512]{1,0:T(8,128)(2,1)S(1)}, bf16[272,512]{1,0:T(8,128)(2,1)S(1)}, u32[]{:S(2)}, u32[]{:S(2)}) collective-permute-start(bf16[272,512]{1,0:T(8,128)(2,1)S(1)} %collective-permute-done.6.refs_3_), channel_id=1, source_target_pairs={{0,4},{4,0},{24,28},{28,24},{1,5},{5,1},{25,29},{29,25},{2,6},{6,2... | collective-permute-start | bytes 835592 | tf_op jit(solution)/shard_map/ppermute | solution.py:318
  31.8 0.7 collective-permute-start.1
  32.5 2.4 %collective-permute-start.3 = (bf16[272,512]{1,0:T(8,128)(2,1)S(1)}, bf16[272,512]{1,0:T(8,128)(2,1)S(1)}, u32[]{:S(2)}, u32[]{:S(2)}) collective-permute-start(bf16[272,512]{1,0:T(8,128)(2,1)S(1)} %collective-permute-done.2.refs_3_), channel_id=1, source_target_pairs={{0,4},{4,0},{24,28},{28,24},{1,5},{5,1},{25,29},{29,25},{2,6},{6,2... | collective-permute-start | bytes 835592 | tf_op jit(solution)/shard_map/ppermute | solution.py:318
  35.0 1.2 %copy-done = bf16[256,2048]{1,0:T(8,128)(2,1)S(1)} copy-done((bf16[256,2048]{1,0:T(8,128)(2,1)S(1)}, bf16[256,2048]{1,0:T(8,128)(2,1)}, u32[]{:S(2)}) %copy-start) | copy-done | bytes 1048600
  36.8 4.9 %shard_map.55 = (f32[4,1,1024]{2,1,0:T(1,128)S(1)}, f32[4,1,1024]{2,1,0:T(1,128)S(1)}, f32[4,128,1024]{2,1,0:T(8,128)S(1)}) custom-call(s32[2]{0:T(128)S(1)} %copy-done.3, bf16[256,2048]{1,0:T(8,128)(2,1)S(1)} %copy-done, bf16[272,512]{1,0:T(8,128)(2,1)S(1)} %maximum_maximum_fusion.refs_2_, bf16[272,512]{1,0:T(8,128)(2,1)S(1)} %collective-permute-done.8.refs_3_, ...), custom_call_target="tpu_custom_call" | custom-call | flops 1610612736 | bytes 12582912 | tf_op jit(solution)/shard_map/pallas_call | solution.py:223
  41.8 3.8 %shard_map.56 = (f32[4,1,1024]{2,1,0:T(1,128)S(1)}, f32[4,1,1024]{2,1,0:T(1,128)S(1)}, f32[4,128,1024]{2,1,0:T(8,128)S(1)}) custom-call(s32[2]{0:T(128)S(1)} %copy-done.3, bf16[256,2048]{1,0:T(8,128)(2,1)S(1)} %copy-done, bf16[272,512]{1,0:T(8,128)(2,1)S(1)} %collective-permute-done.4.refs_2_, bf16[272,512]{1,0:T(8,128)(2,1)S(1)} %collective-permute-done.6.refs_3_, ...), custom_call_target="tpu_custom_call" | custom-call | flops 1073741824 | bytes 8388608 | tf_op jit(solution)/shard_map/pallas_call | solution.py:223
  45.6 3.7 %shard_map.57 = (f32[4,1,1024]{2,1,0:T(1,128)S(1)}, f32[4,1,1024]{2,1,0:T(1,128)S(1)}, f32[4,128,1024]{2,1,0:T(8,128)S(1)}) custom-call(s32[2]{0:T(128)S(1)} %copy-done.3, bf16[256,2048]{1,0:T(8,128)(2,1)S(1)} %copy-done, bf16[272,512]{1,0:T(8,128)(2,1)S(1)} %collective-permute-done.refs_2_, bf16[272,512]{1,0:T(8,128)(2,1)S(1)} %collective-permute-done.2.refs_3_, ...), custom_call_target="tpu_custom_call" | custom-call | flops 1073741824 | bytes 8388608 | tf_op jit(solution)/shard_map/pallas_call | solution.py:223
  49.3 1.3 %copy-done.2 = f32[4,128,1024]{2,1,0:T(8,128)} copy-done((f32[4,128,1024]{2,1,0:T(8,128)}, f32[4,128,1024]{2,1,0:T(8,128)S(1)}, u32[]{:S(2)}) %copy-start.2) | copy-done | bytes 2097176
  50.7 9.3 %shard_map.58 = (bf16[256,2048]{1,0:T(8,128)(2,1)S(1)}, bf16[256,256]{1,0:T(8,128)(2,1)S(1)}, f32[256,256]{1,0:T(8,128)S(1)}, bf16[256,768]{1,0:T(8,128)(2,1)S(1)}, f32[256,768]{1,0:T(8,128)S(1)}) custom-call(s32[2]{0:T(128)S(1)} %copy-done.4, bf16[256,2048]{1,0:T(8,128)(2,1)S(1)} %copy-done.1, bf16[272,512]{1,0:T(8,128)(2,1)S(1)} %collective-permute-done.1.refs_2_, ...), custom_call_target="tpu_custom_call" | custom-call | flops 2684354560 | bytes 4194304 | tf_op jit(solution)/shard_map/pallas_call | solution.py:223
  60.7 1.3 %collective-permute-done.11 = bf16[256,256]{1,0:T(8,128)(2,1)S(1)} collective-permute-done((bf16[256,256]{1,0:T(8,128)(2,1)S(1)}, bf16[256,256]{1,0:T(8,128)(2,1)S(1)}, u32[]{:S(2)}, u32[]{:S(2)}) %collective-permute-start.11) | collective-permute-done | bytes 131104 | tf_op jit(solution)/shard_map/ppermute | solution.py:372
  62.1 5.0 %shard_map.59 = (bf16[256,1024]{1,0:T(8,128)(2,1)S(1)}, f32[256,1024]{1,0:T(8,128)S(1)}) custom-call(s32[2]{0:T(128)S(1)} %add_multiply_fusion.at_ref, bf16[256,2048]{1,0:T(8,128)(2,1)S(1)} %get-tuple-element.30.rows_ref, bf16[2048,4096]{1,0:T(8,128)(2,1)} %weight_ref.1, bf16[256,256]{1,0:T(8,128)(2,1)S(1)} %add_convert_fusion.1.refs_0_, ...), custom_call_target="tpu_custom_call" | custom-call | flops 2147483648 | bytes 8388608 | tf_op jit(solution)/shard_map/pallas_call | solution.py:247
  67.4 1.5 %collective-permute-start.15 = (bf16[256,768]{1,0:T(8,128)(2,1)S(1)}, bf16[256,768]{1,0:T(8,128)(2,1)S(1)}, u32[]{:S(2)}, u32[]{:S(2)}) collective-permute-start(bf16[256,768]{1,0:T(8,128)(2,1)S(1)} %add_convert_fusion.refs_1_), channel_id=1, source_target_pairs={{0,2},{1,3},{2,0},{3,1},{4,6},{5,7},{6,4},{7,5},{8,10},{9,11},{10,... | collective-permute-start | bytes 1179656 | tf_op jit(solution)/shard_map/ppermute | solution.py:376
  69.4 12.2 %collective-permute-done.14.refs_1_ = bf16[256,256]{1,0:T(8,128)(2,1)S(1)} collective-permute-done((bf16[256,256]{1,0:T(8,128)(2,1)S(1)}, bf16[256,256]{1,0:T(8,128)(2,1)S(1)}, u32[]{:S(2)}, u32[]{:S(2)}) %collective-permute-start.14) | collective-permute-done | bytes 131104 | tf_op jit(solution)/shard_map/ppermute | solution.py:376
  81.6 1.0 %shard_map.60 = bf16[256,1024]{1,0:T(8,128)(2,1)} custom-call(f32[256,1024]{1,0:T(8,128)S(1)} %get-tuple-element.35.mine_ref, bf16[256,1024]{1,0:T(8,128)(2,1)S(1)} %collective-permute-done.13.refs_0_, bf16[256,256]{1,0:T(8,128)(2,1)S(1)} %collective-permute-done.14.refs_1_, bf16[256,768]{1,0:T(8,128)(2,1)S(1)} %collective-permute-done.15.refs_2_), custom_call_target="tpu_custom_call" | custom-call | flops 1048576 | bytes 2621440 | tf_op jit(solution)/shard_map/pallas_call | solution.py:278
  (36 shorter events, 3.9 us)
Async XLA Ops:
  2.0 8.4 %collective-permute-start = (bf16[272,512]{1,0:T(8,128)(2,1)S(1)}, bf16[272,512]{1,0:T(8,128)(2,1)S(1)}, u32[]{:S(2)}, u32[]{:S(2)}) collective-permute-start(bf16[272,512]{1,0:T(8,128)(2,1)S(1)} %maximum_maximum_fusion.refs_2_), channel_id=1, source_target_pairs={{8,16},{12,20},{16,8},{20,12},{9,17},{13,21},{17,9},{21,13},{10,18... | collective-permute-start | bytes 835592 | tf_op jit(solution)/shard_map/ppermute | solution.py:318
  2.7 15.0 %collective-permute-start.8 = (bf16[272,512]{1,0:T(8,128)(2,1)S(1)}, bf16[272,512]{1,0:T(8,128)(2,1)S(1)}, u32[]{:S(2)}, u32[]{:S(2)}) collective-permute-start(bf16[272,512]{1,0:T(8,128)(2,1)S(1)} %maximum_maximum_fusion.refs_2_), channel_id=1, source_target_pairs={{0,8},{4,12},{8,0},{12,4},{16,24},{20,28},{24,16},{28,20},{1,9},{5... | collective-permute-start | bytes 835592 | tf_op jit(solution)/shard_map/ppermute | solution.py:318
  8.6 13.0 %collective-permute-start.4 = (bf16[272,512]{1,0:T(8,128)(2,1)S(1)}, bf16[272,512]{1,0:T(8,128)(2,1)S(1)}, u32[]{:S(2)}, u32[]{:S(2)}) collective-permute-start(bf16[272,512]{1,0:T(8,128)(2,1)S(1)} %maximum_maximum_fusion.refs_2_), channel_id=1, source_target_pairs={{0,16},{4,20},{24,8},{28,12},{1,17},{5,21},{25,9},{29,13},{2,18},{... | collective-permute-start | bytes 835592 | tf_op jit(solution)/shard_map/ppermute | solution.py:318
  10.4 17.9 %collective-permute-start.6 = (bf16[272,512]{1,0:T(8,128)(2,1)S(1)}, bf16[272,512]{1,0:T(8,128)(2,1)S(1)}, u32[]{:S(2)}, u32[]{:S(2)}) collective-permute-start(bf16[272,512]{1,0:T(8,128)(2,1)S(1)} %collective-permute-done.refs_2_), channel_id=1, source_target_pairs={{8,0},{12,4},{16,24},{20,28},{9,1},{13,5},{17,25},{21,29},{10,2},{... | collective-permute-start | bytes 835592 | tf_op jit(solution)/shard_map/ppermute | solution.py:318
  11.7 20.1 %collective-permute-start.10 = (bf16[272,512]{1,0:T(8,128)(2,1)S(1)}, bf16[272,512]{1,0:T(8,128)(2,1)S(1)}, u32[]{:S(2)}, u32[]{:S(2)}) collective-permute-start(bf16[272,512]{1,0:T(8,128)(2,1)S(1)} %maximum_maximum_fusion.refs_2_), channel_id=1, source_target_pairs={{0,4},{4,0},{8,12},{12,8},{16,20},{20,16},{24,28},{28,24},{1,5},{5... | collective-permute-start | bytes 835592 | tf_op jit(solution)/shard_map/ppermute | solution.py:318
  13.3 19.2 %collective-permute-start.2 = (bf16[272,512]{1,0:T(8,128)(2,1)S(1)}, bf16[272,512]{1,0:T(8,128)(2,1)S(1)}, u32[]{:S(2)}, u32[]{:S(2)}) collective-permute-start(bf16[272,512]{1,0:T(8,128)(2,1)S(1)} %maximum_maximum_fusion.refs_2_), channel_id=1, source_target_pairs={{0,24},{4,28},{24,0},{28,4},{1,25},{5,29},{25,1},{29,5},{2,26},{6,... | collective-permute-start | bytes 835592 | tf_op jit(solution)/shard_map/ppermute | solution.py:318
  17.7 24.1 %collective-permute-start.9 = (bf16[272,512]{1,0:T(8,128)(2,1)S(1)}, bf16[272,512]{1,0:T(8,128)(2,1)S(1)}, u32[]{:S(2)}, u32[]{:S(2)}) collective-permute-start(bf16[272,512]{1,0:T(8,128)(2,1)S(1)} %collective-permute-done.8.refs_3_), channel_id=1, source_target_pairs={{0,4},{4,0},{8,12},{12,8},{16,20},{20,16},{24,28},{28,24},{1,5},{5... | collective-permute-start | bytes 835592 | tf_op jit(solution)/shard_map/ppermute | solution.py:318
  21.6 24.0 %collective-permute-start.5 = (bf16[272,512]{1,0:T(8,128)(2,1)S(1)}, bf16[272,512]{1,0:T(8,128)(2,1)S(1)}, u32[]{:S(2)}, u32[]{:S(2)}) collective-permute-start(bf16[272,512]{1,0:T(8,128)(2,1)S(1)} %collective-permute-done.4.refs_2_), channel_id=1, source_target_pairs={{8,12},{12,8},{16,20},{20,16},{9,13},{13,9},{17,21},{21,17},{10,14... | collective-permute-start | bytes 835592 | tf_op jit(solution)/shard_map/ppermute | solution.py:318
  28.3 17.2 %collective-permute-start.7 = (bf16[272,512]{1,0:T(8,128)(2,1)S(1)}, bf16[272,512]{1,0:T(8,128)(2,1)S(1)}, u32[]{:S(2)}, u32[]{:S(2)}) collective-permute-start(bf16[272,512]{1,0:T(8,128)(2,1)S(1)} %collective-permute-done.6.refs_3_), channel_id=1, source_target_pairs={{0,4},{4,0},{24,28},{28,24},{1,5},{5,1},{25,29},{29,25},{2,6},{6,2... | collective-permute-start | bytes 835592 | tf_op jit(solution)/shard_map/ppermute | solution.py:318
  31.8 18.9 %collective-permute-start.1 = (bf16[272,512]{1,0:T(8,128)(2,1)S(1)}, bf16[272,512]{1,0:T(8,128)(2,1)S(1)}, u32[]{:S(2)}, u32[]{:S(2)}) collective-permute-start(bf16[272,512]{1,0:T(8,128)(2,1)S(1)} %collective-permute-done.refs_2_), channel_id=1, source_target_pairs={{8,12},{12,8},{16,20},{20,16},{9,13},{13,9},{17,21},{21,17},{10,14... | collective-permute-start | bytes 835592 | tf_op jit(solution)/shard_map/ppermute | solution.py:318
  32.5 18.2 %collective-permute-start.3 = (bf16[272,512]{1,0:T(8,128)(2,1)S(1)}, bf16[272,512]{1,0:T(8,128)(2,1)S(1)}, u32[]{:S(2)}, u32[]{:S(2)}) collective-permute-start(bf16[272,512]{1,0:T(8,128)(2,1)S(1)} %collective-permute-done.2.refs_3_), channel_id=1, source_target_pairs={{0,4},{4,0},{24,28},{28,24},{1,5},{5,1},{25,29},{29,25},{2,6},{6,2... | collective-permute-start | bytes 835592 | tf_op jit(solution)/shard_map/ppermute | solution.py:318
  35.0 1.2 %copy-start = (bf16[256,2048]{1,0:T(8,128)(2,1)S(1)}, bf16[256,2048]{1,0:T(8,128)(2,1)}, u32[]{:S(2)}) copy-start(bf16[256,2048]{1,0:T(8,128)(2,1)} %refs_1_.7) | copy-start | bytes 3145732
  36.2 0.7 copy-start.3
  45.6 5.1 %copy-start.1 = (bf16[256,2048]{1,0:T(8,128)(2,1)S(1)}, bf16[256,2048]{1,0:T(8,128)(2,1)}, u32[]{:S(2)}) copy-start(bf16[256,2048]{1,0:T(8,128)(2,1)} %refs_1_.7) | copy-start | bytes 3145732
  45.6 5.1 %copy-start.4 = (s32[2]{0:T(128)S(1)}, s32[2]{0:T(128)}, u32[]{:S(2)}) copy-start(s32[2]{0:T(128)} %refs_0_.7) | copy-start | bytes 28
  49.3 1.3 %copy-start.2 = (f32[4,128,1024]{2,1,0:T(8,128)}, f32[4,128,1024]{2,1,0:T(8,128)S(1)}, u32[]{:S(2)}) copy-start(f32[4,128,1024]{2,1,0:T(8,128)S(1)} %get-tuple-element.29.refs_6_) | copy-start | bytes 6291460
  60.0 2.0 %collective-permute-start.12 = (bf16[256,768]{1,0:T(8,128)(2,1)S(1)}, bf16[256,768]{1,0:T(8,128)(2,1)S(1)}, u32[]{:S(2)}, u32[]{:S(2)}) collective-permute-start(bf16[256,768]{1,0:T(8,128)(2,1)S(1)} %get-tuple-element.34), channel_id=1, source_target_pairs={{0,1},{1,0},{2,3},{3,2},{4,5},{5,4},{6,7},{7,6},{8,9},{9,8},{10,11... | collective-permute-start | bytes 1179656 | tf_op jit(solution)/shard_map/ppermute | solution.py:372
  60.1 1.9 %collective-permute-start.11 = (bf16[256,256]{1,0:T(8,128)(2,1)S(1)}, bf16[256,256]{1,0:T(8,128)(2,1)S(1)}, u32[]{:S(2)}, u32[]{:S(2)}) collective-permute-start(bf16[256,256]{1,0:T(8,128)(2,1)S(1)} %get-tuple-element.32), channel_id=1, source_target_pairs={{0,1},{1,0},{2,3},{3,2},{4,5},{5,4},{6,7},{7,6},{8,9},{9,8},{10,11... | collective-permute-start | bytes 393224 | tf_op jit(solution)/shard_map/ppermute | solution.py:372
  67.1 14.4 %collective-permute-start.13 = (bf16[256,1024]{1,0:T(8,128)(2,1)S(1)}, bf16[256,1024]{1,0:T(8,128)(2,1)S(1)}, u32[]{:S(2)}, u32[]{:S(2)}) collective-permute-start(bf16[256,1024]{1,0:T(8,128)(2,1)S(1)} %get-tuple-element.36), channel_id=1, source_target_pairs={{0,1},{1,0},{2,3},{3,2},{4,5},{5,4},{6,7},{7,6},{8,9},{9,8},{10,11... | collective-permute-start | bytes 1572872 | tf_op jit(solution)/shard_map/ppermute | solution.py:372
  67.4 14.2 %collective-permute-start.15 = (bf16[256,768]{1,0:T(8,128)(2,1)S(1)}, bf16[256,768]{1,0:T(8,128)(2,1)S(1)}, u32[]{:S(2)}, u32[]{:S(2)}) collective-permute-start(bf16[256,768]{1,0:T(8,128)(2,1)S(1)} %add_convert_fusion.refs_1_), channel_id=1, source_target_pairs={{0,2},{1,3},{2,0},{3,1},{4,6},{5,7},{6,4},{7,5},{8,10},{9,11},{10,... | collective-permute-start | bytes 1179656 | tf_op jit(solution)/shard_map/ppermute | solution.py:376
  68.9 12.7 %collective-permute-start.14 = (bf16[256,256]{1,0:T(8,128)(2,1)S(1)}, bf16[256,256]{1,0:T(8,128)(2,1)S(1)}, u32[]{:S(2)}, u32[]{:S(2)}) collective-permute-start(bf16[256,256]{1,0:T(8,128)(2,1)S(1)} %add_convert_fusion.1.refs_0_), channel_id=1, source_target_pairs={{0,2},{1,3},{2,0},{3,1},{4,6},{5,7},{6,4},{7,5},{8,10},{9,11},{10,... | collective-permute-start | bytes 393224 | tf_op jit(solution)/shard_map/ppermute | solution.py:376

commit v6 on v4

--- a/solution.py
+++ b/solution.py
@@ -144,7 +144,7 @@
             total = total + old_total[c, :, at] * factor
             acc = acc + old_acc[c, :, at] * factor
         if last:
-            done = (acc * (1.0 / total)).T.astype(jnp.bfloat16)
+            done = (acc * (1.0 / total)).astype(jnp.bfloat16).T
             for j in range(pair):
                 outs[0][i * rows : (i + 1) * rows, head_cols(k, p, j)] = done[
                     j * rows : (j + 1) * rows, :
@@ -329,18 +329,12 @@
 
     if outer == 4:
         near = move(own, lambda o, i: (o ^ 1, i))
-        own_crossed = cross(own)
-        mid = move(own, lambda o, i: {1: (2, i), 2: (1, i)}.get(o))
-        far = move(own, lambda o, i: {0: (3, i), 3: (0, i)}.get(o))
-        third = move(own, lambda o, i: {0: (2, i), 3: (1, i)}.get(o))
-        near_crossed = cross(near)
-        onward = move(mid, lambda o, i: {2: (3, i), 1: (0, i)}.get(o))
-        middle, ends = (1, 2), (0, 3)
-        stages = [[(own,), (near,)] + [(x,) for x in own_crossed]]
-        stages.append([(mid, far)] + [(x,) for x in near_crossed] + [(third, onward)])
-        for a, b in ((mid, far), (third, onward)):
-            crossed = zip(cross(a, middle), cross(b, ends))
-            stages += [[pair] for pair in crossed]
+        opposite = move(own, lambda o, i: (o ^ 2, i))
+        mirror = move(own, lambda o, i: (o ^ 3, i))
+        stages = [[(own,), (near,)] + [(x,) for x in cross(own)]]
+        stages.append([(opposite,)] + [(x,) for x in cross(near)])
+        stages.append([(mirror,)] + [(x,) for x in cross(opposite)])
+        stages += [[(x,)] for x in cross(mirror)]
     else:
         blocks = [own]
         for k in range(1, outer):
@@ -357,14 +351,14 @@
     cores = math.gcd(n_tp, 2)
     groups = n_tp // cores
     core, group = tp % cores, tp // cores
-    cuts = [0, share // 4, share] if groups == 2 else [0, share]
+    cuts = [0, share // 2, share] if groups == 2 else [0, share]
     widths = [b - a for a, b in zip(cuts, cuts[1:])]
     jobs = [(cut, r) for r in range(1, groups) for cut in range(len(widths))]
 
-    def begins(r, numbers):
+    def begins(cut, r):
         to = (group + r) % groups * cores
         firsts = jnp.stack([to + (core + 1) % cores, to + core]) * share
-        return jnp.concatenate([firsts + cuts[n] for n in numbers]).astype(jnp.int32)
+        return (firsts + cuts[cut]).astype(jnp.int32)
 
     def to_core(x):
         pairs = [(t, t // cores * cores + (t + 1) % cores) for t in range(n_tp)]
@@ -377,35 +371,29 @@
     state = None
     for blocks in stages[:-1]:
         state = attend(block_order, queries, blocks, state, kv_heads)
-    together = list(range(len(widths)))
-    attended, *products = attend(
+    cut, r = jobs[0] if jobs else (0, 0)
+    attended, send, keep = attend(
         block_order,
         queries,
         stages[-1],
         state,
         kv_heads,
-        (begins(min(1, groups - 1), together), out_weight, widths),
+        (begins(cut, r), out_weight, [widths[cut] if jobs else share]),
     )
-    for r in range(2, groups):
-        for cut in together:
-            products += project(
-                begins(r, [cut]), attended, out_weight, widths[cut], products[-2:-1]
-            )
-
     arriving = [[] for _ in widths]
     after = ()
-    others = [to_core(products[2 * n]) for n in range(len(jobs))] if cores > 1 else None
     for name, (cut, r) in enumerate(jobs):
-        total = products[2 * name + 1]
+        if name > 0:
+            send, keep = project(begins(cut, r), attended, out_weight, widths[cut], after)
         if cores > 1:
-            total = total + others[name].astype(jnp.float32)
-        total = total.astype(jnp.bfloat16)
-        after += (total,)
+            keep = keep + to_core(send).astype(jnp.float32)
+        total = keep.astype(jnp.bfloat16)
+        after = (total,)
         arriving[cut].append(to_group(total, r))
     if jobs:
-        send, mine = project(begins(0, [0]), attended, out_weight, share, after)
+        send, mine = project(begins(0, 0), attended, out_weight, share, after)
     else:
-        send, mine = products
+        mine = keep
     swapped = [to_core(send)] if cores > 1 else []
     return add_up(mine, swapped, arriving, cuts)
 

time: 79.7 us -> 79.1 us (level)
  the two profiles are of different devices: /device:TPU:0 before, /device:TPU:8 now
where the time goes in v6:
time: 79.1 us; the launch traced here: 78.9 us
  waiting for transfers between devices  34.4 us (43%)
  Pallas kernels  28 us (35%)
  starting transfers between devices  12.2 us (15%)
  local copies, waits for them, and re-layouts  3.05 us (4%)
  other arithmetic  1.09 us (1%)
    ppermute x7, waiting for transfers between devices, move(): return lax.ppermute(block, 'ctx', pairs)  19.3 us
    pallas_call x4, Pallas kernels, attend(): pl.pallas_call(functools.partial(attend_kernel, halves, first, last, scal...  18.5 us
    ppermute x2, waiting for transfers between devices, to_group(): return lax.ppermute(x, 'tp', pairs)  12.2 us
    ppermute x7, starting transfers between devices, move(): return lax.ppermute(block, 'ctx', pairs)  9.67 us
    pallas_call x2, Pallas kernels, project(): pl.pallas_call(project_kernel, in_specs=[pl.BlockSpec(memory_space=pltpu....  8.57 us
    ppermute x3, waiting for transfers between devices, to_core(): return lax.ppermute(x, 'tp', pairs)  2.85 us
    ppermute x2, starting transfers between devices, to_group(): return lax.ppermute(x, 'tp', pairs)  2.03 us
    unnamed x8, local copies, waits for them, and re-layouts  1.89 us
  transfers between devices with their start and end apart: 12, of which 7 were waited for; matrix products, arithmetic and copies ran while one was open for 0% of the time, Pallas kernels for 16%

profile of v6, /device:TPU:8, one launch (start us, length us, event | category | flops | bytes accessed | tf_op | source)
XLA Modules:
  0.0 78.9 jit_solution(994433142429303804)
XLA Ops:
  0.0 0.7 convert_bitcast_fusion
  0.9 1.0 %constant_dynamic-slice_fusion = (bf16[256,128]{1,0:T(8,128)(2,1)S(1)}, bf16[256,128]{1,0:T(8,128)(2,1)S(1)}, bf16[256,128]{1,0:T(8,128)(2,1)S(1)}, bf16[256,128]{1,0:T(8,128)(2,1)S(1)}) fusion(bf16[256,1024]{1,0:T(8,128)(2,1)} %param.7, s32[]{:T(128)S(6)} %select_n.52, s32[]{:T(128)S(6)} %add.80, bf16[256,1024]{1,0:T(8,128)(2,1)} %param.6), kind=kLoop, calls=%fused_computation.10 | loop fusion | bytes 524296 | tf_op jit(solution)/shard_map/slice | solution.py:301
  2.0 3.0 %collective-permute-start.2 = (bf16[272,512]{1,0:T(8,128)(2,1)S(1)}, bf16[272,512]{1,0:T(8,128)(2,1)S(1)}, u32[]{:S(2)}, u32[]{:S(2)}) collective-permute-start(bf16[272,512]{1,0:T(8,128)(2,1)S(1)} %maximum_maximum_fusion.refs_2_), channel_id=1, source_target_pairs={{0,16},{4,20},{8,24},{12,28},{16,0},{20,4},{24,8},{28,12},{1,17},{... | collective-permute-start | bytes 835592 | tf_op jit(solution)/shard_map/ppermute | solution.py:318
  5.5 1.5 %collective-permute-start.6 = (bf16[272,512]{1,0:T(8,128)(2,1)S(1)}, bf16[272,512]{1,0:T(8,128)(2,1)S(1)}, u32[]{:S(2)}, u32[]{:S(2)}) collective-permute-start(bf16[272,512]{1,0:T(8,128)(2,1)S(1)} %maximum_maximum_fusion.refs_2_), channel_id=1, source_target_pairs={{0,4},{4,0},{8,12},{12,8},{16,20},{20,16},{24,28},{28,24},{1,5},{5... | collective-permute-start | bytes 835592 | tf_op jit(solution)/shard_map/ppermute | solution.py:318
  7.0 6.4 %collective-permute-done.4.refs_3_ = bf16[272,512]{1,0:T(8,128)(2,1)S(1)} collective-permute-done((bf16[272,512]{1,0:T(8,128)(2,1)S(1)}, bf16[272,512]{1,0:T(8,128)(2,1)S(1)}, u32[]{:S(2)}, u32[]{:S(2)}) %collective-permute-start.4) | collective-permute-done | bytes 278560 | tf_op jit(solution)/shard_map/ppermute | solution.py:318
  13.5 1.7 %collective-permute-start.5 = (bf16[272,512]{1,0:T(8,128)(2,1)S(1)}, bf16[272,512]{1,0:T(8,128)(2,1)S(1)}, u32[]{:S(2)}, u32[]{:S(2)}) collective-permute-start(bf16[272,512]{1,0:T(8,128)(2,1)S(1)} %collective-permute-done.4.refs_3_), channel_id=1, source_target_pairs={{0,4},{4,0},{8,12},{12,8},{16,20},{20,16},{24,28},{28,24},{1,5},{5... | collective-permute-start | bytes 835592 | tf_op jit(solution)/shard_map/ppermute | solution.py:318
  15.1 8.9 %collective-permute-done.2.refs_2_ = bf16[272,512]{1,0:T(8,128)(2,1)S(1)} collective-permute-done((bf16[272,512]{1,0:T(8,128)(2,1)S(1)}, bf16[272,512]{1,0:T(8,128)(2,1)S(1)}, u32[]{:S(2)}, u32[]{:S(2)}) %collective-permute-start.2) | collective-permute-done | bytes 278560 | tf_op jit(solution)/shard_map/ppermute | solution.py:318
  24.1 1.5 %collective-permute-start.3 = (bf16[272,512]{1,0:T(8,128)(2,1)S(1)}, bf16[272,512]{1,0:T(8,128)(2,1)S(1)}, u32[]{:S(2)}, u32[]{:S(2)}) collective-permute-start(bf16[272,512]{1,0:T(8,128)(2,1)S(1)} %collective-permute-done.2.refs_2_), channel_id=1, source_target_pairs={{0,4},{4,0},{8,12},{12,8},{16,20},{20,16},{24,28},{28,24},{1,5},{5... | collective-permute-start | bytes 835592 | tf_op jit(solution)/shard_map/ppermute | solution.py:318
  25.6 3.9 %collective-permute-done.refs_2_ = bf16[272,512]{1,0:T(8,128)(2,1)S(1)} collective-permute-done((bf16[272,512]{1,0:T(8,128)(2,1)S(1)}, bf16[272,512]{1,0:T(8,128)(2,1)S(1)}, u32[]{:S(2)}, u32[]{:S(2)}) %collective-permute-start) | collective-permute-done | bytes 278560 | tf_op jit(solution)/shard_map/ppermute | solution.py:318
  29.6 1.5 %collective-permute-start.1 = (bf16[272,512]{1,0:T(8,128)(2,1)S(1)}, bf16[272,512]{1,0:T(8,128)(2,1)S(1)}, u32[]{:S(2)}, u32[]{:S(2)}) collective-permute-start(bf16[272,512]{1,0:T(8,128)(2,1)S(1)} %collective-permute-done.refs_2_), channel_id=1, source_target_pairs={{0,4},{4,0},{8,12},{12,8},{16,20},{20,16},{24,28},{28,24},{1,5},{5... | collective-permute-start | bytes 835592 | tf_op jit(solution)/shard_map/ppermute | solution.py:318
  31.1 1.2 %copy-done = bf16[256,2048]{1,0:T(8,128)(2,1)S(1)} copy-done((bf16[256,2048]{1,0:T(8,128)(2,1)S(1)}, bf16[256,2048]{1,0:T(8,128)(2,1)}, u32[]{:S(2)}) %copy-start) | copy-done | bytes 1048600
  32.3 0.7 copy-done.2
  32.9 4.9 %shard_map.55 = (f32[4,1,1024]{2,1,0:T(1,128)S(1)}, f32[4,1,1024]{2,1,0:T(1,128)S(1)}, f32[4,128,1024]{2,1,0:T(8,128)S(1)}) custom-call(s32[2]{0:T(128)S(1)} %copy-done.2, bf16[256,2048]{1,0:T(8,128)(2,1)S(1)} %copy-done, bf16[272,512]{1,0:T(8,128)(2,1)S(1)} %maximum_maximum_fusion.refs_2_, bf16[272,512]{1,0:T(8,128)(2,1)S(1)} %collective-permute-done.4.refs_3_, ...), custom_call_target="tpu_custom_call" | custom-call | flops 1610612736 | bytes 12582912 | tf_op jit(solution)/shard_map/pallas_call | solution.py:223
  37.9 3.7 %shard_map.56 = (f32[4,1,1024]{2,1,0:T(1,128)S(1)}, f32[4,1,1024]{2,1,0:T(1,128)S(1)}, f32[4,128,1024]{2,1,0:T(8,128)S(1)}) custom-call(s32[2]{0:T(128)S(1)} %copy-done.2, bf16[256,2048]{1,0:T(8,128)(2,1)S(1)} %copy-done, bf16[272,512]{1,0:T(8,128)(2,1)S(1)} %collective-permute-done.2.refs_2_, bf16[272,512]{1,0:T(8,128)(2,1)S(1)} %collective-permute-done.5.refs_3_, ...), custom_call_target="tpu_custom_call" | custom-call | flops 1073741824 | bytes 8388608 | tf_op jit(solution)/shard_map/pallas_call | solution.py:223
  41.6 3.7 %shard_map.57 = (f32[4,1,1024]{2,1,0:T(1,128)S(1)}, f32[4,1,1024]{2,1,0:T(1,128)S(1)}, f32[4,128,1024]{2,1,0:T(8,128)S(1)}) custom-call(s32[2]{0:T(128)S(1)} %copy-done.2, bf16[256,2048]{1,0:T(8,128)(2,1)S(1)} %copy-done, bf16[272,512]{1,0:T(8,128)(2,1)S(1)} %collective-permute-done.refs_2_, bf16[272,512]{1,0:T(8,128)(2,1)S(1)} %collective-permute-done.3.refs_3_, ...), custom_call_target="tpu_custom_call" | custom-call | flops 1073741824 | bytes 8388608 | tf_op jit(solution)/shard_map/pallas_call | solution.py:223
  45.4 6.2 %shard_map.58 = (bf16[256,2048]{1,0:T(8,128)(2,1)S(1)}, bf16[256,512]{1,0:T(8,128)(2,1)S(1)}, f32[256,512]{1,0:T(8,128)S(1)}) custom-call(s32[2]{0:T(128)S(1)} %copy-done.3, bf16[256,2048]{1,0:T(8,128)(2,1)S(1)} %copy-done.1, bf16[272,512]{1,0:T(8,128)(2,1)S(1)} %collective-permute-done.1.refs_2_, f32[4,1,1024]{2,1,0:T(1,128)S(1)} %get-tuple-element.27.refs_3_, ...), custom_call_target="tpu_custom_call" | custom-call | flops 1610612736 | bytes 4194304 | tf_op jit(solution)/shard_map/pallas_call | solution.py:223
  51.6 1.5 %collective-permute-done.7 = bf16[256,512]{1,0:T(8,128)(2,1)S(1)} collective-permute-done((bf16[256,512]{1,0:T(8,128)(2,1)S(1)}, bf16[256,512]{1,0:T(8,128)(2,1)S(1)}, u32[]{:S(2)}, u32[]{:S(2)}) %collective-permute-start.7) | collective-permute-done | bytes 262176 | tf_op jit(solution)/shard_map/ppermute | solution.py:365
  53.2 3.6 %shard_map.59 = (bf16[256,512]{1,0:T(8,128)(2,1)S(1)}, f32[256,512]{1,0:T(8,128)S(1)}) custom-call(s32[2]{0:T(128)S(1)} %get-tuple-element.37.at_ref, bf16[256,2048]{1,0:T(8,128)(2,1)S(1)} %get-tuple-element.30.rows_ref, bf16[2048,4096]{1,0:T(8,128)(2,1)} %weight_ref.3, bf16[256,512]{1,0:T(8,128)(2,1)S(1)} %add_convert_fusion.1.refs_0_), custom_call_target="tpu_custom_call" | custom-call | flops 1073741824 | bytes 4194304 | tf_op jit(solution)/shard_map/pallas_call | solution.py:247
  57.1 1.3 %collective-permute-done.8 = bf16[256,512]{1,0:T(8,128)(2,1)S(1)} collective-permute-done((bf16[256,512]{1,0:T(8,128)(2,1)S(1)}, bf16[256,512]{1,0:T(8,128)(2,1)S(1)}, u32[]{:S(2)}, u32[]{:S(2)}) %collective-permute-start.8) | collective-permute-done | bytes 262176 | tf_op jit(solution)/shard_map/ppermute | solution.py:365
  58.5 5.0 %shard_map.60 = (bf16[256,1024]{1,0:T(8,128)(2,1)S(1)}, f32[256,1024]{1,0:T(8,128)S(1)}) custom-call(s32[2]{0:T(128)S(1)} %add_multiply_fusion.at_ref, bf16[256,2048]{1,0:T(8,128)(2,1)S(1)} %get-tuple-element.30.rows_ref, bf16[2048,4096]{1,0:T(8,128)(2,1)} %weight_ref.3, bf16[256,512]{1,0:T(8,128)(2,1)S(1)} %add_convert_fusion.refs_0_), custom_call_target="tpu_custom_call" | custom-call | flops 2147483648 | bytes 8388608 | tf_op jit(solution)/shard_map/pallas_call | solution.py:247
  63.7 1.5 %collective-permute-start.10 = (bf16[256,512]{1,0:T(8,128)(2,1)S(1)}, bf16[256,512]{1,0:T(8,128)(2,1)S(1)}, u32[]{:S(2)}, u32[]{:S(2)}) collective-permute-start(bf16[256,512]{1,0:T(8,128)(2,1)S(1)} %add_convert_fusion.1.refs_0_), channel_id=1, source_target_pairs={{0,2},{1,3},{2,0},{3,1},{4,6},{5,7},{6,4},{7,5},{8,10},{9,11},{10,... | collective-permute-start | bytes 786440 | tf_op jit(solution)/shard_map/ppermute | solution.py:369
  65.7 7.2 %collective-permute-done.10.refs_1_ = bf16[256,512]{1,0:T(8,128)(2,1)S(1)} collective-permute-done((bf16[256,512]{1,0:T(8,128)(2,1)S(1)}, bf16[256,512]{1,0:T(8,128)(2,1)S(1)}, u32[]{:S(2)}, u32[]{:S(2)}) %collective-permute-start.10) | collective-permute-done | bytes 262176 | tf_op jit(solution)/shard_map/ppermute | solution.py:369
  72.9 5.0 %collective-permute-done.11.refs_2_ = bf16[256,512]{1,0:T(8,128)(2,1)S(1)} collective-permute-done((bf16[256,512]{1,0:T(8,128)(2,1)S(1)}, bf16[256,512]{1,0:T(8,128)(2,1)S(1)}, u32[]{:S(2)}, u32[]{:S(2)}) %collective-permute-start.11) | collective-permute-done | bytes 262176 | tf_op jit(solution)/shard_map/ppermute | solution.py:369
  77.9 0.9 %shard_map.61 = bf16[256,1024]{1,0:T(8,128)(2,1)} custom-call(f32[256,1024]{1,0:T(8,128)S(1)} %get-tuple-element.35.mine_ref, bf16[256,1024]{1,0:T(8,128)(2,1)S(1)} %collective-permute-done.9.refs_0_, bf16[256,512]{1,0:T(8,128)(2,1)S(1)} %collective-permute-done.10.refs_1_, bf16[256,512]{1,0:T(8,128)(2,1)S(1)} %collective-permute-done.11.refs_2_), custom_call_target="tpu_custom_call" | custom-call | flops 1048576 | bytes 2621440 | tf_op jit(solution)/shard_map/pallas_call | solution.py:278
  (26 shorter events, 2.2 us)
Async XLA Ops:
  2.0 11.5 %collective-permute-start.4 = (bf16[272,512]{1,0:T(8,128)(2,1)S(1)}, bf16[272,512]{1,0:T(8,128)(2,1)S(1)}, u32[]{:S(2)}, u32[]{:S(2)}) collective-permute-start(bf16[272,512]{1,0:T(8,128)(2,1)S(1)} %maximum_maximum_fusion.refs_2_), channel_id=1, source_target_pairs={{0,8},{4,12},{8,0},{12,4},{16,24},{20,28},{24,16},{28,20},{1,9},{5... | collective-permute-start | bytes 835592 | tf_op jit(solution)/shard_map/ppermute | solution.py:318
  2.0 22.0 %collective-permute-start.2 = (bf16[272,512]{1,0:T(8,128)(2,1)S(1)}, bf16[272,512]{1,0:T(8,128)(2,1)S(1)}, u32[]{:S(2)}, u32[]{:S(2)}) collective-permute-start(bf16[272,512]{1,0:T(8,128)(2,1)S(1)} %maximum_maximum_fusion.refs_2_), channel_id=1, source_target_pairs={{0,16},{4,20},{8,24},{12,28},{16,0},{20,4},{24,8},{28,12},{1,17},{... | collective-permute-start | bytes 835592 | tf_op jit(solution)/shard_map/ppermute | solution.py:318
  5.1 24.5 %collective-permute-start = (bf16[272,512]{1,0:T(8,128)(2,1)S(1)}, bf16[272,512]{1,0:T(8,128)(2,1)S(1)}, u32[]{:S(2)}, u32[]{:S(2)}) collective-permute-start(bf16[272,512]{1,0:T(8,128)(2,1)S(1)} %maximum_maximum_fusion.refs_2_), channel_id=1, source_target_pairs={{0,24},{4,28},{8,16},{12,20},{16,8},{20,12},{24,0},{28,4},{1,25},{... | collective-permute-start | bytes 835592 | tf_op jit(solution)/shard_map/ppermute | solution.py:318
  5.5 25.5 %collective-permute-start.6 = (bf16[272,512]{1,0:T(8,128)(2,1)S(1)}, bf16[272,512]{1,0:T(8,128)(2,1)S(1)}, u32[]{:S(2)}, u32[]{:S(2)}) collective-permute-start(bf16[272,512]{1,0:T(8,128)(2,1)S(1)} %maximum_maximum_fusion.refs_2_), channel_id=1, source_target_pairs={{0,4},{4,0},{8,12},{12,8},{16,20},{20,16},{24,28},{28,24},{1,5},{5... | collective-permute-start | bytes 835592 | tf_op jit(solution)/shard_map/ppermute | solution.py:318
  13.5 24.4 %collective-permute-start.5 = (bf16[272,512]{1,0:T(8,128)(2,1)S(1)}, bf16[272,512]{1,0:T(8,128)(2,1)S(1)}, u32[]{:S(2)}, u32[]{:S(2)}) collective-permute-start(bf16[272,512]{1,0:T(8,128)(2,1)S(1)} %collective-permute-done.4.refs_3_), channel_id=1, source_target_pairs={{0,4},{4,0},{8,12},{12,8},{16,20},{20,16},{24,28},{28,24},{1,5},{5... | collective-permute-start | bytes 835592 | tf_op jit(solution)/shard_map/ppermute | solution.py:318
  24.1 17.5 %collective-permute-start.3 = (bf16[272,512]{1,0:T(8,128)(2,1)S(1)}, bf16[272,512]{1,0:T(8,128)(2,1)S(1)}, u32[]{:S(2)}, u32[]{:S(2)}) collective-permute-start(bf16[272,512]{1,0:T(8,128)(2,1)S(1)} %collective-permute-done.2.refs_2_), channel_id=1, source_target_pairs={{0,4},{4,0},{8,12},{12,8},{16,20},{20,16},{24,28},{28,24},{1,5},{5... | collective-permute-start | bytes 835592 | tf_op jit(solution)/shard_map/ppermute | solution.py:318
  29.6 15.8 %collective-permute-start.1 = (bf16[272,512]{1,0:T(8,128)(2,1)S(1)}, bf16[272,512]{1,0:T(8,128)(2,1)S(1)}, u32[]{:S(2)}, u32[]{:S(2)}) collective-permute-start(bf16[272,512]{1,0:T(8,128)(2,1)S(1)} %collective-permute-done.refs_2_), channel_id=1, source_target_pairs={{0,4},{4,0},{8,12},{12,8},{16,20},{20,16},{24,28},{28,24},{1,5},{5... | collective-permute-start | bytes 835592 | tf_op jit(solution)/shard_map/ppermute | solution.py:318
  31.1 1.2 %copy-start = (bf16[256,2048]{1,0:T(8,128)(2,1)S(1)}, bf16[256,2048]{1,0:T(8,128)(2,1)}, u32[]{:S(2)}) copy-start(bf16[256,2048]{1,0:T(8,128)(2,1)} %refs_1_.7) | copy-start | bytes 3145732
  32.3 0.7 copy-start.2
  41.5 3.8 %copy-start.1 = (bf16[256,2048]{1,0:T(8,128)(2,1)S(1)}, bf16[256,2048]{1,0:T(8,128)(2,1)}, u32[]{:S(2)}) copy-start(bf16[256,2048]{1,0:T(8,128)(2,1)} %refs_1_.7) | copy-start | bytes 3145732
  41.6 3.8 %copy-start.3 = (s32[2]{0:T(128)S(1)}, s32[2]{0:T(128)}, u32[]{:S(2)}) copy-start(s32[2]{0:T(128)} %refs_0_.7) | copy-start | bytes 28
  51.6 1.6 %collective-permute-start.7 = (bf16[256,512]{1,0:T(8,128)(2,1)S(1)}, bf16[256,512]{1,0:T(8,128)(2,1)S(1)}, u32[]{:S(2)}, u32[]{:S(2)}) collective-permute-start(bf16[256,512]{1,0:T(8,128)(2,1)S(1)} %get-tuple-element.32), channel_id=1, source_target_pairs={{0,1},{1,0},{2,3},{3,2},{4,5},{5,4},{6,7},{7,6},{8,9},{9,8},{10,11... | collective-permute-start | bytes 786440 | tf_op jit(solution)/shard_map/ppermute | solution.py:365
  56.8 1.6 %collective-permute-start.8 = (bf16[256,512]{1,0:T(8,128)(2,1)S(1)}, bf16[256,512]{1,0:T(8,128)(2,1)S(1)}, u32[]{:S(2)}, u32[]{:S(2)}) collective-permute-start(bf16[256,512]{1,0:T(8,128)(2,1)S(1)} %get-tuple-element.34), channel_id=1, source_target_pairs={{0,1},{1,0},{2,3},{3,2},{4,5},{5,4},{6,7},{7,6},{8,9},{9,8},{10,11... | collective-permute-start | bytes 786440 | tf_op jit(solution)/shard_map/ppermute | solution.py:365
  63.5 14.4 %collective-permute-start.9 = (bf16[256,1024]{1,0:T(8,128)(2,1)S(1)}, bf16[256,1024]{1,0:T(8,128)(2,1)S(1)}, u32[]{:S(2)}, u32[]{:S(2)}) collective-permute-start(bf16[256,1024]{1,0:T(8,128)(2,1)S(1)} %get-tuple-element.36), channel_id=1, source_target_pairs={{0,1},{1,0},{2,3},{3,2},{4,5},{5,4},{6,7},{7,6},{8,9},{9,8},{10,11... | collective-permute-start | bytes 1572872 | tf_op jit(solution)/shard_map/ppermute | solution.py:365
  63.7 9.2 %collective-permute-start.10 = (bf16[256,512]{1,0:T(8,128)(2,1)S(1)}, bf16[256,512]{1,0:T(8,128)(2,1)S(1)}, u32[]{:S(2)}, u32[]{:S(2)}) collective-permute-start(bf16[256,512]{1,0:T(8,128)(2,1)S(1)} %add_convert_fusion.1.refs_0_), channel_id=1, source_target_pairs={{0,2},{1,3},{2,0},{3,1},{4,6},{5,7},{6,4},{7,5},{8,10},{9,11},{10,... | collective-permute-start | bytes 786440 | tf_op jit(solution)/shard_map/ppermute | solution.py:369
  65.2 12.7 %collective-permute-start.11 = (bf16[256,512]{1,0:T(8,128)(2,1)S(1)}, bf16[256,512]{1,0:T(8,128)(2,1)S(1)}, u32[]{:S(2)}, u32[]{:S(2)}) collective-permute-start(bf16[256,512]{1,0:T(8,128)(2,1)S(1)} %add_convert_fusion.refs_0_), channel_id=1, source_target_pairs={{0,2},{1,3},{2,0},{3,1},{4,6},{5,7},{6,4},{7,5},{8,10},{9,11},{10,... | collective-permute-start | bytes 786440 | tf_op jit(solution)/shard_map/ppermute | solution.py:369

commit v7 on v6

--- a/solution.py
+++ b/solution.py
@@ -104,7 +104,7 @@
     pieces = [
         (k, i, p) for k in range(kv_heads) for i in range(parts) for p in range(heads // pair)
     ]
-    tops, totals = {}, {}
+    olds, tops, totals = {}, {}, {}
 
     def head_cols(k, p, j):
         head = k * heads + p * pair + j
@@ -125,7 +125,8 @@
             part = jnp.max(scores, axis=0, keepdims=True)
             top = part if top is None else jnp.maximum(top, part)
         if not first:
-            top = jnp.maximum(top, old_top[k * parts + i, :, p * span : (p + 1) * span])
+            olds[t] = old_top[k * parts + i, :, p * span : (p + 1) * span]
+            top = jnp.maximum(top, olds[t])
         tops[t] = top
 
     def weigh(t):
@@ -140,7 +141,7 @@
         acc = jnp.dot(flip_ref[k], weight_refs[t % 2][...], preferred_element_type=jnp.float32)
         total = totals[t]
         if not first:
-            factor = jnp.exp2(old_top[c, :, at] - tops[t])
+            factor = jnp.exp2(olds[t] - tops[t])
             total = total + old_total[c, :, at] * factor
             acc = acc + old_acc[c, :, at] * factor
         if last:
@@ -226,6 +227,7 @@
         out_specs=[whole] * len(out_shape),
         out_shape=out_shape,
         scratch_shapes=scratch,
+        input_output_aliases={} if first or last else {2 + len(arrays) + n: n for n in range(3)},
         compiler_params=pltpu.CompilerParams(vmem_limit_bytes=WIDE_LIMIT if last else VMEM_LIMIT),
         cost_estimate=pl.CostEstimate(
             flops=flops, bytes_accessed=4 * pairs, transcendentals=pairs

time: 79.1 us -> 79.4 us (level)
  the two profiles are of different devices: /device:TPU:8 before, /device:TPU:12 now
where the time goes in v7:
time: 79.4 us; the launch traced here: 79.2 us
  waiting for transfers between devices  34.5 us (43%)
  Pallas kernels  28.4 us (36%)
  starting transfers between devices  12 us (15%)
  local copies, waits for them, and re-layouts  3.05 us (4%)
  other arithmetic  1.1 us (1%)
    ppermute x7, waiting for transfers between devices, move(): return lax.ppermute(block, 'ctx', pairs)  19.5 us
    pallas_call x4, Pallas kernels, attend(): pl.pallas_call(functools.partial(attend_kernel, halves, first, last, scal...  18.9 us
    ppermute x2, waiting for transfers between devices, to_group(): return lax.ppermute(x, 'tp', pairs)  12.2 us
    ppermute x7, starting transfers between devices, move(): return lax.ppermute(block, 'ctx', pairs)  9.52 us
    pallas_call x2, Pallas kernels, project(): pl.pallas_call(project_kernel, in_specs=[pl.BlockSpec(memory_space=pltpu....  8.57 us
    ppermute x3, waiting for transfers between devices, to_core(): return lax.ppermute(x, 'tp', pairs)  2.85 us
    ppermute x2, starting transfers between devices, to_group(): return lax.ppermute(x, 'tp', pairs)  2.03 us
    unnamed x8, local copies, waits for them, and re-layouts  1.89 us
  transfers between devices with their start and end apart: 12, of which 7 were waited for; matrix products, arithmetic and copies ran while one was open for 0% of the time, Pallas kernels for 16%

profile of v7, /device:TPU:12, one launch (start us, length us, event | category | flops | bytes accessed | tf_op | source)
XLA Modules:
  0.0 79.2 jit_solution(11861923934032216482)
XLA Ops:
  0.0 0.7 convert_bitcast_fusion
  0.9 1.0 %constant_dynamic-slice_fusion = (bf16[256,128]{1,0:T(8,128)(2,1)S(1)}, bf16[256,128]{1,0:T(8,128)(2,1)S(1)}, bf16[256,128]{1,0:T(8,128)(2,1)S(1)}, bf16[256,128]{1,0:T(8,128)(2,1)S(1)}) fusion(bf16[256,1024]{1,0:T(8,128)(2,1)} %param.7, s32[]{:T(128)S(6)} %select_n.52, s32[]{:T(128)S(6)} %add.80, bf16[256,1024]{1,0:T(8,128)(2,1)} %param.6), kind=kLoop, calls=%fused_computation.10 | loop fusion | bytes 524296 | tf_op jit(solution)/shard_map/slice | solution.py:303
  2.5 2.6 %collective-permute-start.2 = (bf16[272,512]{1,0:T(8,128)(2,1)S(1)}, bf16[272,512]{1,0:T(8,128)(2,1)S(1)}, u32[]{:S(2)}, u32[]{:S(2)}) collective-permute-start(bf16[272,512]{1,0:T(8,128)(2,1)S(1)} %maximum_maximum_fusion.refs_2_), channel_id=1, source_target_pairs={{0,16},{4,20},{8,24},{12,28},{16,0},{20,4},{24,8},{28,12},{1,17},{... | collective-permute-start | bytes 835592 | tf_op jit(solution)/shard_map/ppermute | solution.py:320
  5.5 1.5 %collective-permute-start.6 = (bf16[272,512]{1,0:T(8,128)(2,1)S(1)}, bf16[272,512]{1,0:T(8,128)(2,1)S(1)}, u32[]{:S(2)}, u32[]{:S(2)}) collective-permute-start(bf16[272,512]{1,0:T(8,128)(2,1)S(1)} %maximum_maximum_fusion.refs_2_), channel_id=1, source_target_pairs={{0,4},{4,0},{8,12},{12,8},{16,20},{20,16},{24,28},{28,24},{1,5},{5... | collective-permute-start | bytes 835592 | tf_op jit(solution)/shard_map/ppermute | solution.py:320
  7.0 6.6 %collective-permute-done.4.refs_3_ = bf16[272,512]{1,0:T(8,128)(2,1)S(1)} collective-permute-done((bf16[272,512]{1,0:T(8,128)(2,1)S(1)}, bf16[272,512]{1,0:T(8,128)(2,1)S(1)}, u32[]{:S(2)}, u32[]{:S(2)}) %collective-permute-start.4) | collective-permute-done | bytes 278560 | tf_op jit(solution)/shard_map/ppermute | solution.py:320
  13.6 1.5 %collective-permute-start.5 = (bf16[272,512]{1,0:T(8,128)(2,1)S(1)}, bf16[272,512]{1,0:T(8,128)(2,1)S(1)}, u32[]{:S(2)}, u32[]{:S(2)}) collective-permute-start(bf16[272,512]{1,0:T(8,128)(2,1)S(1)} %collective-permute-done.4.refs_3_), channel_id=1, source_target_pairs={{0,4},{4,0},{8,12},{12,8},{16,20},{20,16},{24,28},{28,24},{1,5},{5... | collective-permute-start | bytes 835592 | tf_op jit(solution)/shard_map/ppermute | solution.py:320
  15.1 8.9 %collective-permute-done.2.refs_2_ = bf16[272,512]{1,0:T(8,128)(2,1)S(1)} collective-permute-done((bf16[272,512]{1,0:T(8,128)(2,1)S(1)}, bf16[272,512]{1,0:T(8,128)(2,1)S(1)}, u32[]{:S(2)}, u32[]{:S(2)}) %collective-permute-start.2) | collective-permute-done | bytes 278560 | tf_op jit(solution)/shard_map/ppermute | solution.py:320
  24.1 1.5 %collective-permute-start.3 = (bf16[272,512]{1,0:T(8,128)(2,1)S(1)}, bf16[272,512]{1,0:T(8,128)(2,1)S(1)}, u32[]{:S(2)}, u32[]{:S(2)}) collective-permute-start(bf16[272,512]{1,0:T(8,128)(2,1)S(1)} %collective-permute-done.2.refs_2_), channel_id=1, source_target_pairs={{0,4},{4,0},{8,12},{12,8},{16,20},{20,16},{24,28},{28,24},{1,5},{5... | collective-permute-start | bytes 835592 | tf_op jit(solution)/shard_map/ppermute | solution.py:320
  25.6 3.9 %collective-permute-done.refs_2_ = bf16[272,512]{1,0:T(8,128)(2,1)S(1)} collective-permute-done((bf16[272,512]{1,0:T(8,128)(2,1)S(1)}, bf16[272,512]{1,0:T(8,128)(2,1)S(1)}, u32[]{:S(2)}, u32[]{:S(2)}) %collective-permute-start) | collective-permute-done | bytes 278560 | tf_op jit(solution)/shard_map/ppermute | solution.py:320
  29.6 1.5 %collective-permute-start.1 = (bf16[272,512]{1,0:T(8,128)(2,1)S(1)}, bf16[272,512]{1,0:T(8,128)(2,1)S(1)}, u32[]{:S(2)}, u32[]{:S(2)}) collective-permute-start(bf16[272,512]{1,0:T(8,128)(2,1)S(1)} %collective-permute-done.refs_2_), channel_id=1, source_target_pairs={{0,4},{4,0},{8,12},{12,8},{16,20},{20,16},{24,28},{28,24},{1,5},{5... | collective-permute-start | bytes 835592 | tf_op jit(solution)/shard_map/ppermute | solution.py:320
  31.1 1.2 %copy-done = bf16[256,2048]{1,0:T(8,128)(2,1)S(1)} copy-done((bf16[256,2048]{1,0:T(8,128)(2,1)S(1)}, bf16[256,2048]{1,0:T(8,128)(2,1)}, u32[]{:S(2)}) %copy-start) | copy-done | bytes 1048600
  32.3 0.7 copy-done.2
  32.9 4.9 %shard_map.55 = (f32[4,1,1024]{2,1,0:T(1,128)S(1)}, f32[4,1,1024]{2,1,0:T(1,128)S(1)}, f32[4,128,1024]{2,1,0:T(8,128)S(1)}) custom-call(s32[2]{0:T(128)S(1)} %copy-done.2, bf16[256,2048]{1,0:T(8,128)(2,1)S(1)} %copy-done, bf16[272,512]{1,0:T(8,128)(2,1)S(1)} %maximum_maximum_fusion.refs_2_, bf16[272,512]{1,0:T(8,128)(2,1)S(1)} %collective-permute-done.4.refs_3_, ...), custom_call_target="tpu_custom_call" | custom-call | flops 1610612736 | bytes 12582912 | tf_op jit(solution)/shard_map/pallas_call | solution.py:224
  37.9 3.8 %shard_map.56 = (f32[4,1,1024]{2,1,0:T(1,128)S(1)}, f32[4,1,1024]{2,1,0:T(1,128)S(1)}, f32[4,128,1024]{2,1,0:T(8,128)S(1)}) custom-call(s32[2]{0:T(128)S(1)} %copy-done.2, bf16[256,2048]{1,0:T(8,128)(2,1)S(1)} %copy-done, bf16[272,512]{1,0:T(8,128)(2,1)S(1)} %collective-permute-done.2.refs_2_, ...), custom_call_target="tpu_custom_call", output_to_operand_aliasing={{0}: (4, {}), {1}: (5, {}), {2}: (6, {})} | custom-call | flops 1073741824 | bytes 8388608 | tf_op jit(solution)/shard_map/pallas_call | solution.py:224
  41.7 3.9 %shard_map.57 = (f32[4,1,1024]{2,1,0:T(1,128)S(1)}, f32[4,1,1024]{2,1,0:T(1,128)S(1)}, f32[4,128,1024]{2,1,0:T(8,128)S(1)}) custom-call(s32[2]{0:T(128)S(1)} %copy-done.2, bf16[256,2048]{1,0:T(8,128)(2,1)S(1)} %copy-done, bf16[272,512]{1,0:T(8,128)(2,1)S(1)} %collective-permute-done.refs_2_, ...), custom_call_target="tpu_custom_call", output_to_operand_aliasing={{0}: (4, {}), {1}: (5, {}), {2}: (6, {})} | custom-call | flops 1073741824 | bytes 8388608 | tf_op jit(solution)/shard_map/pallas_call | solution.py:224
  45.7 6.2 %shard_map.58 = (bf16[256,2048]{1,0:T(8,128)(2,1)S(1)}, bf16[256,512]{1,0:T(8,128)(2,1)S(1)}, f32[256,512]{1,0:T(8,128)S(1)}) custom-call(s32[2]{0:T(128)S(1)} %copy-done.3, bf16[256,2048]{1,0:T(8,128)(2,1)S(1)} %copy-done.1, bf16[272,512]{1,0:T(8,128)(2,1)S(1)} %collective-permute-done.1.refs_2_, f32[4,1,1024]{2,1,0:T(1,128)S(1)} %get-tuple-element.27.refs_3_, ...), custom_call_target="tpu_custom_call" | custom-call | flops 1610612736 | bytes 4194304 | tf_op jit(solution)/shard_map/pallas_call | solution.py:224
  52.0 1.5 %collective-permute-done.7 = bf16[256,512]{1,0:T(8,128)(2,1)S(1)} collective-permute-done((bf16[256,512]{1,0:T(8,128)(2,1)S(1)}, bf16[256,512]{1,0:T(8,128)(2,1)S(1)}, u32[]{:S(2)}, u32[]{:S(2)}) %collective-permute-start.7) | collective-permute-done | bytes 262176 | tf_op jit(solution)/shard_map/ppermute | solution.py:367
  53.6 3.6 %shard_map.59 = (bf16[256,512]{1,0:T(8,128)(2,1)S(1)}, f32[256,512]{1,0:T(8,128)S(1)}) custom-call(s32[2]{0:T(128)S(1)} %get-tuple-element.37.at_ref, bf16[256,2048]{1,0:T(8,128)(2,1)S(1)} %get-tuple-element.30.rows_ref, bf16[2048,4096]{1,0:T(8,128)(2,1)} %weight_ref.3, bf16[256,512]{1,0:T(8,128)(2,1)S(1)} %add_convert_fusion.1.refs_0_), custom_call_target="tpu_custom_call" | custom-call | flops 1073741824 | bytes 4194304 | tf_op jit(solution)/shard_map/pallas_call | solution.py:249
  57.4 1.3 %collective-permute-done.8 = bf16[256,512]{1,0:T(8,128)(2,1)S(1)} collective-permute-done((bf16[256,512]{1,0:T(8,128)(2,1)S(1)}, bf16[256,512]{1,0:T(8,128)(2,1)S(1)}, u32[]{:S(2)}, u32[]{:S(2)}) %collective-permute-start.8) | collective-permute-done | bytes 262176 | tf_op jit(solution)/shard_map/ppermute | solution.py:367
  58.8 5.0 %shard_map.60 = (bf16[256,1024]{1,0:T(8,128)(2,1)S(1)}, f32[256,1024]{1,0:T(8,128)S(1)}) custom-call(s32[2]{0:T(128)S(1)} %add_multiply_fusion.at_ref, bf16[256,2048]{1,0:T(8,128)(2,1)S(1)} %get-tuple-element.30.rows_ref, bf16[2048,4096]{1,0:T(8,128)(2,1)} %weight_ref.3, bf16[256,512]{1,0:T(8,128)(2,1)S(1)} %add_convert_fusion.refs_0_), custom_call_target="tpu_custom_call" | custom-call | flops 2147483648 | bytes 8388608 | tf_op jit(solution)/shard_map/pallas_call | solution.py:249
  64.6 1.5 %collective-permute-start.11 = (bf16[256,512]{1,0:T(8,128)(2,1)S(1)}, bf16[256,512]{1,0:T(8,128)(2,1)S(1)}, u32[]{:S(2)}, u32[]{:S(2)}) collective-permute-start(bf16[256,512]{1,0:T(8,128)(2,1)S(1)} %add_convert_fusion.refs_0_), channel_id=1, source_target_pairs={{0,2},{1,3},{2,0},{3,1},{4,6},{5,7},{6,4},{7,5},{8,10},{9,11},{10,... | collective-permute-start | bytes 786440 | tf_op jit(solution)/shard_map/ppermute | solution.py:371
  66.1 7.1 %collective-permute-done.10.refs_1_ = bf16[256,512]{1,0:T(8,128)(2,1)S(1)} collective-permute-done((bf16[256,512]{1,0:T(8,128)(2,1)S(1)}, bf16[256,512]{1,0:T(8,128)(2,1)S(1)}, u32[]{:S(2)}, u32[]{:S(2)}) %collective-permute-start.10) | collective-permute-done | bytes 262176 | tf_op jit(solution)/shard_map/ppermute | solution.py:371
  73.2 5.0 %collective-permute-done.11.refs_2_ = bf16[256,512]{1,0:T(8,128)(2,1)S(1)} collective-permute-done((bf16[256,512]{1,0:T(8,128)(2,1)S(1)}, bf16[256,512]{1,0:T(8,128)(2,1)S(1)}, u32[]{:S(2)}, u32[]{:S(2)}) %collective-permute-start.11) | collective-permute-done | bytes 262176 | tf_op jit(solution)/shard_map/ppermute | solution.py:371
  78.3 0.9 %shard_map.61 = bf16[256,1024]{1,0:T(8,128)(2,1)} custom-call(f32[256,1024]{1,0:T(8,128)S(1)} %get-tuple-element.35.mine_ref, bf16[256,1024]{1,0:T(8,128)(2,1)S(1)} %collective-permute-done.9.refs_0_, bf16[256,512]{1,0:T(8,128)(2,1)S(1)} %collective-permute-done.10.refs_1_, bf16[256,512]{1,0:T(8,128)(2,1)S(1)} %collective-permute-done.11.refs_2_), custom_call_target="tpu_custom_call" | custom-call | flops 1048576 | bytes 2621440 | tf_op jit(solution)/shard_map/pallas_call | solution.py:280
  (26 shorter events, 2.6 us)
Async XLA Ops:
  2.0 11.7 %collective-permute-start.4 = (bf16[272,512]{1,0:T(8,128)(2,1)S(1)}, bf16[272,512]{1,0:T(8,128)(2,1)S(1)}, u32[]{:S(2)}, u32[]{:S(2)}) collective-permute-start(bf16[272,512]{1,0:T(8,128)(2,1)S(1)} %maximum_maximum_fusion.refs_2_), channel_id=1, source_target_pairs={{0,8},{4,12},{8,0},{12,4},{16,24},{20,28},{24,16},{28,20},{1,9},{5... | collective-permute-start | bytes 835592 | tf_op jit(solution)/shard_map/ppermute | solution.py:320
  2.5 21.6 %collective-permute-start.2 = (bf16[272,512]{1,0:T(8,128)(2,1)S(1)}, bf16[272,512]{1,0:T(8,128)(2,1)S(1)}, u32[]{:S(2)}, u32[]{:S(2)}) collective-permute-start(bf16[272,512]{1,0:T(8,128)(2,1)S(1)} %maximum_maximum_fusion.refs_2_), channel_id=1, source_target_pairs={{0,16},{4,20},{8,24},{12,28},{16,0},{20,4},{24,8},{28,12},{1,17},{... | collective-permute-start | bytes 835592 | tf_op jit(solution)/shard_map/ppermute | solution.py:320
  5.1 24.5 %collective-permute-start = (bf16[272,512]{1,0:T(8,128)(2,1)S(1)}, bf16[272,512]{1,0:T(8,128)(2,1)S(1)}, u32[]{:S(2)}, u32[]{:S(2)}) collective-permute-start(bf16[272,512]{1,0:T(8,128)(2,1)S(1)} %maximum_maximum_fusion.refs_2_), channel_id=1, source_target_pairs={{0,24},{4,28},{8,16},{12,20},{16,8},{20,12},{24,0},{28,4},{1,25},{... | collective-permute-start | bytes 835592 | tf_op jit(solution)/shard_map/ppermute | solution.py:320
  5.5 25.5 %collective-permute-start.6 = (bf16[272,512]{1,0:T(8,128)(2,1)S(1)}, bf16[272,512]{1,0:T(8,128)(2,1)S(1)}, u32[]{:S(2)}, u32[]{:S(2)}) collective-permute-start(bf16[272,512]{1,0:T(8,128)(2,1)S(1)} %maximum_maximum_fusion.refs_2_), channel_id=1, source_target_pairs={{0,4},{4,0},{8,12},{12,8},{16,20},{20,16},{24,28},{28,24},{1,5},{5... | collective-permute-start | bytes 835592 | tf_op jit(solution)/shard_map/ppermute | solution.py:320
  13.6 24.2 %collective-permute-start.5 = (bf16[272,512]{1,0:T(8,128)(2,1)S(1)}, bf16[272,512]{1,0:T(8,128)(2,1)S(1)}, u32[]{:S(2)}, u32[]{:S(2)}) collective-permute-start(bf16[272,512]{1,0:T(8,128)(2,1)S(1)} %collective-permute-done.4.refs_3_), channel_id=1, source_target_pairs={{0,4},{4,0},{8,12},{12,8},{16,20},{20,16},{24,28},{28,24},{1,5},{5... | collective-permute-start | bytes 835592 | tf_op jit(solution)/shard_map/ppermute | solution.py:320
  24.1 17.7 %collective-permute-start.3 = (bf16[272,512]{1,0:T(8,128)(2,1)S(1)}, bf16[272,512]{1,0:T(8,128)(2,1)S(1)}, u32[]{:S(2)}, u32[]{:S(2)}) collective-permute-start(bf16[272,512]{1,0:T(8,128)(2,1)S(1)} %collective-permute-done.2.refs_2_), channel_id=1, source_target_pairs={{0,4},{4,0},{8,12},{12,8},{16,20},{20,16},{24,28},{28,24},{1,5},{5... | collective-permute-start | bytes 835592 | tf_op jit(solution)/shard_map/ppermute | solution.py:320
  29.6 16.1 %collective-permute-start.1 = (bf16[272,512]{1,0:T(8,128)(2,1)S(1)}, bf16[272,512]{1,0:T(8,128)(2,1)S(1)}, u32[]{:S(2)}, u32[]{:S(2)}) collective-permute-start(bf16[272,512]{1,0:T(8,128)(2,1)S(1)} %collective-permute-done.refs_2_), channel_id=1, source_target_pairs={{0,4},{4,0},{8,12},{12,8},{16,20},{20,16},{24,28},{28,24},{1,5},{5... | collective-permute-start | bytes 835592 | tf_op jit(solution)/shard_map/ppermute | solution.py:320
  31.1 1.2 %copy-start = (bf16[256,2048]{1,0:T(8,128)(2,1)S(1)}, bf16[256,2048]{1,0:T(8,128)(2,1)}, u32[]{:S(2)}) copy-start(bf16[256,2048]{1,0:T(8,128)(2,1)} %refs_1_.7) | copy-start | bytes 3145732
  32.3 0.7 copy-start.2
  41.7 3.9 %copy-start.1 = (bf16[256,2048]{1,0:T(8,128)(2,1)S(1)}, bf16[256,2048]{1,0:T(8,128)(2,1)}, u32[]{:S(2)}) copy-start(bf16[256,2048]{1,0:T(8,128)(2,1)} %refs_1_.7) | copy-start | bytes 3145732
  41.7 3.9 %copy-start.3 = (s32[2]{0:T(128)S(1)}, s32[2]{0:T(128)}, u32[]{:S(2)}) copy-start(s32[2]{0:T(128)} %refs_0_.7) | copy-start | bytes 28
  51.9 1.6 %collective-permute-start.7 = (bf16[256,512]{1,0:T(8,128)(2,1)S(1)}, bf16[256,512]{1,0:T(8,128)(2,1)S(1)}, u32[]{:S(2)}, u32[]{:S(2)}) collective-permute-start(bf16[256,512]{1,0:T(8,128)(2,1)S(1)} %get-tuple-element.32), channel_id=1, source_target_pairs={{0,1},{1,0},{2,3},{3,2},{4,5},{5,4},{6,7},{7,6},{8,9},{9,8},{10,11... | collective-permute-start | bytes 786440 | tf_op jit(solution)/shard_map/ppermute | solution.py:367
  57.2 1.6 %collective-permute-start.8 = (bf16[256,512]{1,0:T(8,128)(2,1)S(1)}, bf16[256,512]{1,0:T(8,128)(2,1)S(1)}, u32[]{:S(2)}, u32[]{:S(2)}) collective-permute-start(bf16[256,512]{1,0:T(8,128)(2,1)S(1)} %get-tuple-element.34), channel_id=1, source_target_pairs={{0,1},{1,0},{2,3},{3,2},{4,5},{5,4},{6,7},{7,6},{8,9},{9,8},{10,11... | collective-permute-start | bytes 786440 | tf_op jit(solution)/shard_map/ppermute | solution.py:367
  63.9 14.4 %collective-permute-start.9 = (bf16[256,1024]{1,0:T(8,128)(2,1)S(1)}, bf16[256,1024]{1,0:T(8,128)(2,1)S(1)}, u32[]{:S(2)}, u32[]{:S(2)}) collective-permute-start(bf16[256,1024]{1,0:T(8,128)(2,1)S(1)} %get-tuple-element.36), channel_id=1, source_target_pairs={{0,1},{1,0},{2,3},{3,2},{4,5},{5,4},{6,7},{7,6},{8,9},{9,8},{10,11... | collective-permute-start | bytes 1572872 | tf_op jit(solution)/shard_map/ppermute | solution.py:367
  64.1 9.2 %collective-permute-start.10 = (bf16[256,512]{1,0:T(8,128)(2,1)S(1)}, bf16[256,512]{1,0:T(8,128)(2,1)S(1)}, u32[]{:S(2)}, u32[]{:S(2)}) collective-permute-start(bf16[256,512]{1,0:T(8,128)(2,1)S(1)} %add_convert_fusion.1.refs_0_), channel_id=1, source_target_pairs={{0,2},{1,3},{2,0},{3,1},{4,6},{5,7},{6,4},{7,5},{8,10},{9,11},{10,... | collective-permute-start | bytes 786440 | tf_op jit(solution)/shard_map/ppermute | solution.py:371
  64.6 13.7 %collective-permute-start.11 = (bf16[256,512]{1,0:T(8,128)(2,1)S(1)}, bf16[256,512]{1,0:T(8,128)(2,1)S(1)}, u32[]{:S(2)}, u32[]{:S(2)}) collective-permute-start(bf16[256,512]{1,0:T(8,128)(2,1)S(1)} %add_convert_fusion.refs_0_), channel_id=1, source_target_pairs={{0,2},{1,3},{2,0},{3,1},{4,6},{5,7},{6,4},{7,5},{8,10},{9,11},{10,... | collective-permute-start | bytes 786440 | tf_op jit(solution)/shard_map/ppermute | solution.py:371

commit v8 on v7

--- a/solution.py
+++ b/solution.py
@@ -333,9 +333,11 @@
         near = move(own, lambda o, i: (o ^ 1, i))
         opposite = move(own, lambda o, i: (o ^ 2, i))
         mirror = move(own, lambda o, i: (o ^ 3, i))
-        stages = [[(own,), (near,)] + [(x,) for x in cross(own)]]
-        stages.append([(opposite,)] + [(x,) for x in cross(near)])
-        stages.append([(mirror,)] + [(x,) for x in cross(opposite)])
+        own_crossed = [(x,) for x in cross(own)]
+        near_crossed = [(x,) for x in cross(near)]
+        opposite_crossed = [(x,) for x in cross(opposite)]
+        stages = [[(own,)], [(near,)] + own_crossed + [(opposite,)]]
+        stages.append(near_crossed + [(mirror,)] + opposite_crossed)
         stages += [[(x,)] for x in cross(mirror)]
     else:
         blocks = [own]

time: 79.4 us -> 80.1 us (level)
  the two profiles are of different devices: /device:TPU:12 before, /device:TPU:0 now
where the time goes in v8:
time: 80.1 us; the launch traced here: 79.8 us
  waiting for transfers between devices  31.5 us (39%)
  Pallas kernels  30.2 us (38%)
  starting transfers between devices  13.6 us (17%)
  local copies, waits for them, and re-layouts  3.05 us (4%)
  other arithmetic  1.18 us (1%)
    pallas_call x4, Pallas kernels, attend(): pl.pallas_call(functools.partial(attend_kernel, halves, first, last, scal...  20.7 us
    ppermute x7, waiting for transfers between devices, move(): return lax.ppermute(block, 'ctx', pairs)  16.5 us
    ppermute x2, waiting for transfers between devices, to_group(): return lax.ppermute(x, 'tp', pairs)  12.2 us
    ppermute x7, starting transfers between devices, move(): return lax.ppermute(block, 'ctx', pairs)  11.1 us
    pallas_call x2, Pallas kernels, project(): pl.pallas_call(project_kernel, in_specs=[pl.BlockSpec(memory_space=pltpu....  8.57 us
    ppermute x3, waiting for transfers between devices, to_core(): return lax.ppermute(x, 'tp', pairs)  2.85 us
    ppermute x2, starting transfers between devices, to_group(): return lax.ppermute(x, 'tp', pairs)  2.03 us
    unnamed x10, local copies, waits for them, and re-layouts  1.89 us
  transfers between devices with their start and end apart: 12, of which 6 were waited for; matrix products, arithmetic and copies ran while one was open for 0% of the time, Pallas kernels for 18%

profile of v8, /device:TPU:0, one launch (start us, length us, event | category | flops | bytes accessed | tf_op | source)
XLA Modules:
  0.0 79.8 jit_solution(15394177616440363080)
XLA Ops:
  0.0 0.8 convert_bitcast_fusion
  1.0 1.0 %constant_dynamic-slice_fusion = (bf16[256,128]{1,0:T(8,128)(2,1)S(1)}, bf16[256,128]{1,0:T(8,128)(2,1)S(1)}, bf16[256,128]{1,0:T(8,128)(2,1)S(1)}, bf16[256,128]{1,0:T(8,128)(2,1)S(1)}) fusion(bf16[256,1024]{1,0:T(8,128)(2,1)} %param.7, s32[]{:T(128)S(6)} %select_n.52, s32[]{:T(128)S(6)} %add.80, bf16[256,1024]{1,0:T(8,128)(2,1)} %param.6), kind=kLoop, calls=%fused_computation.10 | loop fusion | bytes 524296 | tf_op jit(solution)/shard_map/slice | solution.py:303
  2.1 3.1 %collective-permute-start.2 = (bf16[272,512]{1,0:T(8,128)(2,1)S(1)}, bf16[272,512]{1,0:T(8,128)(2,1)}, u32[]{:S(2)}, u32[]{:S(2)}) collective-permute-start(bf16[272,512]{1,0:T(8,128)(2,1)S(1)} %maximum_maximum_fusion.refs_2_), channel_id=1, source_target_pairs={{0,8},{4,12},{8,0},{12,4},{16,24},{20,28},{24,16},{28,20},{1,9},{5... | collective-permute-start | bytes 835592 | tf_op jit(solution)/shard_map/ppermute | solution.py:320
  5.2 2.6 %collective-permute-start.4 = (bf16[272,512]{1,0:T(8,128)(2,1)S(1)}, bf16[272,512]{1,0:T(8,128)(2,1)}, u32[]{:S(2)}, u32[]{:S(2)}) collective-permute-start(bf16[272,512]{1,0:T(8,128)(2,1)S(1)} %maximum_maximum_fusion.refs_2_), channel_id=1, source_target_pairs={{0,16},{4,20},{8,24},{12,28},{16,0},{20,4},{24,8},{28,12},{1,17},{... | collective-permute-start | bytes 835592 | tf_op jit(solution)/shard_map/ppermute | solution.py:320
  7.8 1.7 %collective-permute-start.6 = (bf16[272,512]{1,0:T(8,128)(2,1)S(1)}, bf16[272,512]{1,0:T(8,128)(2,1)}, u32[]{:S(2)}, u32[]{:S(2)}) collective-permute-start(bf16[272,512]{1,0:T(8,128)(2,1)S(1)} %maximum_maximum_fusion.refs_2_), channel_id=1, source_target_pairs={{0,4},{4,0},{8,12},{12,8},{16,20},{20,16},{24,28},{28,24},{1,5},{5... | collective-permute-start | bytes 835592 | tf_op jit(solution)/shard_map/ppermute | solution.py:320
  9.5 7.7 %collective-permute-done.2.refs_2_ = bf16[272,512]{1,0:T(8,128)(2,1)} collective-permute-done((bf16[272,512]{1,0:T(8,128)(2,1)S(1)}, bf16[272,512]{1,0:T(8,128)(2,1)}, u32[]{:S(2)}, u32[]{:S(2)}) %collective-permute-start.2) | collective-permute-done | bytes 278560 | tf_op jit(solution)/shard_map/ppermute | solution.py:320
  17.2 1.7 %collective-permute-start.3 = (bf16[272,512]{1,0:T(8,128)(2,1)}, bf16[272,512]{1,0:T(8,128)(2,1)}, u32[]{:S(2)}, u32[]{:S(2)}) collective-permute-start(bf16[272,512]{1,0:T(8,128)(2,1)} %collective-permute-done.2.refs_2_), channel_id=1, source_target_pairs={{0,4},{4,0},{8,12},{12,8},{16,20},{20,16},{24,28},{28,24},{1,5},{5... | collective-permute-start | bytes 835592 | tf_op jit(solution)/shard_map/ppermute | solution.py:320
  18.8 8.8 %collective-permute-done.4.refs_4_ = bf16[272,512]{1,0:T(8,128)(2,1)} collective-permute-done((bf16[272,512]{1,0:T(8,128)(2,1)S(1)}, bf16[272,512]{1,0:T(8,128)(2,1)}, u32[]{:S(2)}, u32[]{:S(2)}) %collective-permute-start.4) | collective-permute-done | bytes 278560 | tf_op jit(solution)/shard_map/ppermute | solution.py:320
  27.7 1.5 %collective-permute-start.5 = (bf16[272,512]{1,0:T(8,128)(2,1)}, bf16[272,512]{1,0:T(8,128)(2,1)}, u32[]{:S(2)}, u32[]{:S(2)}) collective-permute-start(bf16[272,512]{1,0:T(8,128)(2,1)} %collective-permute-done.4.refs_4_), channel_id=1, source_target_pairs={{0,4},{4,0},{8,12},{12,8},{16,20},{20,16},{24,28},{28,24},{1,5},{5... | collective-permute-start | bytes 835592 | tf_op jit(solution)/shard_map/ppermute | solution.py:320
  29.1 1.2 %copy-done = bf16[256,2048]{1,0:T(8,128)(2,1)S(1)} copy-done((bf16[256,2048]{1,0:T(8,128)(2,1)S(1)}, bf16[256,2048]{1,0:T(8,128)(2,1)}, u32[]{:S(2)}) %copy-start) | copy-done | bytes 1048600
  30.4 0.7 copy-done.3
  31.0 2.6 %shard_map.55 = (f32[4,1,1024]{2,1,0:T(1,128)S(1)}, f32[4,1,1024]{2,1,0:T(1,128)S(1)}, f32[4,128,1024]{2,1,0:T(8,128)S(1)}) custom-call(s32[2]{0:T(128)S(1)} %copy-done.3, bf16[256,2048]{1,0:T(8,128)(2,1)S(1)} %copy-done, bf16[272,512]{1,0:T(8,128)(2,1)S(1)} %maximum_maximum_fusion.refs_2_), custom_call_target="tpu_custom_call" | custom-call | flops 536870912 | bytes 4194304 | tf_op jit(solution)/shard_map/pallas_call | solution.py:224
  33.8 0.5 collective-permute-start.1
  34.4 5.9 %shard_map.56 = (f32[4,1,1024]{2,1,0:T(1,128)S(1)}, f32[4,1,1024]{2,1,0:T(1,128)S(1)}, f32[4,128,1024]{2,1,0:T(8,128)S(1)}) custom-call(s32[2]{0:T(128)S(1)} %copy-done.4, bf16[256,2048]{1,0:T(8,128)(2,1)S(1)} %copy-done.1, bf16[272,512]{1,0:T(8,128)(2,1)} %collective-permute-done.2.refs_2_, ...), custom_call_target="tpu_custom_call", output_to_operand_aliasing={{0}: (5, {}), {1}: (6, {}), {2}: (7, {})} | custom-call | flops 1610612736 | bytes 12582912 | tf_op jit(solution)/shard_map/pallas_call | solution.py:224
  40.3 6.0 %shard_map.57 = (f32[4,1,1024]{2,1,0:T(1,128)S(1)}, f32[4,1,1024]{2,1,0:T(1,128)S(1)}, f32[4,128,1024]{2,1,0:T(8,128)S(1)}) custom-call(s32[2]{0:T(128)S(1)} %copy-done.4, bf16[256,2048]{1,0:T(8,128)(2,1)S(1)} %copy-done.1, bf16[272,512]{1,0:T(8,128)(2,1)} %collective-permute-done.3.refs_2_, ...), custom_call_target="tpu_custom_call", output_to_operand_aliasing={{0}: (5, {}), {1}: (6, {}), {2}: (7, {})} | custom-call | flops 1610612736 | bytes 12582912 | tf_op jit(solution)/shard_map/pallas_call | solution.py:224
  46.3 6.2 %shard_map.58 = (bf16[256,2048]{1,0:T(8,128)(2,1)S(1)}, bf16[256,512]{1,0:T(8,128)(2,1)S(1)}, f32[256,512]{1,0:T(8,128)S(1)}) custom-call(s32[2]{0:T(128)S(1)} %copy-done.4, bf16[256,2048]{1,0:T(8,128)(2,1)S(1)} %copy-done.2, bf16[272,512]{1,0:T(8,128)(2,1)S(1)} %collective-permute-done.1.refs_2_, f32[4,1,1024]{2,1,0:T(1,128)S(1)} %get-tuple-element.27.refs_3_, ...), custom_call_target="tpu_custom_call" | custom-call | flops 1610612736 | bytes 4194304 | tf_op jit(solution)/shard_map/pallas_call | solution.py:224
  52.6 1.5 %collective-permute-done.7 = bf16[256,512]{1,0:T(8,128)(2,1)S(1)} collective-permute-done((bf16[256,512]{1,0:T(8,128)(2,1)S(1)}, bf16[256,512]{1,0:T(8,128)(2,1)S(1)}, u32[]{:S(2)}, u32[]{:S(2)}) %collective-permute-start.7) | collective-permute-done | bytes 262176 | tf_op jit(solution)/shard_map/ppermute | solution.py:369
  54.2 3.6 %shard_map.59 = (bf16[256,512]{1,0:T(8,128)(2,1)S(1)}, f32[256,512]{1,0:T(8,128)S(1)}) custom-call(s32[2]{0:T(128)S(1)} %get-tuple-element.37.at_ref, bf16[256,2048]{1,0:T(8,128)(2,1)S(1)} %get-tuple-element.30.rows_ref, bf16[2048,4096]{1,0:T(8,128)(2,1)} %weight_ref.3, bf16[256,512]{1,0:T(8,128)(2,1)S(1)} %add_convert_fusion.1.refs_0_), custom_call_target="tpu_custom_call" | custom-call | flops 1073741824 | bytes 4194304 | tf_op jit(solution)/shard_map/pallas_call | solution.py:249
  58.0 1.3 %collective-permute-done.8 = bf16[256,512]{1,0:T(8,128)(2,1)S(1)} collective-permute-done((bf16[256,512]{1,0:T(8,128)(2,1)S(1)}, bf16[256,512]{1,0:T(8,128)(2,1)S(1)}, u32[]{:S(2)}, u32[]{:S(2)}) %collective-permute-start.8) | collective-permute-done | bytes 262176 | tf_op jit(solution)/shard_map/ppermute | solution.py:369
  59.4 5.0 %shard_map.60 = (bf16[256,1024]{1,0:T(8,128)(2,1)S(1)}, f32[256,1024]{1,0:T(8,128)S(1)}) custom-call(s32[2]{0:T(128)S(1)} %add_multiply_fusion.at_ref, bf16[256,2048]{1,0:T(8,128)(2,1)S(1)} %get-tuple-element.30.rows_ref, bf16[2048,4096]{1,0:T(8,128)(2,1)} %weight_ref.3, bf16[256,512]{1,0:T(8,128)(2,1)S(1)} %add_convert_fusion.refs_0_), custom_call_target="tpu_custom_call" | custom-call | flops 2147483648 | bytes 8388608 | tf_op jit(solution)/shard_map/pallas_call | solution.py:249
  64.6 1.5 %collective-permute-start.10 = (bf16[256,512]{1,0:T(8,128)(2,1)S(1)}, bf16[256,512]{1,0:T(8,128)(2,1)S(1)}, u32[]{:S(2)}, u32[]{:S(2)}) collective-permute-start(bf16[256,512]{1,0:T(8,128)(2,1)S(1)} %add_convert_fusion.1.refs_0_), channel_id=1, source_target_pairs={{0,2},{1,3},{2,0},{3,1},{4,6},{5,7},{6,4},{7,5},{8,10},{9,11},{10,... | collective-permute-start | bytes 786440 | tf_op jit(solution)/shard_map/ppermute | solution.py:373
  66.7 7.1 %collective-permute-done.10.refs_1_ = bf16[256,512]{1,0:T(8,128)(2,1)S(1)} collective-permute-done((bf16[256,512]{1,0:T(8,128)(2,1)S(1)}, bf16[256,512]{1,0:T(8,128)(2,1)S(1)}, u32[]{:S(2)}, u32[]{:S(2)}) %collective-permute-start.10) | collective-permute-done | bytes 262176 | tf_op jit(solution)/shard_map/ppermute | solution.py:373
  73.8 5.0 %collective-permute-done.11.refs_2_ = bf16[256,512]{1,0:T(8,128)(2,1)S(1)} collective-permute-done((bf16[256,512]{1,0:T(8,128)(2,1)S(1)}, bf16[256,512]{1,0:T(8,128)(2,1)S(1)}, u32[]{:S(2)}, u32[]{:S(2)}) %collective-permute-start.11) | collective-permute-done | bytes 262176 | tf_op jit(solution)/shard_map/ppermute | solution.py:373
  78.9 0.9 %shard_map.61 = bf16[256,1024]{1,0:T(8,128)(2,1)} custom-call(f32[256,1024]{1,0:T(8,128)S(1)} %get-tuple-element.35.mine_ref, bf16[256,1024]{1,0:T(8,128)(2,1)S(1)} %collective-permute-done.9.refs_0_, bf16[256,512]{1,0:T(8,128)(2,1)S(1)} %collective-permute-done.10.refs_1_, bf16[256,512]{1,0:T(8,128)(2,1)S(1)} %collective-permute-done.11.refs_2_), custom_call_target="tpu_custom_call" | custom-call | flops 1048576 | bytes 2621440 | tf_op jit(solution)/shard_map/pallas_call | solution.py:280
  (28 shorter events, 1.6 us)
Async XLA Ops:
  0.0 34.3 %copy-start.4 = (s32[2]{0:T(128)S(1)}, s32[2]{0:T(128)}, u32[]{:S(2)}) copy-start(s32[2]{0:T(128)} %refs_0_.7) | copy-start | bytes 28
  0.0 34.3 %copy-start.1 = (bf16[256,2048]{1,0:T(8,128)(2,1)S(1)}, bf16[256,2048]{1,0:T(8,128)(2,1)}, u32[]{:S(2)}) copy-start(bf16[256,2048]{1,0:T(8,128)(2,1)} %refs_1_.7) | copy-start | bytes 3145732
  2.1 15.1 %collective-permute-start.2 = (bf16[272,512]{1,0:T(8,128)(2,1)S(1)}, bf16[272,512]{1,0:T(8,128)(2,1)}, u32[]{:S(2)}, u32[]{:S(2)}) collective-permute-start(bf16[272,512]{1,0:T(8,128)(2,1)S(1)} %maximum_maximum_fusion.refs_2_), channel_id=1, source_target_pairs={{0,8},{4,12},{8,0},{12,4},{16,24},{20,28},{24,16},{28,20},{1,9},{5... | collective-permute-start | bytes 835592 | tf_op jit(solution)/shard_map/ppermute | solution.py:320
  5.2 22.5 %collective-permute-start.4 = (bf16[272,512]{1,0:T(8,128)(2,1)S(1)}, bf16[272,512]{1,0:T(8,128)(2,1)}, u32[]{:S(2)}, u32[]{:S(2)}) collective-permute-start(bf16[272,512]{1,0:T(8,128)(2,1)S(1)} %maximum_maximum_fusion.refs_2_), channel_id=1, source_target_pairs={{0,16},{4,20},{8,24},{12,28},{16,0},{20,4},{24,8},{28,12},{1,17},{... | collective-permute-start | bytes 835592 | tf_op jit(solution)/shard_map/ppermute | solution.py:320
  7.8 26.0 %collective-permute-start = (bf16[272,512]{1,0:T(8,128)(2,1)S(1)}, bf16[272,512]{1,0:T(8,128)(2,1)}, u32[]{:S(2)}, u32[]{:S(2)}) collective-permute-start(bf16[272,512]{1,0:T(8,128)(2,1)S(1)} %maximum_maximum_fusion.refs_2_), channel_id=1, source_target_pairs={{0,24},{4,28},{8,16},{12,20},{16,8},{20,12},{24,0},{28,4},{1,25},{... | collective-permute-start | bytes 835592 | tf_op jit(solution)/shard_map/ppermute | solution.py:320
  7.8 26.6 %collective-permute-start.6 = (bf16[272,512]{1,0:T(8,128)(2,1)S(1)}, bf16[272,512]{1,0:T(8,128)(2,1)}, u32[]{:S(2)}, u32[]{:S(2)}) collective-permute-start(bf16[272,512]{1,0:T(8,128)(2,1)S(1)} %maximum_maximum_fusion.refs_2_), channel_id=1, source_target_pairs={{0,4},{4,0},{8,12},{12,8},{16,20},{20,16},{24,28},{28,24},{1,5},{5... | collective-permute-start | bytes 835592 | tf_op jit(solution)/shard_map/ppermute | solution.py:320
  17.2 23.1 %collective-permute-start.3 = (bf16[272,512]{1,0:T(8,128)(2,1)}, bf16[272,512]{1,0:T(8,128)(2,1)}, u32[]{:S(2)}, u32[]{:S(2)}) collective-permute-start(bf16[272,512]{1,0:T(8,128)(2,1)} %collective-permute-done.2.refs_2_), channel_id=1, source_target_pairs={{0,4},{4,0},{8,12},{12,8},{16,20},{20,16},{24,28},{28,24},{1,5},{5... | collective-permute-start | bytes 835592 | tf_op jit(solution)/shard_map/ppermute | solution.py:320
  27.7 12.6 %collective-permute-start.5 = (bf16[272,512]{1,0:T(8,128)(2,1)}, bf16[272,512]{1,0:T(8,128)(2,1)}, u32[]{:S(2)}, u32[]{:S(2)}) collective-permute-start(bf16[272,512]{1,0:T(8,128)(2,1)} %collective-permute-done.4.refs_4_), channel_id=1, source_target_pairs={{0,4},{4,0},{8,12},{12,8},{16,20},{20,16},{24,28},{28,24},{1,5},{5... | collective-permute-start | bytes 835592 | tf_op jit(solution)/shard_map/ppermute | solution.py:320
  29.1 1.2 %copy-start = (bf16[256,2048]{1,0:T(8,128)(2,1)S(1)}, bf16[256,2048]{1,0:T(8,128)(2,1)}, u32[]{:S(2)}) copy-start(bf16[256,2048]{1,0:T(8,128)(2,1)} %refs_1_.7) | copy-start | bytes 3145732
  30.4 0.7 copy-start.3
  33.8 12.5 %collective-permute-start.1 = (bf16[272,512]{1,0:T(8,128)(2,1)}, bf16[272,512]{1,0:T(8,128)(2,1)S(1)}, u32[]{:S(2)}, u32[]{:S(2)}) collective-permute-start(bf16[272,512]{1,0:T(8,128)(2,1)} %collective-permute-done.refs_3_), channel_id=1, source_target_pairs={{0,4},{4,0},{8,12},{12,8},{16,20},{20,16},{24,28},{28,24},{1,5},{5... | collective-permute-start | bytes 835592 | tf_op jit(solution)/shard_map/ppermute | solution.py:320
  40.3 6.0 %copy-start.2 = (bf16[256,2048]{1,0:T(8,128)(2,1)S(1)}, bf16[256,2048]{1,0:T(8,128)(2,1)}, u32[]{:S(2)}) copy-start(bf16[256,2048]{1,0:T(8,128)(2,1)} %refs_1_.7) | copy-start | bytes 3145732
  52.5 1.6 %collective-permute-start.7 = (bf16[256,512]{1,0:T(8,128)(2,1)S(1)}, bf16[256,512]{1,0:T(8,128)(2,1)S(1)}, u32[]{:S(2)}, u32[]{:S(2)}) collective-permute-start(bf16[256,512]{1,0:T(8,128)(2,1)S(1)} %get-tuple-element.32), channel_id=1, source_target_pairs={{0,1},{1,0},{2,3},{3,2},{4,5},{5,4},{6,7},{7,6},{8,9},{9,8},{10,11... | collective-permute-start | bytes 786440 | tf_op jit(solution)/shard_map/ppermute | solution.py:369
  57.8 1.6 %collective-permute-start.8 = (bf16[256,512]{1,0:T(8,128)(2,1)S(1)}, bf16[256,512]{1,0:T(8,128)(2,1)S(1)}, u32[]{:S(2)}, u32[]{:S(2)}) collective-permute-start(bf16[256,512]{1,0:T(8,128)(2,1)S(1)} %get-tuple-element.34), channel_id=1, source_target_pairs={{0,1},{1,0},{2,3},{3,2},{4,5},{5,4},{6,7},{7,6},{8,9},{9,8},{10,11... | collective-permute-start | bytes 786440 | tf_op jit(solution)/shard_map/ppermute | solution.py:369
  64.4 14.4 %collective-permute-start.9 = (bf16[256,1024]{1,0:T(8,128)(2,1)S(1)}, bf16[256,1024]{1,0:T(8,128)(2,1)S(1)}, u32[]{:S(2)}, u32[]{:S(2)}) collective-permute-start(bf16[256,1024]{1,0:T(8,128)(2,1)S(1)} %get-tuple-element.36), channel_id=1, source_target_pairs={{0,1},{1,0},{2,3},{3,2},{4,5},{5,4},{6,7},{7,6},{8,9},{9,8},{10,11... | collective-permute-start | bytes 1572872 | tf_op jit(solution)/shard_map/ppermute | solution.py:369
  64.6 9.2 %collective-permute-start.10 = (bf16[256,512]{1,0:T(8,128)(2,1)S(1)}, bf16[256,512]{1,0:T(8,128)(2,1)S(1)}, u32[]{:S(2)}, u32[]{:S(2)}) collective-permute-start(bf16[256,512]{1,0:T(8,128)(2,1)S(1)} %add_convert_fusion.1.refs_0_), channel_id=1, source_target_pairs={{0,2},{1,3},{2,0},{3,1},{4,6},{5,7},{6,4},{7,5},{8,10},{9,11},{10,... | collective-permute-start | bytes 786440 | tf_op jit(solution)/shard_map/ppermute | solution.py:373
  66.2 12.7 %collective-permute-start.11 = (bf16[256,512]{1,0:T(8,128)(2,1)S(1)}, bf16[256,512]{1,0:T(8,128)(2,1)S(1)}, u32[]{:S(2)}, u32[]{:S(2)}) collective-permute-start(bf16[256,512]{1,0:T(8,128)(2,1)S(1)} %add_convert_fusion.refs_0_), channel_id=1, source_target_pairs={{0,2},{1,3},{2,0},{3,1},{4,6},{5,7},{6,4},{7,5},{8,10},{9,11},{10,... | collective-permute-start | bytes 786440 | tf_op jit(solution)/shard_map/ppermute | solution.py:373

commit v9 on v8

--- a/solution.py
+++ b/solution.py
@@ -227,7 +227,6 @@
         out_specs=[whole] * len(out_shape),
         out_shape=out_shape,
         scratch_shapes=scratch,
-        input_output_aliases={} if first or last else {2 + len(arrays) + n: n for n in range(3)},
         compiler_params=pltpu.CompilerParams(vmem_limit_bytes=WIDE_LIMIT if last else VMEM_LIMIT),
         cost_estimate=pl.CostEstimate(
             flops=flops, bytes_accessed=4 * pairs, transcendentals=pairs
@@ -337,8 +336,8 @@
         near_crossed = [(x,) for x in cross(near)]
         opposite_crossed = [(x,) for x in cross(opposite)]
         stages = [[(own,)], [(near,)] + own_crossed + [(opposite,)]]
-        stages.append(near_crossed + [(mirror,)] + opposite_crossed)
-        stages += [[(x,)] for x in cross(mirror)]
+        stages.append(near_crossed + [(mirror,)])
+        stages.append(opposite_crossed + [(x,) for x in cross(mirror)])
     else:
         blocks = [own]
         for k in range(1, outer):

time: 80.1 us -> 79.5 us (level)
  the two profiles are of different devices: /device:TPU:0 before, /device:TPU:12 now
where the time goes in v9:
time: 79.5 us; the launch traced here: 79.2 us
  waiting for transfers between devices  34.5 us (43%)
  Pallas kernels  28.4 us (36%)
  starting transfers between devices  12 us (15%)
  local copies, waits for them, and re-layouts  3.05 us (4%)
  other arithmetic  1.09 us (1%)
    ppermute x7, waiting for transfers between devices, move(): return lax.ppermute(block, 'ctx', pairs)  19.5 us
    pallas_call x4, Pallas kernels, attend(): pl.pallas_call(functools.partial(attend_kernel, halves, first, last, scal...  18.9 us
    ppermute x2, waiting for transfers between devices, to_group(): return lax.ppermute(x, 'tp', pairs)  12.2 us
    ppermute x7, starting transfers between devices, move(): return lax.ppermute(block, 'ctx', pairs)  9.52 us
    pallas_call x2, Pallas kernels, project(): pl.pallas_call(project_kernel, in_specs=[pl.BlockSpec(memory_space=pltpu....  8.57 us
    ppermute x3, waiting for transfers between devices, to_core(): return lax.ppermute(x, 'tp', pairs)  2.85 us
    ppermute x2, starting transfers between devices, to_group(): return lax.ppermute(x, 'tp', pairs)  2.03 us
    unnamed x8, local copies, waits for them, and re-layouts  1.89 us
  transfers between devices with their start and end apart: 12, of which 7 were waited for; matrix products, arithmetic and copies ran while one was open for 0% of the time, Pallas kernels for 14%

profile of v9, /device:TPU:12, one launch (start us, length us, event | category | flops | bytes accessed | tf_op | source)
XLA Modules:
  0.0 79.2 jit_solution(14648089029879833564)
XLA Ops:
  0.0 0.7 convert_bitcast_fusion
  0.9 1.0 %constant_dynamic-slice_fusion = (bf16[256,128]{1,0:T(8,128)(2,1)S(1)}, bf16[256,128]{1,0:T(8,128)(2,1)S(1)}, bf16[256,128]{1,0:T(8,128)(2,1)S(1)}, bf16[256,128]{1,0:T(8,128)(2,1)S(1)}) fusion(bf16[256,1024]{1,0:T(8,128)(2,1)} %param.7, s32[]{:T(128)S(6)} %select_n.52, s32[]{:T(128)S(6)} %add.80, bf16[256,1024]{1,0:T(8,128)(2,1)} %param.6), kind=kLoop, calls=%fused_computation.10 | loop fusion | bytes 524296 | tf_op jit(solution)/shard_map/slice | solution.py:302
  2.5 2.6 %collective-permute-start = (bf16[272,512]{1,0:T(8,128)(2,1)S(1)}, bf16[272,512]{1,0:T(8,128)(2,1)S(1)}, u32[]{:S(2)}, u32[]{:S(2)}) collective-permute-start(bf16[272,512]{1,0:T(8,128)(2,1)S(1)} %maximum_maximum_fusion.refs_2_), channel_id=1, source_target_pairs={{0,16},{4,20},{8,24},{12,28},{16,0},{20,4},{24,8},{28,12},{1,17},{... | collective-permute-start | bytes 835592 | tf_op jit(solution)/shard_map/ppermute | solution.py:319
  5.5 1.5 %collective-permute-start.6 = (bf16[272,512]{1,0:T(8,128)(2,1)S(1)}, bf16[272,512]{1,0:T(8,128)(2,1)S(1)}, u32[]{:S(2)}, u32[]{:S(2)}) collective-permute-start(bf16[272,512]{1,0:T(8,128)(2,1)S(1)} %maximum_maximum_fusion.refs_2_), channel_id=1, source_target_pairs={{0,4},{4,0},{8,12},{12,8},{16,20},{20,16},{24,28},{28,24},{1,5},{5... | collective-permute-start | bytes 835592 | tf_op jit(solution)/shard_map/ppermute | solution.py:319
  7.0 6.6 %collective-permute-done.4.refs_2_ = bf16[272,512]{1,0:T(8,128)(2,1)S(1)} collective-permute-done((bf16[272,512]{1,0:T(8,128)(2,1)S(1)}, bf16[272,512]{1,0:T(8,128)(2,1)S(1)}, u32[]{:S(2)}, u32[]{:S(2)}) %collective-permute-start.4) | collective-permute-done | bytes 278560 | tf_op jit(solution)/shard_map/ppermute | solution.py:319
  13.6 1.5 %collective-permute-start.5 = (bf16[272,512]{1,0:T(8,128)(2,1)S(1)}, bf16[272,512]{1,0:T(8,128)(2,1)S(1)}, u32[]{:S(2)}, u32[]{:S(2)}) collective-permute-start(bf16[272,512]{1,0:T(8,128)(2,1)S(1)} %collective-permute-done.4.refs_2_), channel_id=1, source_target_pairs={{0,4},{4,0},{8,12},{12,8},{16,20},{20,16},{24,28},{28,24},{1,5},{5... | collective-permute-start | bytes 835592 | tf_op jit(solution)/shard_map/ppermute | solution.py:319
  15.2 8.9 %collective-permute-done.refs_4_ = bf16[272,512]{1,0:T(8,128)(2,1)S(1)} collective-permute-done((bf16[272,512]{1,0:T(8,128)(2,1)S(1)}, bf16[272,512]{1,0:T(8,128)(2,1)S(1)}, u32[]{:S(2)}, u32[]{:S(2)}) %collective-permute-start) | collective-permute-done | bytes 278560 | tf_op jit(solution)/shard_map/ppermute | solution.py:319
  24.1 1.5 %collective-permute-start.1 = (bf16[272,512]{1,0:T(8,128)(2,1)S(1)}, bf16[272,512]{1,0:T(8,128)(2,1)S(1)}, u32[]{:S(2)}, u32[]{:S(2)}) collective-permute-start(bf16[272,512]{1,0:T(8,128)(2,1)S(1)} %collective-permute-done.refs_4_), channel_id=1, source_target_pairs={{0,4},{4,0},{8,12},{12,8},{16,20},{20,16},{24,28},{28,24},{1,5},{5... | collective-permute-start | bytes 835592 | tf_op jit(solution)/shard_map/ppermute | solution.py:319
  25.5 4.0 %collective-permute-done.2.refs_3_ = bf16[272,512]{1,0:T(8,128)(2,1)S(1)} collective-permute-done((bf16[272,512]{1,0:T(8,128)(2,1)S(1)}, bf16[272,512]{1,0:T(8,128)(2,1)S(1)}, u32[]{:S(2)}, u32[]{:S(2)}) %collective-permute-start.2) | collective-permute-done | bytes 278560 | tf_op jit(solution)/shard_map/ppermute | solution.py:319
  29.6 1.5 %collective-permute-start.3 = (bf16[272,512]{1,0:T(8,128)(2,1)S(1)}, bf16[272,512]{1,0:T(8,128)(2,1)S(1)}, u32[]{:S(2)}, u32[]{:S(2)}) collective-permute-start(bf16[272,512]{1,0:T(8,128)(2,1)S(1)} %collective-permute-done.2.refs_3_), channel_id=1, source_target_pairs={{0,4},{4,0},{8,12},{12,8},{16,20},{20,16},{24,28},{28,24},{1,5},{5... | collective-permute-start | bytes 835592 | tf_op jit(solution)/shard_map/ppermute | solution.py:319
  31.1 1.2 %copy-done = bf16[256,2048]{1,0:T(8,128)(2,1)S(1)} copy-done((bf16[256,2048]{1,0:T(8,128)(2,1)S(1)}, bf16[256,2048]{1,0:T(8,128)(2,1)}, u32[]{:S(2)}) %copy-start) | copy-done | bytes 1048600
  32.3 0.7 copy-done.2
  32.9 2.6 %shard_map.55 = (f32[4,1,1024]{2,1,0:T(1,128)S(1)}, f32[4,1,1024]{2,1,0:T(1,128)S(1)}, f32[4,128,1024]{2,1,0:T(8,128)S(1)}) custom-call(s32[2]{0:T(128)S(1)} %copy-done.2, bf16[256,2048]{1,0:T(8,128)(2,1)S(1)} %copy-done, bf16[272,512]{1,0:T(8,128)(2,1)S(1)} %maximum_maximum_fusion.refs_2_), custom_call_target="tpu_custom_call" | custom-call | flops 536870912 | bytes 4194304 | tf_op jit(solution)/shard_map/pallas_call | solution.py:224
  35.6 5.1 %shard_map.56 = (f32[4,1,1024]{2,1,0:T(1,128)S(1)}, f32[4,1,1024]{2,1,0:T(1,128)S(1)}, f32[4,128,1024]{2,1,0:T(8,128)S(1)}) custom-call(s32[2]{0:T(128)S(1)} %copy-done.2, bf16[256,2048]{1,0:T(8,128)(2,1)S(1)} %copy-done, bf16[272,512]{1,0:T(8,128)(2,1)S(1)} %collective-permute-done.4.refs_2_, bf16[272,512]{1,0:T(8,128)(2,1)S(1)} %collective-permute-done.6.refs_3_, ...), custom_call_target="tpu_custom_call" | custom-call | flops 1610612736 | bytes 12582912 | tf_op jit(solution)/shard_map/pallas_call | solution.py:224
  40.8 3.7 %shard_map.57 = (f32[4,1,1024]{2,1,0:T(1,128)S(1)}, f32[4,1,1024]{2,1,0:T(1,128)S(1)}, f32[4,128,1024]{2,1,0:T(8,128)S(1)}) custom-call(s32[2]{0:T(128)S(1)} %copy-done.2, bf16[256,2048]{1,0:T(8,128)(2,1)S(1)} %copy-done, bf16[272,512]{1,0:T(8,128)(2,1)S(1)} %collective-permute-done.5.refs_2_, bf16[272,512]{1,0:T(8,128)(2,1)S(1)} %collective-permute-done.2.refs_3_, ...), custom_call_target="tpu_custom_call" | custom-call | flops 1073741824 | bytes 8388608 | tf_op jit(solution)/shard_map/pallas_call | solution.py:224
  44.5 7.4 %shard_map.58 = (bf16[256,2048]{1,0:T(8,128)(2,1)S(1)}, bf16[256,512]{1,0:T(8,128)(2,1)S(1)}, f32[256,512]{1,0:T(8,128)S(1)}) custom-call(s32[2]{0:T(128)S(1)} %copy-done.3, bf16[256,2048]{1,0:T(8,128)(2,1)S(1)} %copy-done.1, bf16[272,512]{1,0:T(8,128)(2,1)S(1)} %collective-permute-done.1.refs_2_, bf16[272,512]{1,0:T(8,128)(2,1)S(1)} %collective-permute-done.3.refs_3_, ...), custom_call_target="tpu_custom_call" | custom-call | flops 2147483648 | bytes 8388608 | tf_op jit(solution)/shard_map/pallas_call | solution.py:224
  52.0 1.5 %collective-permute-done.7 = bf16[256,512]{1,0:T(8,128)(2,1)S(1)} collective-permute-done((bf16[256,512]{1,0:T(8,128)(2,1)S(1)}, bf16[256,512]{1,0:T(8,128)(2,1)S(1)}, u32[]{:S(2)}, u32[]{:S(2)}) %collective-permute-start.7) | collective-permute-done | bytes 262176 | tf_op jit(solution)/shard_map/ppermute | solution.py:368
  53.6 3.6 %shard_map.59 = (bf16[256,512]{1,0:T(8,128)(2,1)S(1)}, f32[256,512]{1,0:T(8,128)S(1)}) custom-call(s32[2]{0:T(128)S(1)} %get-tuple-element.37.at_ref, bf16[256,2048]{1,0:T(8,128)(2,1)S(1)} %get-tuple-element.30.rows_ref, bf16[2048,4096]{1,0:T(8,128)(2,1)} %weight_ref.3, bf16[256,512]{1,0:T(8,128)(2,1)S(1)} %add_convert_fusion.1.refs_0_), custom_call_target="tpu_custom_call" | custom-call | flops 1073741824 | bytes 4194304 | tf_op jit(solution)/shard_map/pallas_call | solution.py:248
  57.5 1.3 %collective-permute-done.8 = bf16[256,512]{1,0:T(8,128)(2,1)S(1)} collective-permute-done((bf16[256,512]{1,0:T(8,128)(2,1)S(1)}, bf16[256,512]{1,0:T(8,128)(2,1)S(1)}, u32[]{:S(2)}, u32[]{:S(2)}) %collective-permute-start.8) | collective-permute-done | bytes 262176 | tf_op jit(solution)/shard_map/ppermute | solution.py:368
  58.9 5.0 %shard_map.60 = (bf16[256,1024]{1,0:T(8,128)(2,1)S(1)}, f32[256,1024]{1,0:T(8,128)S(1)}) custom-call(s32[2]{0:T(128)S(1)} %add_multiply_fusion.at_ref, bf16[256,2048]{1,0:T(8,128)(2,1)S(1)} %get-tuple-element.30.rows_ref, bf16[2048,4096]{1,0:T(8,128)(2,1)} %weight_ref.3, bf16[256,512]{1,0:T(8,128)(2,1)S(1)} %add_convert_fusion.refs_0_), custom_call_target="tpu_custom_call" | custom-call | flops 2147483648 | bytes 8388608 | tf_op jit(solution)/shard_map/pallas_call | solution.py:248
  64.6 1.5 %collective-permute-start.11 = (bf16[256,512]{1,0:T(8,128)(2,1)S(1)}, bf16[256,512]{1,0:T(8,128)(2,1)S(1)}, u32[]{:S(2)}, u32[]{:S(2)}) collective-permute-start(bf16[256,512]{1,0:T(8,128)(2,1)S(1)} %add_convert_fusion.refs_0_), channel_id=1, source_target_pairs={{0,2},{1,3},{2,0},{3,1},{4,6},{5,7},{6,4},{7,5},{8,10},{9,11},{10,... | collective-permute-start | bytes 786440 | tf_op jit(solution)/shard_map/ppermute | solution.py:372
  66.1 7.1 %collective-permute-done.10.refs_1_ = bf16[256,512]{1,0:T(8,128)(2,1)S(1)} collective-permute-done((bf16[256,512]{1,0:T(8,128)(2,1)S(1)}, bf16[256,512]{1,0:T(8,128)(2,1)S(1)}, u32[]{:S(2)}, u32[]{:S(2)}) %collective-permute-start.10) | collective-permute-done | bytes 262176 | tf_op jit(solution)/shard_map/ppermute | solution.py:372
  73.2 5.0 %collective-permute-done.11.refs_2_ = bf16[256,512]{1,0:T(8,128)(2,1)S(1)} collective-permute-done((bf16[256,512]{1,0:T(8,128)(2,1)S(1)}, bf16[256,512]{1,0:T(8,128)(2,1)S(1)}, u32[]{:S(2)}, u32[]{:S(2)}) %collective-permute-start.11) | collective-permute-done | bytes 262176 | tf_op jit(solution)/shard_map/ppermute | solution.py:372
  78.3 0.9 %shard_map.61 = bf16[256,1024]{1,0:T(8,128)(2,1)} custom-call(f32[256,1024]{1,0:T(8,128)S(1)} %get-tuple-element.35.mine_ref, bf16[256,1024]{1,0:T(8,128)(2,1)S(1)} %collective-permute-done.9.refs_0_, bf16[256,512]{1,0:T(8,128)(2,1)S(1)} %collective-permute-done.10.refs_1_, bf16[256,512]{1,0:T(8,128)(2,1)S(1)} %collective-permute-done.11.refs_2_), custom_call_target="tpu_custom_call" | custom-call | flops 1048576 | bytes 2621440 | tf_op jit(solution)/shard_map/pallas_call | solution.py:279
  (26 shorter events, 2.6 us)
Async XLA Ops:
  2.0 11.7 %collective-permute-start.4 = (bf16[272,512]{1,0:T(8,128)(2,1)S(1)}, bf16[272,512]{1,0:T(8,128)(2,1)S(1)}, u32[]{:S(2)}, u32[]{:S(2)}) collective-permute-start(bf16[272,512]{1,0:T(8,128)(2,1)S(1)} %maximum_maximum_fusion.refs_2_), channel_id=1, source_target_pairs={{0,8},{4,12},{8,0},{12,4},{16,24},{20,28},{24,16},{28,20},{1,9},{5... | collective-permute-start | bytes 835592 | tf_op jit(solution)/shard_map/ppermute | solution.py:319
  2.5 21.6 %collective-permute-start = (bf16[272,512]{1,0:T(8,128)(2,1)S(1)}, bf16[272,512]{1,0:T(8,128)(2,1)S(1)}, u32[]{:S(2)}, u32[]{:S(2)}) collective-permute-start(bf16[272,512]{1,0:T(8,128)(2,1)S(1)} %maximum_maximum_fusion.refs_2_), channel_id=1, source_target_pairs={{0,16},{4,20},{8,24},{12,28},{16,0},{20,4},{24,8},{28,12},{1,17},{... | collective-permute-start | bytes 835592 | tf_op jit(solution)/shard_map/ppermute | solution.py:319
  5.1 24.5 %collective-permute-start.2 = (bf16[272,512]{1,0:T(8,128)(2,1)S(1)}, bf16[272,512]{1,0:T(8,128)(2,1)S(1)}, u32[]{:S(2)}, u32[]{:S(2)}) collective-permute-start(bf16[272,512]{1,0:T(8,128)(2,1)S(1)} %maximum_maximum_fusion.refs_2_), channel_id=1, source_target_pairs={{0,24},{4,28},{8,16},{12,20},{16,8},{20,12},{24,0},{28,4},{1,25},{... | collective-permute-start | bytes 835592 | tf_op jit(solution)/shard_map/ppermute | solution.py:319
  5.5 30.1 %collective-permute-start.6 = (bf16[272,512]{1,0:T(8,128)(2,1)S(1)}, bf16[272,512]{1,0:T(8,128)(2,1)S(1)}, u32[]{:S(2)}, u32[]{:S(2)}) collective-permute-start(bf16[272,512]{1,0:T(8,128)(2,1)S(1)} %maximum_maximum_fusion.refs_2_), channel_id=1, source_target_pairs={{0,4},{4,0},{8,12},{12,8},{16,20},{20,16},{24,28},{28,24},{1,5},{5... | collective-permute-start | bytes 835592 | tf_op jit(solution)/shard_map/ppermute | solution.py:319
  13.6 27.1 %collective-permute-start.5 = (bf16[272,512]{1,0:T(8,128)(2,1)S(1)}, bf16[272,512]{1,0:T(8,128)(2,1)S(1)}, u32[]{:S(2)}, u32[]{:S(2)}) collective-permute-start(bf16[272,512]{1,0:T(8,128)(2,1)S(1)} %collective-permute-done.4.refs_2_), channel_id=1, source_target_pairs={{0,4},{4,0},{8,12},{12,8},{16,20},{20,16},{24,28},{28,24},{1,5},{5... | collective-permute-start | bytes 835592 | tf_op jit(solution)/shard_map/ppermute | solution.py:319
  24.1 20.4 %collective-permute-start.1 = (bf16[272,512]{1,0:T(8,128)(2,1)S(1)}, bf16[272,512]{1,0:T(8,128)(2,1)S(1)}, u32[]{:S(2)}, u32[]{:S(2)}) collective-permute-start(bf16[272,512]{1,0:T(8,128)(2,1)S(1)} %collective-permute-done.refs_4_), channel_id=1, source_target_pairs={{0,4},{4,0},{8,12},{12,8},{16,20},{20,16},{24,28},{28,24},{1,5},{5... | collective-permute-start | bytes 835592 | tf_op jit(solution)/shard_map/ppermute | solution.py:319
  29.6 14.9 %collective-permute-start.3 = (bf16[272,512]{1,0:T(8,128)(2,1)S(1)}, bf16[272,512]{1,0:T(8,128)(2,1)S(1)}, u32[]{:S(2)}, u32[]{:S(2)}) collective-permute-start(bf16[272,512]{1,0:T(8,128)(2,1)S(1)} %collective-permute-done.2.refs_3_), channel_id=1, source_target_pairs={{0,4},{4,0},{8,12},{12,8},{16,20},{20,16},{24,28},{28,24},{1,5},{5... | collective-permute-start | bytes 835592 | tf_op jit(solution)/shard_map/ppermute | solution.py:319
  31.1 1.2 %copy-start = (bf16[256,2048]{1,0:T(8,128)(2,1)S(1)}, bf16[256,2048]{1,0:T(8,128)(2,1)}, u32[]{:S(2)}) copy-start(bf16[256,2048]{1,0:T(8,128)(2,1)} %refs_1_.7) | copy-start | bytes 3145732
  32.3 0.7 copy-start.2
  40.7 3.8 %copy-start.1 = (bf16[256,2048]{1,0:T(8,128)(2,1)S(1)}, bf16[256,2048]{1,0:T(8,128)(2,1)}, u32[]{:S(2)}) copy-start(bf16[256,2048]{1,0:T(8,128)(2,1)} %refs_1_.7) | copy-start | bytes 3145732
  40.8 3.8 %copy-start.3 = (s32[2]{0:T(128)S(1)}, s32[2]{0:T(128)}, u32[]{:S(2)}) copy-start(s32[2]{0:T(128)} %refs_0_.7) | copy-start | bytes 28
  51.9 1.6 %collective-permute-start.7 = (bf16[256,512]{1,0:T(8,128)(2,1)S(1)}, bf16[256,512]{1,0:T(8,128)(2,1)S(1)}, u32[]{:S(2)}, u32[]{:S(2)}) collective-permute-start(bf16[256,512]{1,0:T(8,128)(2,1)S(1)} %get-tuple-element.32), channel_id=1, source_target_pairs={{0,1},{1,0},{2,3},{3,2},{4,5},{5,4},{6,7},{7,6},{8,9},{9,8},{10,11... | collective-permute-start | bytes 786440 | tf_op jit(solution)/shard_map/ppermute | solution.py:368
  57.2 1.6 %collective-permute-start.8 = (bf16[256,512]{1,0:T(8,128)(2,1)S(1)}, bf16[256,512]{1,0:T(8,128)(2,1)S(1)}, u32[]{:S(2)}, u32[]{:S(2)}) collective-permute-start(bf16[256,512]{1,0:T(8,128)(2,1)S(1)} %get-tuple-element.34), channel_id=1, source_target_pairs={{0,1},{1,0},{2,3},{3,2},{4,5},{5,4},{6,7},{7,6},{8,9},{9,8},{10,11... | collective-permute-start | bytes 786440 | tf_op jit(solution)/shard_map/ppermute | solution.py:368
  63.9 14.4 %collective-permute-start.9 = (bf16[256,1024]{1,0:T(8,128)(2,1)S(1)}, bf16[256,1024]{1,0:T(8,128)(2,1)S(1)}, u32[]{:S(2)}, u32[]{:S(2)}) collective-permute-start(bf16[256,1024]{1,0:T(8,128)(2,1)S(1)} %get-tuple-element.36), channel_id=1, source_target_pairs={{0,1},{1,0},{2,3},{3,2},{4,5},{5,4},{6,7},{7,6},{8,9},{9,8},{10,11... | collective-permute-start | bytes 1572872 | tf_op jit(solution)/shard_map/ppermute | solution.py:368
  64.1 9.2 %collective-permute-start.10 = (bf16[256,512]{1,0:T(8,128)(2,1)S(1)}, bf16[256,512]{1,0:T(8,128)(2,1)S(1)}, u32[]{:S(2)}, u32[]{:S(2)}) collective-permute-start(bf16[256,512]{1,0:T(8,128)(2,1)S(1)} %add_convert_fusion.1.refs_0_), channel_id=1, source_target_pairs={{0,2},{1,3},{2,0},{3,1},{4,6},{5,7},{6,4},{7,5},{8,10},{9,11},{10,... | collective-permute-start | bytes 786440 | tf_op jit(solution)/shard_map/ppermute | solution.py:372
  64.6 13.7 %collective-permute-start.11 = (bf16[256,512]{1,0:T(8,128)(2,1)S(1)}, bf16[256,512]{1,0:T(8,128)(2,1)S(1)}, u32[]{:S(2)}, u32[]{:S(2)}) collective-permute-start(bf16[256,512]{1,0:T(8,128)(2,1)S(1)} %add_convert_fusion.refs_0_), channel_id=1, source_target_pairs={{0,2},{1,3},{2,0},{3,1},{4,6},{5,7},{6,4},{7,5},{8,10},{9,11},{10,... | collective-permute-start | bytes 786440 | tf_op jit(solution)/shard_map/ppermute | solution.py:372
